TPU v7x, 32 devices: a whole 2x2x4 slice. The times are simulated.
32 devices in a mesh: group: 2 (over y), seq: 4 (over z), blk: 2 (over x), tp: 2 (over core).
Axes of the slice: x: 2, y: 2, z: 4, core: 2. Of those that a mesh axis runs over, the one named last changes fastest.
Arguments:
- tokens: bfloat16 [2048, 3072], P(('group', 'blk'), ('seq', 'tp')), parts along dimension 0, may hold values from -64 to 64
- timestep: int32 [2], P('group'), parts along dimension 0, may hold values from 25 to 49
- padded_heads: int32 [2], P('group'), parts along dimension 0, may hold values from 1 to 3
- modulation: float32 [50, 3, 3072], replicated, may hold values from -3 to 3
- qkv_weight: bfloat16 [3, 3072, 1024], P(None, 'blk', ('seq', 'tp')), may hold values from -1 to 1
- out_weight: bfloat16 [1024, 3072], P(('seq', 'tp'), 'blk'), may hold values from -0.5 to 0.5
Outputs:
- update: bfloat16 [2048, 3072], P(('group', 'blk'), ('seq', 'tp')), parts along dimension 0
There are 2 independent parts, one for each index of `group`. A program takes and returns all parts, laid end to end along the dimension named above; an argument that names none is the same for every part. Nothing has to cross between parts.
All inputs are finite; a program needn't handle non-finite values.
Results may differ from a plain program's by a relative error of at most 0.023.
Values may be sent and summed in bfloat16 or wider, within the bound.
No kernel may reach another device: no remote copies, remote signals or barrier semaphores. Data moves between devices by JAX's collectives and lax.ppermute only.
A program may use at most 64 MiB of HBM per device.

v0:
```python
import math

import jax
import jax.numpy as jnp
from jax import lax
from jax.sharding import PartitionSpec as P

epsilon = 1e-06
neg_large = -1e30


def collect(own_part):
    gathered = lax.all_gather(own_part, ("seq", "tp"), axis=1, tiled=True)
    return gathered


def attend_block(running, queries, key_block, value_block, factor):
    largest, totals, weighted = running
    scores = (
        lax.dot_general(
            queries, key_block, (((1,), (1,)), ((), ())), preferred_element_type=jnp.float32
        )
        * factor
    )
    new_max = jnp.maximum(largest, jnp.max(scores, axis=1))
    rescale = jnp.exp(largest - new_max)
    weights = jnp.exp(scores - new_max[:, None])
    totals = totals * rescale + jnp.sum(weights, axis=1)
    weighted = weighted * rescale[:, None] + jnp.dot(
        weights.astype(jnp.bfloat16), value_block, preferred_element_type=jnp.float32
    )
    return (new_max, totals, weighted)


def body(tokens, timestep, padded_heads, modulation, qkv_weight, out_weight):
    slices = lax.axis_size(("seq", "tp"))
    own_index = lax.axis_index(("seq", "tp"))
    model_width = modulation.shape[2]
    own_width = model_width // slices
    token_rows = tokens.shape[0]
    head_size = out_weight.shape[0]
    table_row = lax.dynamic_index_in_dim(modulation, timestep[0], 0, keepdims=False)
    own_entry = lax.dynamic_slice_in_dim(table_row, own_index * own_width, own_width, 1)
    gathered = collect(tokens).astype(jnp.float32)
    average = jnp.mean(gathered, axis=1, keepdims=True)
    centered = gathered - average
    spread = jnp.mean(centered * centered, axis=1, keepdims=True)
    normed = centered * lax.rsqrt(spread + epsilon)
    modulated = (normed * (1.0 + table_row[1]) + table_row[0]).astype(jnp.bfloat16)
    projected = jnp.einsum(
        "td,kde->kte",
        modulated,
        lax.all_gather(qkv_weight, "blk", axis=1, tiled=True),
        preferred_element_type=jnp.float32,
    ).astype(jnp.bfloat16)
    queries = projected[0]
    factor = 1.0 / math.sqrt(head_size)
    initial = (
        jnp.full((token_rows,), neg_large, jnp.float32),
        jnp.zeros((token_rows,), jnp.float32),
        jnp.zeros((token_rows, head_size), jnp.float32),
    )
    key_piece = lax.all_gather(projected[1], "blk", axis=0, tiled=True)
    value_piece = lax.all_gather(projected[2], "blk", axis=0, tiled=True)
    length = key_piece.shape[0]

    def one_block(counter, inner_state):
        key_block = lax.dynamic_slice_in_dim(key_piece, counter * 512, 512, 0)
        value_block = lax.dynamic_slice_in_dim(value_piece, counter * 512, 512, 0)
        return attend_block(inner_state, queries, key_block, value_block, factor)

    largest, exp_totals, weighted = lax.fori_loop(0, length // 512, one_block, initial)
    attended = weighted / exp_totals[:, None]
    live_heads = slices - padded_heads[0]
    masked = jnp.where(own_index < live_heads, attended, 0.0).astype(jnp.bfloat16)
    head_term = jnp.dot(
        masked,
        lax.all_gather(out_weight, "blk", axis=1, tiled=True),
        preferred_element_type=jnp.float32,
    )
    summed = lax.psum_scatter(
        head_term.astype(jnp.bfloat16), ("seq", "tp"), scatter_dimension=1, tiled=True
    ).astype(jnp.float32)
    return (own_entry[2] * summed).astype(jnp.bfloat16)


def solution(mesh):
    return jax.shard_map(
        body,
        mesh=mesh,
        in_specs=(
            P(("group", "blk"), ("seq", "tp")),
            P("group"),
            P("group"),
            P(),
            P(None, "blk", ("seq", "tp")),
            P(("seq", "tp"), "blk"),
        ),
        out_specs=P(("group", "blk"), ("seq", "tp")),
        check_vma=False,
    )
```

profile of v0, /device:TPU:0, one launch (start us, length us, event | category | flops | bytes accessed | tf_op | source)
XLA Modules:
  0.0 157.3 jit_solution(16973399973763437814)
XLA Ops:
  6.5 0.0 all-gather.5.cloned.1.call-start
  6.5 0.7 all-gather.5.cloned.1.call-update
  7.3 0.0 all-gather.7.cloned.1.call-start
  7.3 0.7 all-gather.7.cloned.1.call-update
  8.0 0.0 reduce-scatter.4.cloned.1.call-start
  9.4 14.8 %all_gather.19 = bf16[128,3072]{1,0:T(8,128)(2,1)} all-gather(bf16[128,1536]{1,0:T(8,128)(2,1)} %param.13), channel_id=1, replica_groups=mesh['group'=2,'seq'=4,'blk'=2,'tp'=2] {'blk'}, dimensions={1}, use_global_device_ids=true | all-gather | bytes 1179648 | tf_op jit(solution)/shard_map/all_gather | solution.py:78
  24.1 1.0 dynamic-slice_add_fusion
  25.1 24.4 %all-gather.5.cloned.1.call-done = bf16[512,3072]{1,0:T(8,128)(2,1)} async-done(((bf16[512,384]{1,0:T(8,128)(2,1)}), bf16[512,3072]{1,0:T(8,128)(2,1)}) %all-gather.5.cloned.1.call-update) | async-done | bytes 3145744 | tf_op jit(solution)/shard_map/all_gather | solution.py:13
  49.5 0.0 copy-start
  49.5 2.5 %convert_reduce_fusion = f32[512]{0:T(512)S(1)} fusion(bf16[512,3072]{1,0:T(8,128)(2,1)} %all-gather.5.cloned.1.call-done), kind=kLoop, calls=%fused_computation.16 | loop fusion | flops 3145216 | bytes 3147776 | tf_op jit(solution)/shard_map/reduce_sum | solution.py:45
  52.0 0.3 copy-done
  52.3 1.0 fusion.11
  53.3 33.1 %all-gather.7.cloned.1.call-done = bf16[3,3072,128]{2,1,0:T(8,128)(2,1)} async-done(((bf16[3,1536,128]{2,1,0:T(8,128)(2,1)}), bf16[3,3072,128]{2,1,0:T(8,128)(2,1)}) %all-gather.7.cloned.1.call-update) | async-done | bytes 2359312 | tf_op jit(solution)/shard_map/all_gather | solution.py:53
  86.4 3.5 %fusion.21 = bf16[3,512,128]{2,1,0:T(8,128)(2,1)S(1)} fusion(bf16[3,3072,128]{2,1,0:T(8,128)(2,1)} %all-gather.7.cloned.1.call-done, bf16[512,3072]{1,0:T(8,128)(2,1)S(1)} %copy-done, f32[3072]{0:T(1024)S(1)} %bitcast.32, f32[3072]{0:T(1024)S(1)} %bitcast.31, f32[512]{0:T(512)S(1)} %add_rsqrt_fusion, f32[512]{0:T(512)S(1)} %broadcast_multiply_fusion), kind=kOutput, calls=%fused_computation.27 | convolution fusion | flops 1217593344 | bytes 5926912 | tf_op jit(solution)/shard_map/td,kde->kte/dot_general | solution.py:50
  90.0 5.7 %all-gather = bf16[1,1024,128]{2,1,0:T(8,128)(2,1)S(1)} all-gather(bf16[1,512,128]{2,1,0:T(8,128)(2,1)S(1)} %get-tuple-element.178), channel_id=2, replica_groups=mesh['group'=2,'seq'=4,'blk'=2,'tp'=2] {'blk'}, dimensions={1}, use_global_device_ids=true | all-gather | bytes 393216 | tf_op jit(solution)/shard_map/all_gather | solution.py:63
  95.7 5.6 %all-gather.1 = bf16[1,1024,128]{2,1,0:T(8,128)(2,1)S(1)} all-gather(bf16[1,512,128]{2,1,0:T(8,128)(2,1)S(1)} %get-tuple-element.176), channel_id=3, replica_groups=mesh['group'=2,'seq'=4,'blk'=2,'tp'=2] {'blk'}, dimensions={1}, use_global_device_ids=true | all-gather | bytes 393216 | tf_op jit(solution)/shard_map/all_gather | solution.py:64
  101.3 1.9 %while.18 = (s32[]{:T(128)}, f32[512]{0:T(512)S(1)}, f32[512]{0:T(512)S(1)}, f32[512,128]{1,0:T(8,128)S(1)}, bf16[1024,128]{1,0:T(8,128)(2,1)S(1)}, /*index=5*/b...) while((s32[]{:T(128)}, f32[512]{0:T(512)S(1)}, ...), condition=%wide.region_5.6_spmd.clone, body=%wide.region_2.5_spmd.clone.sunk | while | flops 135989760 | bytes 4096175 | solution.py:72
  101.3 0.3 fusion.42
  101.7 0.2 fusion.43
  101.9 0.4 convolution_add_fusion.2
  102.3 0.3 fusion.42
  102.6 0.2 fusion.43
  102.8 0.4 convolution_add_fusion.2
  103.2 2.2 %convolution_convert_fusion = bf16[512,3072]{1,0:T(8,128)(2,1)S(1)} fusion(bf16[128,3072]{1,0:T(8,128)(2,1)} %all_gather.19, f32[512,128]{1,0:T(8,128)S(1)} %get-tuple-element.130, f32[512]{0:T(512)S(1)} %get-tuple-element.131, pred[]{:T(512)S(6)} %lt.25), kind=kOutput, calls=%fused_computation.23 | convolution fusion | flops 404422656 | bytes 4196353 | tf_op jit(solution)/shard_map/dot_general | solution.py:76
  105.4 2.8 %copy.7 = bf16[512,3072]{0,1:T(8,128)(2,1)} copy(bf16[512,3072]{1,0:T(8,128)(2,1)S(1)} %convolution_convert_fusion) | data formatting | bytes 6291456
  108.2 0.0 reduce-scatter.4.cloned.1.call-update
  108.3 0.8 dynamic-slice_reduce_fusion
  109.1 39.7 %reduce-scatter.4.cloned.1.call-done = bf16[384,512]{1,0:T(8,128)(2,1)} async-done(((bf16[3072,512]{1,0:T(8,128)(2,1)}), bf16[384,512]{1,0:T(8,128)(2,1)}) %reduce-scatter.4.cloned.1.call-update) | async-done | bytes 393232
  148.8 1.2 copy.8
  150.0 0.8 multiply_convert_fusion
  (12 shorter events, 0.1 us)
Async XLA Ops:
  6.5 42.9 %all-gather.5.cloned.1.call-start = ((), (), s32[]{:S(2)}) async-start(), calls=%async_computation.1 | async-start | bytes 3538944 | tf_op jit(solution)/shard_map/all_gather | solution.py:13
  7.3 79.2 %all-gather.7.cloned.1.call-start = ((), (), s32[]{:S(2)}) async-start(), calls=%async_computation.2 | async-start | bytes 3538944 | tf_op jit(solution)/shard_map/all_gather | solution.py:53
  8.0 140.8 %reduce-scatter.4.cloned.1.call-start = ((), (), s32[]{:S(2)}) async-start(), calls=%async_computation.3 | async-start | bytes 3538944
  49.5 2.8 %copy-start = (bf16[512,3072]{1,0:T(8,128)(2,1)S(1)}, bf16[512,3072]{1,0:T(8,128)(2,1)}, u32[]{:S(2)}) copy-start(bf16[512,3072]{1,0:T(8,128)(2,1)} %all-gather.5.cloned.1.call-done) | copy-start | bytes 9437188
Sparse Core Ops, SparseCore 0:
  8.9 40.4 all-gather.4
  51.0 35.3 all-gather.6
  108.4 40.3 reduce-scatter.3
where the time goes:
time: 158 us; the launch traced here: 157 us
  waiting for transfers between devices  98.6 us (62%)
  blocking collectives  26.1 us (17%)
  between operations  14.5 us (9%)
  matrix products  7.03 us (4%)
  other arithmetic  5.73 us (4%)
  local copies, waits for them, and re-layouts  5.18 us (3%)
    unnamed x4, waiting for transfers between devices  41.1 us
    all_gather x1, waiting for transfers between devices, body(): lax.all_gather(qkv_weight, 'blk', axis=1, tiled=True)  33.1 us
    all_gather x1, waiting for transfers between devices, collect(): gathered = lax.all_gather(own_part, ('seq', 'tp'), axis=1, tiled=True)  24.4 us
    all_gather x1, blocking collectives, body(): lax.all_gather(out_weight, 'blk', axis=1, tiled=True)  14.8 us
    all_gather x1, blocking collectives, body(): key_piece = lax.all_gather(projected[1], 'blk', axis=0, tiled=True)  5.73 us
    all_gather x1, blocking collectives, body(): value_piece = lax.all_gather(projected[2], 'blk', axis=0, tiled=True)  5.62 us
    unnamed x4, local copies, waits for them, and re-layouts  4.33 us
    dot_general x1, matrix products, body(): jnp.einsum('td,kde->kte', modulated, lax.all_gather(qkv_weight, 'blk', ax...  3.52 us
  transfers between devices with their start and end apart: 3, of which 3 were waited for; matrix products, arithmetic and copies ran while one was open for 3% of the time, Pallas kernels for 0%

commit v1 on v0

v1 whole, which is shorter than its diff:
```python
import functools
import math

import jax
import jax.numpy as jnp
from jax import lax
from jax.experimental import pallas as pl
from jax.experimental.pallas import tpu as pltpu
from jax.sharding import PartitionSpec as P

epsilon = 1e-06
ANY = pl.BlockSpec(memory_space=pl.ANY)
VMEM = pl.BlockSpec(memory_space=pltpu.VMEM)
SMEM = pl.BlockSpec(memory_space=pltpu.SMEM)
PARAMS = pltpu.CompilerParams(vmem_limit_bytes=16 << 20)
LANES = 128
f32, bf16 = jnp.float32, jnp.bfloat16


def folded_order(count):
    return list(range(1, count, 2)) + list(range(0, count, 2))[::-1]


def ring_pairs(order, step=1):
    count = len(order)
    return [(order[i], order[(i + step) % count]) for i in range(count)]


def ring_source(count, at, step):
    order = folded_order(count)
    source = 0
    for i, device in enumerate(order):
        source = jnp.where(at == device, order[(i - step) % count], source)
    return source


def rotation(count, offset):
    return [(i, (i + offset) % count) for i in range(count)]


def back(at, offset, count):
    return lax.rem(at + count - offset, count)


def near(x):
    return pltpu.with_memory_space_constraint(x, pltpu.VMEM)


def far(x):
    return pltpu.with_memory_space_constraint(x, pltpu.HBM)


def kernel(body, outs, ins, scratch=()):
    specs = {"near": VMEM, "far": ANY, "smem": SMEM}
    places = {"near": near, "far": far, "smem": lambda x: x}
    return pl.pallas_call(
        body,
        out_shape=tuple(pltpu.VMEM(shape, dtype) for shape, dtype in outs),
        in_specs=[specs[where] for _, where in ins],
        out_specs=tuple(VMEM for _ in outs),
        scratch_shapes=list(scratch),
        compiler_params=PARAMS,
    )(*[places[where](x) for x, where in ins])


def run_copies(copies):
    for copy in copies:
        copy.start()
    for copy in copies:
        copy.wait()


def split_body(x_ref, top_ref, bottom_ref, sem):
    half = top_ref.shape[0]
    run_copies(
        [
            pltpu.make_async_copy(x_ref.at[pl.ds(0, half)], top_ref, sem.at[0]),
            pltpu.make_async_copy(x_ref.at[pl.ds(half, half)], bottom_ref, sem.at[1]),
        ]
    )


def thirds_body(w_ref, relayed_ref, direct_ref, sem):
    run_copies(
        [
            pltpu.make_async_copy(w_ref.at[lax.axis_index("group")], relayed_ref, sem.at[0]),
            pltpu.make_async_copy(w_ref.at[2], direct_ref, sem.at[1]),
        ]
    )


def column_of(sizes, shift, u, width):
    _, n_seq, n_blk, n_tp = sizes
    n_low = n_seq // n_blk
    if shift is None:
        shift = lax.axis_index("group")
    place = lax.rem(lax.rem(lax.axis_index("seq"), n_low) + shift, n_low)
    core = lax.rem(lax.axis_index("tp") + u, n_tp)
    return pl.multiple_of((place * n_tp + core) * width, math.gcd(width, LANES))


def columns_body(sizes, shift, w_ref, *refs):
    *out_refs, sem = refs
    width = out_refs[0].shape[1]
    run_copies(
        [
            pltpu.make_async_copy(
                w_ref.at[:, pl.ds(column_of(sizes, shift, u, width), width)], out_ref, sem.at[u]
            )
            for u, out_ref in enumerate(out_refs)
        ]
    )


def stack_body(*refs):
    *in_refs, out_ref = refs
    rows = in_refs[0].shape[0]
    for i, in_ref in enumerate(in_refs):
        out_ref[i * rows : (i + 1) * rows, :] = in_ref[...]


def merge_body(pieces, table_ref, *refs):
    w_refs = refs[: len(pieces)]
    out_ref, vec_ref, sem = refs[len(pieces) :]
    blk_at, grp_at = lax.axis_index("blk"), lax.axis_index("group")
    copies = []
    for j, (planes, place, column) in enumerate(pieces):
        rows, head = w_refs[j].shape[-2:]
        first = pl.multiple_of(place(blk_at) * rows, rows)
        for i in range(planes):
            source = w_refs[j].at[i] if planes > 1 else w_refs[j]
            at = i * head if planes > 1 else pl.multiple_of(column(grp_at) * head, head)
            copies.append(
                pltpu.make_async_copy(
                    source, out_ref.at[pl.ds(first, rows), pl.ds(at, head)], sem.at[j, i]
                )
            )
    run_copies(copies)
    _, slices, width = table_ref.shape
    total = None
    for f in range(slices):
        shift, scale = table_ref[0, f : f + 1, :], 1.0 + table_ref[1, f : f + 1, :]
        rest = jnp.concatenate([scale, shift], axis=0)
        parts = []
        for _ in range(3):
            part = rest.astype(bf16)
            parts.append(part)
            rest = rest - part.astype(f32)
        vectors = jnp.concatenate(
            [p.astype(f32) for p in parts] + [jnp.zeros((2, width), f32)], axis=0
        ).astype(bf16)
        part = jnp.dot(
            vectors, out_ref[f * width : (f + 1) * width, :], preferred_element_type=f32
        )
        total = part if total is None else total + part
    vec_ref[0:2, :] = total[0:2] + total[2:4] + total[4:6]


def fold(values):
    width = values.shape[1]
    if width % LANES:
        return jnp.sum(values, axis=1, keepdims=True)
    return functools.reduce(
        jnp.add, [values[:, i : i + LANES] for i in range(0, width, LANES)]
    )


def slot_place(sizes, step, u):
    _, n_seq, _, n_tp = sizes
    source = ring_source(n_seq, lax.axis_index("seq"), step)
    return source * n_tp + back(lax.axis_index("tp"), u, n_tp)


def early_body(sizes, slots, table_ref, *refs):
    x_refs = refs[: len(slots)]
    y_ref, mean_ref, square_ref = refs[len(slots) :]
    rows, width = x_refs[0].shape
    tile = 32 if rows % 32 == 0 else rows
    scales = [1.0 + table_ref[1, pl.ds(slot_place(sizes, *slot), 1), :] for slot in slots]

    def step(t, _):
        at = pl.ds(pl.multiple_of(t * tile, tile), tile)
        total = functools.reduce(jnp.add, [fold(x_ref[at, :].astype(f32)) for x_ref in x_refs])
        average = jnp.sum(total, axis=1, keepdims=True) / (len(slots) * width)
        total = None
        for s, x_ref in enumerate(x_refs):
            centred = x_ref[at, :].astype(f32) - average
            y_ref[s, at, :] = (centred * scales[s]).astype(bf16)
            part = fold(centred * centred)
            total = part if total is None else total + part
        mean_ref[at, :] = jnp.broadcast_to(average, (tile, LANES))
        square_ref[at, :] = jnp.broadcast_to(
            jnp.sum(total, axis=1, keepdims=True), (tile, LANES)
        )
        return 0

    lax.fori_loop(0, rows // tile, step, 0)


def project_body(sizes, early, last, table_ref, w_ref, vec_ref, y_ref, mean_ref, square_ref, *refs):
    x_refs = refs[: len(last)]
    q_ref, kv_ref, buf = refs[len(last) :]
    _, width = x_refs[0].shape
    head = q_ref.shape[1]
    features = (len(early) + len(last)) * width
    centre = mean_ref[:, 0:1]
    total, squares = None, None
    for s, x_ref in enumerate(x_refs):
        scale = 1.0 + table_ref[1, pl.ds(slot_place(sizes, *last[s]), 1), :]
        centred = x_ref[...].astype(f32) - centre
        buf[s] = (centred * scale).astype(bf16)
        part, square = fold(centred), fold(centred * centred)
        total = part if total is None else total + part
        squares = square if squares is None else squares + square
    delta = jnp.sum(total, axis=1, keepdims=True) / features
    spread = (square_ref[:, 0:1] + jnp.sum(squares, axis=1, keepdims=True)) / features
    inverse = lax.rsqrt(spread - delta * delta + epsilon)
    acc = None
    for s, slot in enumerate(early + last):
        first = pl.multiple_of(slot_place(sizes, *slot) * width, width)
        values = y_ref[s] if s < len(early) else buf[s - len(early)]
        part = jnp.dot(values, w_ref[pl.ds(first, width), :], preferred_element_type=f32)
        acc = part if acc is None else acc + part
    result = ((acc - delta * vec_ref[0:1, :]) * inverse + vec_ref[1:2, :]).astype(bf16)
    q_ref[...] = result[:, :head]
    kv_ref[...] = result[:, head:]


def attend_body(q_count, kv_count, factor, first, last, live_heads, *refs):
    q_refs = refs[:q_count]
    kv_refs = refs[q_count : q_count + kv_count]
    refs = refs[q_count + kv_count :]
    if not first:
        old_refs, refs = refs[:3], refs[3:]
    row = 0
    for q_ref in q_refs:
        rows, head = q_ref.shape
        at = slice(row, row + rows)
        queries = q_ref[...]
        scores = [
            lax.dot_general(
                queries,
                kv_ref[:, :head],
                (((1,), (1,)), ((), ())),
                preferred_element_type=f32,
            )
            * factor
            for kv_ref in kv_refs
        ]
        largest = jnp.max(functools.reduce(jnp.maximum, scores), axis=1, keepdims=True)
        if not first:
            old = old_refs[0][at, 0:1]
            largest = jnp.maximum(largest, old)
            rescale = jnp.exp(old - largest)
        total, weighted = None, None
        for block, kv_ref in zip(scores, kv_refs):
            weights = jnp.exp(block - largest)
            part = jnp.dot(
                weights.astype(bf16), kv_ref[:, head:], preferred_element_type=f32
            )
            weighted = part if weighted is None else weighted + part
            total = weights if total is None else total + weights
        total = jnp.sum(total, axis=1, keepdims=True)
        if not first:
            total = total + old_refs[1][at, 0:1] * rescale
            weighted = weighted + old_refs[2][at, :] * rescale
        if last:
            live = live_heads[0] > 0
            refs[0][at, :] = jnp.where(live, weighted / total, 0.0).astype(bf16)
        else:
            refs[0][at, :] = jnp.broadcast_to(largest, (rows, LANES))
            refs[1][at, :] = jnp.broadcast_to(total, (rows, LANES))
            refs[2][at, :] = weighted
        row += rows


def output_early_body(sizes, slots, last_step, sources, *refs):
    n_tp = sizes[3]
    att_refs = refs[: len(slots)]
    w_refs = refs[len(slots) : len(slots) + len(sources)]
    acc_ref, rest_ref, buf = refs[len(slots) + len(sources) :]
    for w_ref, source in zip(w_refs, sources):
        buf[source()] = w_ref[...]
    seq_at = lax.axis_index("seq")
    acc = None
    for i in range(0, len(slots), n_tp):
        values = jnp.concatenate([r[...] for r in att_refs[i : i + n_tp]], axis=1)
        weight = buf[ring_source(sizes[1], seq_at, slots[i][0])]
        part = jnp.dot(values, weight, preferred_element_type=f32)
        acc = part if acc is None else acc + part
    acc_ref[...] = acc
    rest_ref[...] = buf[ring_source(sizes[1], seq_at, last_step)]


def output_body(sizes, table_ref, acc_ref, w_ref, *refs):
    *att_refs, out_ref = refs
    values = jnp.concatenate([r[...] for r in att_refs], axis=1)
    summed = acc_ref[...] + jnp.dot(values, w_ref[...], preferred_element_type=f32)
    own = lax.axis_index("seq") * sizes[3] + lax.axis_index("tp")
    out_ref[...] = (summed * table_ref[2, pl.ds(own, 1), :]).astype(bf16)


def shares_weights(sizes):
    n_grp, _, n_blk, _ = sizes
    return n_grp == 2 and n_blk == 2


def shares_columns(sizes):
    n_grp, n_seq, n_blk, _ = sizes
    return n_grp == n_seq // n_blk


def body(sizes, *arrays):
    return block(sizes, *arrays)


def block(sizes, tokens, timestep, padded_heads, modulation, qkv_weight, out_weight):
    n_grp, n_seq, n_blk, n_tp = sizes
    slices = n_seq * n_tp
    own_width = tokens.shape[1]
    half = tokens.shape[0] // 2
    head = out_weight.shape[0]
    order = folded_order(n_seq)
    forward, backward = ring_pairs(order), ring_pairs(order, -1)
    DMA = pltpu.SemaphoreType.DMA

    current = list(
        kernel(split_body, [((half, own_width), bf16)] * 2, [(tokens, "far")], [DMA((2,))])
    )
    slots = [{}, {}]
    for step in range(n_seq):
        for chunk in range(2):
            if step:
                current[chunk] = lax.ppermute(current[chunk], "seq", forward)
            slots[chunk][step, 0] = current[chunk]
            for u in range(1, n_tp):
                slots[chunk][step, u] = lax.ppermute(current[chunk], "tp", rotation(n_tp, u))

    table = lax.dynamic_index_in_dim(modulation, timestep[0], 0, keepdims=False)
    table = table.reshape(3, slices, own_width)

    parts, pieces = [(qkv_weight, "far")], [(3, lambda b: b, None)]
    if shares_weights(sizes):
        relayed, direct = kernel(
            thirds_body, [(qkv_weight.shape[1:], bf16)] * 2, [(qkv_weight, "far")], [DMA((2,))]
        )
        first = lax.ppermute(relayed, "blk", rotation(2, 1))
        second = lax.ppermute(direct, "blk", rotation(2, 1))
        third = lax.ppermute(first, "group", rotation(2, 1))
        parts += [(first, "near"), (second, "near"), (third, "near")]
        pieces += [
            (1, lambda b: 1 - b, lambda g: g),
            (1, lambda b: 1 - b, lambda g: 2),
            (1, lambda b: 1 - b, lambda g: 1 - g),
        ]
    else:
        for j in range(1, n_blk):
            parts.append((lax.ppermute(qkv_weight, "blk", rotation(n_blk, j)), "near"))
            pieces.append((3, lambda b, j=j: back(b, j, n_blk), None))
    weight, vectors = kernel(
        functools.partial(merge_body, pieces),
        [((slices * own_width, 3 * head), bf16), ((8, 3 * head), f32)],
        [(table, "near")] + parts,
        [DMA((len(pieces), 3))],
    )

    n_low = n_seq // n_blk
    shared = shares_columns(sizes)
    o_parts, o_sources = [], []

    def source_of(k3, shift):
        def source():
            low = lax.rem(lax.axis_index("seq"), n_low)
            s = back(lax.axis_index("group"), -shift, n_grp) if shared else shift
            return back(lax.axis_index("blk"), k3, n_blk) * n_low + lax.rem(low - s + n_low, n_low)

        return source

    for k1 in range(1 if shared else n_low):
        received = list(
            kernel(
                functools.partial(columns_body, sizes, None if shared else k1),
                [((head, own_width), bf16)] * n_tp,
                [(out_weight, "far")],
                [DMA((n_tp,))],
            )
            if own_width % LANES == 0
            else [
                lax.dynamic_slice(
                    out_weight,
                    (0, column_of(sizes, None if shared else k1, u, own_width)),
                    (head, own_width),
                )
                for u in range(n_tp)
            ]
        )
        for u in range(1, n_tp):
            received[u] = lax.ppermute(received[u], "tp", rotation(n_tp, u))
        (rows,) = kernel(
            stack_body, [((n_tp * head, own_width), bf16)], [(x, "near") for x in received]
        )
        for k3 in range(1 if shared else n_blk):
            pairs = []
            for g in range(n_grp):
                for z in range(n_seq):
                    for b in range(n_blk):
                        l2 = (z % n_low + (g if shared else k1)) % n_low
                        target = (g * n_seq + b * n_low + l2) * n_blk + (z // n_low + k3) % n_blk
                        pairs.append(((g * n_seq + z) * n_blk + b, target))
            arrived = lax.ppermute(rows, ("group", "seq", "blk"), pairs)
            o_parts.append(arrived)
            o_sources.append(source_of(k3, 0 if shared else k1))
        if shared:
            for g in range(n_grp):
                for j in range(n_blk):
                    if g or j:
                        swap = [
                            (p * n_blk + b, (p + g) % n_grp * n_blk + (b + j) % n_blk)
                            for p in range(n_grp)
                            for b in range(n_blk)
                        ]
                        o_parts.append(lax.ppermute(arrived, ("group", "blk"), swap))
                        o_sources.append(source_of(j, -g))

    early = [(s, u) for s in range(n_seq - 1) for u in range(n_tp)]
    last = [(n_seq - 1, u) for u in range(n_tp)]
    starts = [
        kernel(
            functools.partial(early_body, sizes, early),
            [
                ((len(early), half, own_width), bf16),
                ((half, LANES), f32),
                ((half, LANES), f32),
            ],
            [(table, "near")] + [(slots[chunk][slot], "near") for slot in early],
        )
        for chunk in range(2)
    ]
    q_parts, kv_own, kv_rest = [], [], []
    for chunk in range(2):
        q, kv = kernel(
            functools.partial(project_body, sizes, early, last),
            [((half, head), bf16), ((half, 2 * head), bf16)],
            [(x, "near") for x in (table, weight, vectors, *starts[chunk])]
            + [(slots[chunk][slot], "near") for slot in last],
            [pltpu.VMEM((len(last), half, own_width), bf16)],
        )
        q_parts.append(q)
        kv_own.append(kv)
        for j in range(1, n_blk):
            kv_rest.append(lax.ppermute(kv, "blk", rotation(n_blk, j)))

    own_index = lax.axis_index("seq") * n_tp + lax.axis_index("tp")
    live = (own_index < slices - padded_heads).astype(jnp.int32)
    factor = 1.0 / math.sqrt(head)
    state = kernel(
        functools.partial(attend_body, 2, len(kv_own), factor, True, False),
        [((2 * half, LANES), f32), ((2 * half, LANES), f32), ((2 * half, head), f32)],
        [(live, "smem")] + [(x, "near") for x in q_parts + kv_own],
    )
    (masked,) = kernel(
        functools.partial(attend_body, 2, len(kv_rest), factor, False, True),
        [((2 * half, head), bf16)],
        [(live, "smem")] + [(x, "near") for x in (*q_parts, *kv_rest, *state)],
    )

    att = {(0, 0): masked}
    up, down = masked, masked
    last_step = n_seq // 2
    for step in range(1, last_step + 1):
        up = att[step, 0] = lax.ppermute(up, "seq", forward)
        if n_seq - step > step:
            down = att[n_seq - step, 0] = lax.ppermute(down, "seq", backward)
    for step in range(n_seq):
        for u in range(1, n_tp):
            att[step, u] = lax.ppermute(att[step, 0], "tp", rotation(n_tp, u))
    first_slots = [(s, u) for s in range(n_seq) if s != last_step for u in range(n_tp)]
    acc, rest = kernel(
        functools.partial(output_early_body, sizes, first_slots, last_step, o_sources),
        [((2 * half, own_width), f32), ((n_tp * head, own_width), bf16)],
        [(att[slot], "near") for slot in first_slots] + [(x, "near") for x in o_parts],
        [pltpu.VMEM((n_seq, n_tp * head, own_width), bf16)],
    )
    return pl.pallas_call(
        functools.partial(output_body, sizes),
        out_shape=jax.ShapeDtypeStruct((2 * half, own_width), bf16),
        in_specs=[VMEM] * (3 + n_tp),
        out_specs=VMEM,
        compiler_params=PARAMS,
        name="output",
    )(near(table), near(acc), near(rest), *[near(att[last_step, u]) for u in range(n_tp)])


def solution(mesh):
    sizes = tuple(mesh.shape[a] for a in ("group", "seq", "blk", "tp"))
    return jax.shard_map(
        functools.partial(body, sizes),
        mesh=mesh,
        in_specs=(
            P(("group", "blk"), ("seq", "tp")),
            P("group"),
            P("group"),
            P(),
            P(None, "blk", ("seq", "tp")),
            P(("seq", "tp"), "blk"),
        ),
        out_specs=P(("group", "blk"), ("seq", "tp")),
        check_vma=False,
    )
```

time: 158 us -> 89.2 us (0.56)
  waiting for transfers between devices: 98.6 us -> 17.5 us
  starting transfers between devices: 0.08 us -> 32.4 us
  blocking collectives: 26.1 us -> 0 us
  Pallas kernels: 0 us -> 19.8 us
  between operations: 14.5 us -> 1.51 us
  local copies, waits for them, and re-layouts: 5.18 us -> 17.2 us
  matrix products: 7.03 us -> 0 us
  other arithmetic: 5.73 us -> 0 us
    all_gather x2 -> x0, waiting for transfers between devices: 57.5 us -> none  [the longest x1 33.1 us: body(): lax.all_gather(qkv_weight, 'blk', axis=1, tiled=True)]
    unnamed x4 -> x0, waiting for transfers between devices: 41.1 us -> none
    ppermute x0 -> x31, starting transfers between devices: none -> 32.4 us  [the longest x6 11.9 us: block(): current[chunk] = lax.ppermute(current[chunk], 'seq', forward)]
    all_gather x3 -> x0, blocking collectives: 26.1 us -> none  [the longest x1 14.8 us: body(): lax.all_gather(out_weight, 'blk', axis=1, tiled=True)]
    pallas_call x0 -> x13, Pallas kernels: none -> 19.8 us  [the longest x12 18.8 us: kernel(): pl.pallas_call(body, out_shape=tuple((pltpu.VMEM(shape, dtype) for shape,...]
    ppermute x0 -> x31, waiting for transfers between devices: none -> 17.5 us  [the longest x6 10.1 us: block(): current[chunk] = lax.ppermute(current[chunk], 'seq', forward)]
    unnamed x4 -> x51, local copies, waits for them, and re-layouts: 4.33 us -> 17.1 us
    dot_general x6 -> x0, matrix products: 7.03 us -> none  [the longest x1 3.52 us: body(): jnp.einsum('td,kde->kte', modulated, lax.all_gather(qkv_weight, 'blk', ax...]
  transfers between devices with their start and end apart: 3 -> 31, of which waited for: 3 -> 9; matrix products, arithmetic and copies ran while one was open for 3% -> 0% of each run, Pallas kernels for 0% -> 20%
where the time goes in v1:
time: 89.2 us; the launch traced here: 88.5 us
  starting transfers between devices  32.4 us (36%)
  Pallas kernels  19.8 us (22%)
  waiting for transfers between devices  17.5 us (20%)
  local copies, waits for them, and re-layouts  17.2 us (19%)
  between operations  1.51 us (2%)
    pallas_call x12, Pallas kernels, kernel(): pl.pallas_call(body, out_shape=tuple((pltpu.VMEM(shape, dtype) for shape,...  18.8 us
    unnamed x51, local copies, waits for them, and re-layouts  17.1 us
    ppermute x6, starting transfers between devices, block(): current[chunk] = lax.ppermute(current[chunk], 'seq', forward)  11.9 us
    ppermute x6, waiting for transfers between devices, block(): current[chunk] = lax.ppermute(current[chunk], 'seq', forward)  10.1 us
    ppermute x2, starting transfers between devices, block(): up = att[step, 0] = lax.ppermute(up, 'seq', forward)  3.87 us
    ppermute x2, waiting for transfers between devices, block(): kv_rest.append(lax.ppermute(kv, 'blk', rotation(n_blk, j)))  3.79 us
    ppermute x3, starting transfers between devices, block(): o_parts.append(lax.ppermute(arrived, ('group', 'blk'), swap))  3.58 us
    ppermute x3, waiting for transfers between devices, block(): o_parts.append(lax.ppermute(arrived, ('group', 'blk'), swap))  3.24 us
  transfers between devices with their start and end apart: 31, of which 9 were waited for; matrix products, arithmetic and copies ran while one was open for 0% of the time, Pallas kernels for 20%

profile of v1, /device:TPU:0, one launch (start us, length us, event | category | flops | bytes accessed | tf_op | source)
XLA Modules:
  0.0 88.5 jit_solution(652758679309386550)
XLA Ops:
  0.0 1.1 %shard_map.73 = (bf16[128,384]{1,0:T(8,128)(2,1)S(1)}, bf16[128,384]{1,0:T(8,128)(2,1)S(1)}) custom-call(bf16[128,1536]{1,0:T(8,128)(2,1)} %w_ref.3), custom_call_target="tpu_custom_call" | custom-call | tf_op jit(solution)/shard_map/pallas_call | solution.py:56
  1.7 1.0 %shard_map.66 = (bf16[256,384]{1,0:T(8,128)(2,1)S(1)}, bf16[256,384]{1,0:T(8,128)(2,1)S(1)}) custom-call(bf16[512,384]{1,0:T(8,128)(2,1)} %x_ref.1), custom_call_target="tpu_custom_call" | custom-call | tf_op jit(solution)/shard_map/pallas_call | solution.py:56
  2.8 2.6 %collective-permute-start.4 = (bf16[256,384]{1,0:T(8,128)(2,1)S(1)}, bf16[256,384]{1,0:T(8,128)(2,1)S(1)}, u32[]{:S(2)}, u32[]{:S(2)}) collective-permute-start(bf16[256,384]{1,0:T(8,128)(2,1)S(1)} %get-tuple-element.32.refs_0_), channel_id=1, source_target_pairs={{4,12},{12,8},{8,0},{0,4},{5,13},{13,9},{9,1},{1,5},{6,14},{14,10}... | collective-permute-start | bytes 589832 | tf_op jit(solution)/shard_map/ppermute | solution.py:334
  5.4 1.9 %shard_map.64 = (bf16[1536,128]{1,0:T(8,128)(2,1)S(1)}, bf16[1536,128]{1,0:T(8,128)(2,1)}) custom-call(bf16[3,1536,128]{2,1,0:T(8,128)(2,1)} %refs_0_.1), custom_call_target="tpu_custom_call" | custom-call | tf_op jit(solution)/shard_map/pallas_call | solution.py:56
  7.3 1.6 %collective-permute-start = (bf16[1536,128]{1,0:T(8,128)(2,1)S(1)}, bf16[1536,128]{1,0:T(8,128)(2,1)S(1)}, u32[]{:S(2)}, u32[]{:S(2)}) collective-permute-start(bf16[1536,128]{1,0:T(8,128)(2,1)S(1)} %get-tuple-element.28), channel_id=1, source_target_pairs={{0,2},{2,0},{1,3},{3,1},{4,6},{6,4},{5,7},{7,5},{8,10},{10,8},{9,1... | collective-permute-start | bytes 1179656 | tf_op jit(solution)/shard_map/ppermute | solution.py:347
  8.8 2.6 %collective-permute-start.11 = (bf16[256,384]{1,0:T(8,128)(2,1)S(1)}, bf16[256,384]{1,0:T(8,128)(2,1)S(1)}, u32[]{:S(2)}, u32[]{:S(2)}) collective-permute-start(bf16[256,384]{1,0:T(8,128)(2,1)S(1)} %get-tuple-element.37.refs_0_), channel_id=1, source_target_pairs={{4,12},{12,8},{8,0},{0,4},{5,13},{13,9},{9,1},{1,5},{6,14},{14,10}... | collective-permute-start | bytes 589832 | tf_op jit(solution)/shard_map/ppermute | solution.py:334
  12.3 0.8 collective-permute-start.6
  14.5 3.0 %collective-permute-done.11.refs_2_ = bf16[256,384]{1,0:T(8,128)(2,1)S(1)} collective-permute-done((bf16[256,384]{1,0:T(8,128)(2,1)S(1)}, bf16[256,384]{1,0:T(8,128)(2,1)S(1)}, u32[]{:S(2)}, u32[]{:S(2)}) %collective-permute-start.11) | collective-permute-done | bytes 196640 | tf_op jit(solution)/shard_map/ppermute | solution.py:334
  18.2 1.7 %collective-permute-start.13 = (bf16[256,384]{1,0:T(8,128)(2,1)S(1)}, bf16[256,384]{1,0:T(8,128)(2,1)}, u32[]{:S(2)}, u32[]{:S(2)}) collective-permute-start(bf16[256,384]{1,0:T(8,128)(2,1)S(1)} %collective-permute-done.11.refs_2_), channel_id=1, source_target_pairs={{4,12},{12,8},{8,0},{0,4},{5,13},{13,9},{9,1},{1,5},{6,14},{14,10}... | collective-permute-start | bytes 589832 | tf_op jit(solution)/shard_map/ppermute | solution.py:334
  20.6 0.7 collective-permute-done.6.refs_4_
  21.9 0.7 copy-done.17
  22.6 1.5 %collective-permute-start.2 = (bf16[1536,128]{1,0:T(8,128)(2,1)S(1)}, bf16[1536,128]{1,0:T(8,128)(2,1)S(1)}, u32[]{:S(2)}, u32[]{:S(2)}) collective-permute-start(bf16[1536,128]{1,0:T(8,128)(2,1)S(1)} %collective-permute-done.refs_1_), channel_id=1, source_target_pairs={{0,16},{16,0},{1,17},{17,1},{2,18},{18,2},{3,19},{19,3},{4,20},{20... | collective-permute-start | bytes 1179656 | tf_op jit(solution)/shard_map/ppermute | solution.py:349
  24.8 2.0 %collective-permute-start.8 = (bf16[256,384]{1,0:T(8,128)(2,1)S(1)}, bf16[256,384]{1,0:T(8,128)(2,1)}, u32[]{:S(2)}, u32[]{:S(2)}) collective-permute-start(bf16[256,384]{1,0:T(8,128)(2,1)S(1)} %collective-permute-done.6.refs_4_), channel_id=1, source_target_pairs={{4,12},{12,8},{8,0},{0,4},{5,13},{13,9},{9,1},{1,5},{6,14},{14,10}... | collective-permute-start | bytes 589832 | tf_op jit(solution)/shard_map/ppermute | solution.py:334
  26.9 0.7 copy-done.15
  27.6 2.1 %collective-permute-start.15 = (bf16[256,384]{1,0:T(8,128)(2,1)}, bf16[256,384]{1,0:T(8,128)(2,1)S(1)}, u32[]{:S(2)}, u32[]{:S(2)}) collective-permute-start(bf16[256,384]{1,0:T(8,128)(2,1)} %collective-permute-done.13.refs_4_), channel_id=1, source_target_pairs={{4,12},{12,8},{8,0},{0,4},{5,13},{13,9},{9,1},{1,5},{6,14},{14,10}... | collective-permute-start | bytes 589832 | tf_op jit(solution)/shard_map/ppermute | solution.py:334
  30.4 3.2 %collective-permute-done.8.refs_0_ = bf16[256,384]{1,0:T(8,128)(2,1)} collective-permute-done((bf16[256,384]{1,0:T(8,128)(2,1)S(1)}, bf16[256,384]{1,0:T(8,128)(2,1)}, u32[]{:S(2)}, u32[]{:S(2)}) %collective-permute-start.8) | collective-permute-done | bytes 196640 | tf_op jit(solution)/shard_map/ppermute | solution.py:334
  33.6 3.1 %collective-permute-done.15.refs_0_ = bf16[256,384]{1,0:T(8,128)(2,1)S(1)} collective-permute-done((bf16[256,384]{1,0:T(8,128)(2,1)}, bf16[256,384]{1,0:T(8,128)(2,1)S(1)}, u32[]{:S(2)}, u32[]{:S(2)}) %collective-permute-start.15) | collective-permute-done | bytes 196640 | tf_op jit(solution)/shard_map/ppermute | solution.py:334
  37.5 0.9 copy-done.22
  38.4 0.9 %copy-done.24 = bf16[128,384]{1,0:T(8,128)(2,1)S(1)} copy-done((bf16[128,384]{1,0:T(8,128)(2,1)S(1)}, bf16[128,384]{1,0:T(8,128)(2,1)}, u32[]{:S(2)}) %copy-start.24) | copy-done | bytes 98328
  40.0 0.9 %copy-done.4 = bf16[256,384]{1,0:T(8,128)(2,1)S(1)} copy-done((bf16[256,384]{1,0:T(8,128)(2,1)S(1)}, bf16[256,384]{1,0:T(8,128)(2,1)}, u32[]{:S(2)}) %copy-start.4) | copy-done | bytes 196632
  40.9 0.9 %copy-done.8 = bf16[256,384]{1,0:T(8,128)(2,1)S(1)} copy-done((bf16[256,384]{1,0:T(8,128)(2,1)S(1)}, bf16[256,384]{1,0:T(8,128)(2,1)}, u32[]{:S(2)}) %copy-start.8) | copy-done | bytes 196632
  41.8 0.9 %copy-done.12 = bf16[256,384]{1,0:T(8,128)(2,1)S(1)} copy-done((bf16[256,384]{1,0:T(8,128)(2,1)S(1)}, bf16[256,384]{1,0:T(8,128)(2,1)}, u32[]{:S(2)}) %copy-start.12) | copy-done | bytes 196632
  42.8 0.9 %copy-done.16 = bf16[256,384]{1,0:T(8,128)(2,1)S(1)} copy-done((bf16[256,384]{1,0:T(8,128)(2,1)S(1)}, bf16[256,384]{1,0:T(8,128)(2,1)}, u32[]{:S(2)}) %copy-start.16) | copy-done | bytes 196632
  43.7 0.9 %copy-done.18 = bf16[256,384]{1,0:T(8,128)(2,1)S(1)} copy-done((bf16[256,384]{1,0:T(8,128)(2,1)S(1)}, bf16[256,384]{1,0:T(8,128)(2,1)}, u32[]{:S(2)}) %copy-start.18) | copy-done | bytes 196632
  44.6 0.9 %copy-done.20 = bf16[256,384]{1,0:T(8,128)(2,1)S(1)} copy-done((bf16[256,384]{1,0:T(8,128)(2,1)S(1)}, bf16[256,384]{1,0:T(8,128)(2,1)}, u32[]{:S(2)}) %copy-start.20) | copy-done | bytes 196632
  45.5 1.8 %shard_map.67 = (bf16[6,256,384]{2,1,0:T(8,128)(2,1)S(1)}, f32[256,128]{1,0:T(8,128)S(1)}, f32[256,128]{1,0:T(8,128)S(1)}) custom-call(f32[3,8,384]{2,1,0:T(8,128)S(1)} %bitcast.9, bf16[256,384]{1,0:T(8,128)(2,1)S(1)} %copy-done.4, bf16[256,384]{1,0:T(8,128)(2,1)S(1)} %copy-done.12, bf16[256,384]{1,0:T(8,128)(2,1)S(1)} %copy-done.8, ...), custom_call_target="tpu_custom_call" | custom-call | tf_op jit(solution)/shard_map/pallas_call | solution.py:56
  47.3 3.0 %collective-permute-start.25 = (bf16[256,384]{1,0:T(8,128)(2,1)}, bf16[256,384]{1,0:T(8,128)(2,1)}, u32[]{:S(2)}, u32[]{:S(2)}) collective-permute-start(bf16[256,384]{1,0:T(8,128)(2,1)} %shard_map.74), channel_id=1, source_target_pairs={{0,0},{2,8},{4,4},{6,12},{8,2},{10,10},{12,6},{14,14},{16,20},{18,... | collective-permute-start | bytes 589832 | tf_op jit(solution)/shard_map/ppermute | solution.py:410
  50.3 0.9 %copy-done.2 = bf16[256,384]{1,0:T(8,128)(2,1)S(1)} copy-done((bf16[256,384]{1,0:T(8,128)(2,1)S(1)}, bf16[256,384]{1,0:T(8,128)(2,1)}, u32[]{:S(2)}) %copy-start.2) | copy-done | bytes 196632
  51.3 0.9 %copy-done.6 = bf16[256,384]{1,0:T(8,128)(2,1)S(1)} copy-done((bf16[256,384]{1,0:T(8,128)(2,1)S(1)}, bf16[256,384]{1,0:T(8,128)(2,1)}, u32[]{:S(2)}) %copy-start.6) | copy-done | bytes 196632
  52.2 0.9 %copy-done.10 = bf16[256,384]{1,0:T(8,128)(2,1)S(1)} copy-done((bf16[256,384]{1,0:T(8,128)(2,1)S(1)}, bf16[256,384]{1,0:T(8,128)(2,1)}, u32[]{:S(2)}) %copy-start.10) | copy-done | bytes 196632
  53.1 0.9 %copy-done.14 = bf16[256,384]{1,0:T(8,128)(2,1)S(1)} copy-done((bf16[256,384]{1,0:T(8,128)(2,1)S(1)}, bf16[256,384]{1,0:T(8,128)(2,1)}, u32[]{:S(2)}) %copy-start.14) | copy-done | bytes 196632
  54.0 2.8 %shard_map.69 = (bf16[6,256,384]{2,1,0:T(8,128)(2,1)S(1)}, f32[256,128]{1,0:T(8,128)S(1)}, f32[256,128]{1,0:T(8,128)S(1)}) custom-call(f32[3,8,384]{2,1,0:T(8,128)S(1)} %bitcast.10, bf16[256,384]{1,0:T(8,128)(2,1)S(1)} %copy-done.2, bf16[256,384]{1,0:T(8,128)(2,1)S(1)} %copy-done.10, bf16[256,384]{1,0:T(8,128)(2,1)S(1)} %copy-done.6, ...), custom_call_target="tpu_custom_call" | custom-call | tf_op jit(solution)/shard_map/pallas_call | solution.py:56
  56.9 1.8 %shard_map.65 = (bf16[3072,384]{1,0:T(8,128)(2,1)S(1)}, f32[8,384]{1,0:T(8,128)S(1)}) custom-call(f32[3,8,384]{2,1,0:T(8,128)S(1)} %bitcast.11, bf16[3,1536,128]{2,1,0:T(8,128)(2,1)} %refs_0_.1, bf16[1536,128]{1,0:T(8,128)(2,1)S(1)} %collective-permute-done.refs_1_, bf16[1536,128]{1,0:T(8,128)(2,1)S(1)} %collective-permute-done.1.refs_2_, ...), custom_call_target="tpu_custom_call" | custom-call | tf_op jit(solution)/shard_map/pallas_call | solution.py:56
  58.7 2.2 %shard_map.68 = (bf16[256,128]{1,0:T(8,128)(2,1)S(1)}, bf16[256,256]{1,0:T(8,128)(2,1)S(1)}) custom-call(f32[3,8,384]{2,1,0:T(8,128)S(1)} %bitcast.12, bf16[3072,384]{1,0:T(8,128)(2,1)S(1)} %get-tuple-element.30.w_ref, f32[8,384]{1,0:T(8,128)S(1)} %get-tuple-element.31.vec_ref, bf16[6,256,384]{2,1,0:T(8,128)(2,1)S(1)} %get-tuple-element.33.y_ref, ...), custom_call_target="tpu_custom_call" | custom-call | tf_op jit(solution)/shard_map/pallas_call | solution.py:56
  60.9 2.0 %collective-permute-start.17 = (bf16[256,256]{1,0:T(8,128)(2,1)S(1)}, bf16[256,256]{1,0:T(8,128)(2,1)S(1)}, u32[]{:S(2)}, u32[]{:S(2)}) collective-permute-start(bf16[256,256]{1,0:T(8,128)(2,1)S(1)} %get-tuple-element.42.refs_2_), channel_id=1, source_target_pairs={{0,2},{2,0},{1,3},{3,1},{4,6},{6,4},{5,7},{7,5},{8,10},{10,8},{9,1... | collective-permute-start | bytes 393224 | tf_op jit(solution)/shard_map/ppermute | solution.py:451
  62.9 2.1 %shard_map.70 = (bf16[256,128]{1,0:T(8,128)(2,1)S(1)}, bf16[256,256]{1,0:T(8,128)(2,1)S(1)}) custom-call(f32[3,8,384]{2,1,0:T(8,128)S(1)} %bitcast.13, bf16[3072,384]{1,0:T(8,128)(2,1)S(1)} %get-tuple-element.30.w_ref, f32[8,384]{1,0:T(8,128)S(1)} %get-tuple-element.31.vec_ref, bf16[6,256,384]{2,1,0:T(8,128)(2,1)S(1)} %get-tuple-element.38.y_ref, ...), custom_call_target="tpu_custom_call" | custom-call | tf_op jit(solution)/shard_map/pallas_call | solution.py:56
  65.8 0.8 shard_map.71
  66.9 3.5 %collective-permute-done.18.refs_3_ = bf16[256,256]{1,0:T(8,128)(2,1)S(1)} collective-permute-done((bf16[256,256]{1,0:T(8,128)(2,1)S(1)}, bf16[256,256]{1,0:T(8,128)(2,1)S(1)}, u32[]{:S(2)}, u32[]{:S(2)}) %collective-permute-start.18) | collective-permute-done | bytes 131104 | tf_op jit(solution)/shard_map/ppermute | solution.py:451
  70.4 1.0 %shard_map.72.refs_0_ = bf16[512,128]{1,0:T(8,128)(2,1)S(1)} custom-call(s32[1]{0:T(128)S(6)} %convert_element_type.3.live_heads, bf16[256,128]{1,0:T(8,128)(2,1)S(1)} %get-tuple-element.36.refs_0_, bf16[256,128]{1,0:T(8,128)(2,1)S(1)} %get-tuple-element.41.refs_1_, bf16[256,256]{1,0:T(8,128)(2,1)S(1)} %collective-permute-done.17.refs_2_, ...), custom_call_target="tpu_custom_call" | custom-call | tf_op jit(solution)/shard_map/pallas_call | solution.py:56
  71.4 2.7 %collective-permute-start.20 = (bf16[512,128]{1,0:T(8,128)(2,1)S(1)}, bf16[512,128]{1,0:T(8,128)(2,1)S(1)}, u32[]{:S(2)}, u32[]{:S(2)}) collective-permute-start(bf16[512,128]{1,0:T(8,128)(2,1)S(1)} %shard_map.72.refs_0_), channel_id=1, source_target_pairs={{4,12},{12,8},{8,0},{0,4},{5,13},{13,9},{9,1},{1,5},{6,14},{14,10}... | collective-permute-start | bytes 393224 | tf_op jit(solution)/shard_map/ppermute | solution.py:471
  74.1 0.9 %collective-permute-start.26 = (bf16[256,384]{1,0:T(8,128)(2,1)}, bf16[256,384]{1,0:T(8,128)(2,1)S(1)}, u32[]{:S(2)}, u32[]{:S(2)}) collective-permute-start(bf16[256,384]{1,0:T(8,128)(2,1)} %collective-permute-done.25.refs_6_), channel_id=1, source_target_pairs={{0,2},{2,0},{16,18},{18,16},{1,3},{3,1},{17,19},{19,17},{4,6},{6,4... | collective-permute-start | bytes 589832 | tf_op jit(solution)/shard_map/ppermute | solution.py:422
  75.0 2.8 %collective-permute-start.22 = (bf16[512,128]{1,0:T(8,128)(2,1)S(1)}, bf16[512,128]{1,0:T(8,128)(2,1)S(1)}, u32[]{:S(2)}, u32[]{:S(2)}) collective-permute-start(bf16[512,128]{1,0:T(8,128)(2,1)S(1)} %shard_map.72.refs_0_), channel_id=1, source_target_pairs={{4,0},{12,4},{8,12},{0,8},{5,1},{13,5},{9,13},{1,9},{6,2},{14,6},{... | collective-permute-start | bytes 393224 | tf_op jit(solution)/shard_map/ppermute | solution.py:473
  77.8 1.2 %collective-permute-start.29 = (bf16[512,128]{1,0:T(8,128)(2,1)S(1)}, bf16[512,128]{1,0:T(8,128)(2,1)S(1)}, u32[]{:S(2)}, u32[]{:S(2)}) collective-permute-start(bf16[512,128]{1,0:T(8,128)(2,1)S(1)} %collective-permute-done.20.refs_2_), channel_id=1, source_target_pairs={{4,12},{12,8},{8,0},{0,4},{5,13},{13,9},{9,1},{1,5},{6,14},{14,10}... | collective-permute-start | bytes 393224 | tf_op jit(solution)/shard_map/ppermute | solution.py:471
  79.0 2.6 %collective-permute-start.28 = (bf16[256,384]{1,0:T(8,128)(2,1)}, bf16[256,384]{1,0:T(8,128)(2,1)S(1)}, u32[]{:S(2)}, u32[]{:S(2)}) collective-permute-start(bf16[256,384]{1,0:T(8,128)(2,1)} %collective-permute-done.25.refs_6_), channel_id=1, source_target_pairs={{0,18},{2,16},{16,2},{18,0},{1,19},{3,17},{17,3},{19,1},{4,22},{6,... | collective-permute-start | bytes 589832 | tf_op jit(solution)/shard_map/ppermute | solution.py:422
  81.7 1.4 %collective-permute-done.27.refs_8_ = bf16[256,384]{1,0:T(8,128)(2,1)S(1)} collective-permute-done((bf16[256,384]{1,0:T(8,128)(2,1)}, bf16[256,384]{1,0:T(8,128)(2,1)S(1)}, u32[]{:S(2)}, u32[]{:S(2)}) %collective-permute-start.27) | collective-permute-done | bytes 196640 | tf_op jit(solution)/shard_map/ppermute | solution.py:422
  83.9 1.9 %collective-permute-done.28.refs_9_ = bf16[256,384]{1,0:T(8,128)(2,1)S(1)} collective-permute-done((bf16[256,384]{1,0:T(8,128)(2,1)}, bf16[256,384]{1,0:T(8,128)(2,1)S(1)}, u32[]{:S(2)}, u32[]{:S(2)}) %collective-permute-start.28) | collective-permute-done | bytes 196640 | tf_op jit(solution)/shard_map/ppermute | solution.py:422
  85.8 1.6 %shard_map.75 = (f32[512,384]{1,0:T(8,128)S(1)}, bf16[256,384]{1,0:T(8,128)(2,1)S(1)}) custom-call(bf16[512,128]{1,0:T(8,128)(2,1)S(1)} %shard_map.72.refs_0_, bf16[512,128]{1,0:T(8,128)(2,1)S(1)} %collective-permute-done.19.refs_1_, bf16[512,128]{1,0:T(8,128)(2,1)S(1)} %collective-permute-done.20.refs_2_, ...), custom_call_target="tpu_custom_call" | custom-call | tf_op jit(solution)/shard_map/pallas_call | solution.py:56
  87.4 1.0 %output.1 = bf16[512,384]{1,0:T(8,128)(2,1)} custom-call(f32[3,8,384]{2,1,0:T(8,128)S(1)} %bitcast.14, f32[512,384]{1,0:T(8,128)S(1)} %get-tuple-element.49.acc_ref, bf16[256,384]{1,0:T(8,128)(2,1)S(1)} %get-tuple-element.50.w_ref, bf16[512,128]{1,0:T(8,128)(2,1)S(1)} %collective-permute-done.29.refs_0_, bf16[512,128]{1,0:T(8,128)(2,1)S(1)} %collective-permute-done.30.refs_1_), custom_call_target="tpu_custom_call" | custom-call | tf_op jit(solution)/shard_map/output/pallas_call | solution.py:484
  (79 shorter events, 8.4 us)
Async XLA Ops:
  0.0 37.4 %copy-start = (f32[50,3,3072]{2,0,1:T(8,128)S(1)}, f32[50,3,3072]{2,0,1:T(8,128)}, u32[]{:S(2)}) copy-start(f32[50,3,3072]{2,0,1:T(8,128)} %param.9) | copy-start | bytes 5529604
  1.1 1.6 %copy-start.21 = (bf16[128,384]{1,0:T(8,128)(2,1)}, bf16[128,384]{1,0:T(8,128)(2,1)S(1)}, u32[]{:S(2)}) copy-start(bf16[128,384]{1,0:T(8,128)(2,1)S(1)} %get-tuple-element.47.refs_0_) | copy-start | bytes 294916
  1.1 10.3 %collective-permute-start.24 = (bf16[128,384]{1,0:T(8,128)(2,1)S(1)}, bf16[128,384]{1,0:T(8,128)(2,1)S(1)}, u32[]{:S(2)}, u32[]{:S(2)}) collective-permute-start(bf16[128,384]{1,0:T(8,128)(2,1)S(1)} %get-tuple-element.48), channel_id=1, source_target_pairs={{0,1},{1,0},{2,3},{3,2},{4,5},{5,4},{6,7},{7,6},{8,9},{9,8},{10,11... | collective-permute-start | bytes 294920 | tf_op jit(solution)/shard_map/ppermute | solution.py:398
  2.7 34.0 %copy-start.1 = (bf16[256,384]{1,0:T(8,128)(2,1)}, bf16[256,384]{1,0:T(8,128)(2,1)S(1)}, u32[]{:S(2)}) copy-start(bf16[256,384]{1,0:T(8,128)(2,1)S(1)} %get-tuple-element.37.refs_0_) | copy-start | bytes 589828
  2.7 34.0 %copy-start.3 = (bf16[256,384]{1,0:T(8,128)(2,1)}, bf16[256,384]{1,0:T(8,128)(2,1)S(1)}, u32[]{:S(2)}) copy-start(bf16[256,384]{1,0:T(8,128)(2,1)S(1)} %get-tuple-element.32.refs_0_) | copy-start | bytes 589828
  2.8 9.5 %collective-permute-start.4 = (bf16[256,384]{1,0:T(8,128)(2,1)S(1)}, bf16[256,384]{1,0:T(8,128)(2,1)S(1)}, u32[]{:S(2)}, u32[]{:S(2)}) collective-permute-start(bf16[256,384]{1,0:T(8,128)(2,1)S(1)} %get-tuple-element.32.refs_0_), channel_id=1, source_target_pairs={{4,12},{12,8},{8,0},{0,4},{5,13},{13,9},{9,1},{1,5},{6,14},{14,10}... | collective-permute-start | bytes 589832 | tf_op jit(solution)/shard_map/ppermute | solution.py:334
  7.3 14.0 %collective-permute-start = (bf16[1536,128]{1,0:T(8,128)(2,1)S(1)}, bf16[1536,128]{1,0:T(8,128)(2,1)S(1)}, u32[]{:S(2)}, u32[]{:S(2)}) collective-permute-start(bf16[1536,128]{1,0:T(8,128)(2,1)S(1)} %get-tuple-element.28), channel_id=1, source_target_pairs={{0,2},{2,0},{1,3},{3,1},{4,6},{6,4},{5,7},{7,5},{8,10},{10,8},{9,1... | collective-permute-start | bytes 1179656 | tf_op jit(solution)/shard_map/ppermute | solution.py:347
  8.8 4.3 %collective-permute-start.3 = (bf16[256,384]{1,0:T(8,128)(2,1)S(1)}, bf16[256,384]{1,0:T(8,128)(2,1)S(1)}, u32[]{:S(2)}, u32[]{:S(2)}) collective-permute-start(bf16[256,384]{1,0:T(8,128)(2,1)S(1)} %get-tuple-element.32.refs_0_), channel_id=1, source_target_pairs={{0,1},{1,0},{2,3},{3,2},{4,5},{5,4},{6,7},{7,6},{8,9},{9,8},{10,11... | collective-permute-start | bytes 589832 | tf_op jit(solution)/shard_map/ppermute | solution.py:337
  8.8 8.7 %collective-permute-start.11 = (bf16[256,384]{1,0:T(8,128)(2,1)S(1)}, bf16[256,384]{1,0:T(8,128)(2,1)S(1)}, u32[]{:S(2)}, u32[]{:S(2)}) collective-permute-start(bf16[256,384]{1,0:T(8,128)(2,1)S(1)} %get-tuple-element.37.refs_0_), channel_id=1, source_target_pairs={{4,12},{12,8},{8,0},{0,4},{5,13},{13,9},{9,1},{1,5},{6,14},{14,10}... | collective-permute-start | bytes 589832 | tf_op jit(solution)/shard_map/ppermute | solution.py:334
  12.0 5.5 %collective-permute-start.10 = (bf16[256,384]{1,0:T(8,128)(2,1)S(1)}, bf16[256,384]{1,0:T(8,128)(2,1)S(1)}, u32[]{:S(2)}, u32[]{:S(2)}) collective-permute-start(bf16[256,384]{1,0:T(8,128)(2,1)S(1)} %get-tuple-element.37.refs_0_), channel_id=1, source_target_pairs={{0,1},{1,0},{2,3},{3,2},{4,5},{5,4},{6,7},{7,6},{8,9},{9,8},{10,11... | collective-permute-start | bytes 589832 | tf_op jit(solution)/shard_map/ppermute | solution.py:337
  12.3 9.0 %collective-permute-start.6 = (bf16[256,384]{1,0:T(8,128)(2,1)S(1)}, bf16[256,384]{1,0:T(8,128)(2,1)S(1)}, u32[]{:S(2)}, u32[]{:S(2)}) collective-permute-start(bf16[256,384]{1,0:T(8,128)(2,1)S(1)} %collective-permute-done.4.refs_2_), channel_id=1, source_target_pairs={{4,12},{12,8},{8,0},{0,4},{5,13},{13,9},{9,1},{1,5},{6,14},{14,10}... | collective-permute-start | bytes 589832 | tf_op jit(solution)/shard_map/ppermute | solution.py:334
  13.8 8.2 %collective-permute-start.5 = (bf16[256,384]{1,0:T(8,128)(2,1)S(1)}, bf16[256,384]{1,0:T(8,128)(2,1)S(1)}, u32[]{:S(2)}, u32[]{:S(2)}) collective-permute-start(bf16[256,384]{1,0:T(8,128)(2,1)S(1)} %collective-permute-done.4.refs_2_), channel_id=1, source_target_pairs={{0,1},{1,0},{2,3},{3,2},{4,5},{5,4},{6,7},{7,6},{8,9},{9,8},{10,11... | collective-permute-start | bytes 589832 | tf_op jit(solution)/shard_map/ppermute | solution.py:337
  17.5 6.6 %collective-permute-start.12 = (bf16[256,384]{1,0:T(8,128)(2,1)S(1)}, bf16[256,384]{1,0:T(8,128)(2,1)S(1)}, u32[]{:S(2)}, u32[]{:S(2)}) collective-permute-start(bf16[256,384]{1,0:T(8,128)(2,1)S(1)} %collective-permute-done.11.refs_2_), channel_id=1, source_target_pairs={{0,1},{1,0},{2,3},{3,2},{4,5},{5,4},{6,7},{7,6},{8,9},{9,8},{10,11... | collective-permute-start | bytes 589832 | tf_op jit(solution)/shard_map/ppermute | solution.py:337
  18.2 9.4 %collective-permute-start.13 = (bf16[256,384]{1,0:T(8,128)(2,1)S(1)}, bf16[256,384]{1,0:T(8,128)(2,1)}, u32[]{:S(2)}, u32[]{:S(2)}) collective-permute-start(bf16[256,384]{1,0:T(8,128)(2,1)S(1)} %collective-permute-done.11.refs_2_), channel_id=1, source_target_pairs={{4,12},{12,8},{8,0},{0,4},{5,13},{13,9},{9,1},{1,5},{6,14},{14,10}... | collective-permute-start | bytes 589832 | tf_op jit(solution)/shard_map/ppermute | solution.py:334
  21.3 8.4 %collective-permute-start.7 = (bf16[256,384]{1,0:T(8,128)(2,1)S(1)}, bf16[256,384]{1,0:T(8,128)(2,1)S(1)}, u32[]{:S(2)}, u32[]{:S(2)}) collective-permute-start(bf16[256,384]{1,0:T(8,128)(2,1)S(1)} %collective-permute-done.6.refs_4_), channel_id=1, source_target_pairs={{0,1},{1,0},{2,3},{3,2},{4,5},{5,4},{6,7},{7,6},{8,9},{9,8},{10,11... | collective-permute-start | bytes 589832 | tf_op jit(solution)/shard_map/ppermute | solution.py:337
  21.3 35.6 %collective-permute-start.1 = (bf16[1536,128]{1,0:T(8,128)(2,1)}, bf16[1536,128]{1,0:T(8,128)(2,1)S(1)}, u32[]{:S(2)}, u32[]{:S(2)}) collective-permute-start(bf16[1536,128]{1,0:T(8,128)(2,1)} %get-tuple-element.29), channel_id=1, source_target_pairs={{0,2},{2,0},{1,3},{3,1},{4,6},{6,4},{5,7},{7,5},{8,10},{10,8},{9,1... | collective-permute-start | bytes 1179656 | tf_op jit(solution)/shard_map/ppermute | solution.py:348
  21.9 0.7 copy-start.17
  22.6 34.2 %collective-permute-start.2 = (bf16[1536,128]{1,0:T(8,128)(2,1)S(1)}, bf16[1536,128]{1,0:T(8,128)(2,1)S(1)}, u32[]{:S(2)}, u32[]{:S(2)}) collective-permute-start(bf16[1536,128]{1,0:T(8,128)(2,1)S(1)} %collective-permute-done.refs_1_), channel_id=1, source_target_pairs={{0,16},{16,0},{1,17},{17,1},{2,18},{18,2},{3,19},{19,3},{4,20},{20... | collective-permute-start | bytes 1179656 | tf_op jit(solution)/shard_map/ppermute | solution.py:349
  24.8 8.8 %collective-permute-start.8 = (bf16[256,384]{1,0:T(8,128)(2,1)S(1)}, bf16[256,384]{1,0:T(8,128)(2,1)}, u32[]{:S(2)}, u32[]{:S(2)}) collective-permute-start(bf16[256,384]{1,0:T(8,128)(2,1)S(1)} %collective-permute-done.6.refs_4_), channel_id=1, source_target_pairs={{4,12},{12,8},{8,0},{0,4},{5,13},{13,9},{9,1},{1,5},{6,14},{14,10}... | collective-permute-start | bytes 589832 | tf_op jit(solution)/shard_map/ppermute | solution.py:334
  27.6 9.1 %collective-permute-start.15 = (bf16[256,384]{1,0:T(8,128)(2,1)}, bf16[256,384]{1,0:T(8,128)(2,1)S(1)}, u32[]{:S(2)}, u32[]{:S(2)}) collective-permute-start(bf16[256,384]{1,0:T(8,128)(2,1)} %collective-permute-done.13.refs_4_), channel_id=1, source_target_pairs={{4,12},{12,8},{8,0},{0,4},{5,13},{13,9},{9,1},{1,5},{6,14},{14,10}... | collective-permute-start | bytes 589832 | tf_op jit(solution)/shard_map/ppermute | solution.py:334
  30.4 17.0 %collective-permute-start.14 = (bf16[256,384]{1,0:T(8,128)(2,1)}, bf16[256,384]{1,0:T(8,128)(2,1)}, u32[]{:S(2)}, u32[]{:S(2)}) collective-permute-start(bf16[256,384]{1,0:T(8,128)(2,1)} %collective-permute-done.13.refs_4_), channel_id=1, source_target_pairs={{0,1},{1,0},{2,3},{3,2},{4,5},{5,4},{6,7},{7,6},{8,9},{9,8},{10,11... | collective-permute-start | bytes 589832 | tf_op jit(solution)/shard_map/ppermute | solution.py:337
  33.6 25.1 %collective-permute-start.9 = (bf16[256,384]{1,0:T(8,128)(2,1)}, bf16[256,384]{1,0:T(8,128)(2,1)}, u32[]{:S(2)}, u32[]{:S(2)}) collective-permute-start(bf16[256,384]{1,0:T(8,128)(2,1)} %collective-permute-done.8.refs_0_), channel_id=1, source_target_pairs={{0,1},{1,0},{2,3},{3,2},{4,5},{5,4},{6,7},{7,6},{8,9},{9,8},{10,11... | collective-permute-start | bytes 589832 | tf_op jit(solution)/shard_map/ppermute | solution.py:337
  36.7 26.2 %collective-permute-start.16 = (bf16[256,384]{1,0:T(8,128)(2,1)S(1)}, bf16[256,384]{1,0:T(8,128)(2,1)}, u32[]{:S(2)}, u32[]{:S(2)}) collective-permute-start(bf16[256,384]{1,0:T(8,128)(2,1)S(1)} %collective-permute-done.15.refs_0_), channel_id=1, source_target_pairs={{0,1},{1,0},{2,3},{3,2},{4,5},{5,4},{6,7},{7,6},{8,9},{9,8},{10,11... | collective-permute-start | bytes 589832 | tf_op jit(solution)/shard_map/ppermute | solution.py:337
  37.5 0.9 %copy-start.22 = (bf16[128,384]{1,0:T(8,128)(2,1)S(1)}, bf16[128,384]{1,0:T(8,128)(2,1)}, u32[]{:S(2)}) copy-start(bf16[128,384]{1,0:T(8,128)(2,1)} %copy-done.21) | copy-start | bytes 294916
  38.4 0.9 %copy-start.24 = (bf16[128,384]{1,0:T(8,128)(2,1)S(1)}, bf16[128,384]{1,0:T(8,128)(2,1)}, u32[]{:S(2)}) copy-start(bf16[128,384]{1,0:T(8,128)(2,1)} %copy-done.23) | copy-start | bytes 294916
  40.0 0.9 %copy-start.4 = (bf16[256,384]{1,0:T(8,128)(2,1)S(1)}, bf16[256,384]{1,0:T(8,128)(2,1)}, u32[]{:S(2)}) copy-start(bf16[256,384]{1,0:T(8,128)(2,1)} %copy-done.3) | copy-start | bytes 589828
  40.9 0.9 %copy-start.8 = (bf16[256,384]{1,0:T(8,128)(2,1)S(1)}, bf16[256,384]{1,0:T(8,128)(2,1)}, u32[]{:S(2)}) copy-start(bf16[256,384]{1,0:T(8,128)(2,1)} %copy-done.7) | copy-start | bytes 589828
  41.8 0.9 %copy-start.12 = (bf16[256,384]{1,0:T(8,128)(2,1)S(1)}, bf16[256,384]{1,0:T(8,128)(2,1)}, u32[]{:S(2)}) copy-start(bf16[256,384]{1,0:T(8,128)(2,1)} %copy-done.11) | copy-start | bytes 589828
  42.8 0.9 %copy-start.16 = (bf16[256,384]{1,0:T(8,128)(2,1)S(1)}, bf16[256,384]{1,0:T(8,128)(2,1)}, u32[]{:S(2)}) copy-start(bf16[256,384]{1,0:T(8,128)(2,1)} %copy-done.15) | copy-start | bytes 589828
  43.7 0.9 %copy-start.18 = (bf16[256,384]{1,0:T(8,128)(2,1)S(1)}, bf16[256,384]{1,0:T(8,128)(2,1)}, u32[]{:S(2)}) copy-start(bf16[256,384]{1,0:T(8,128)(2,1)} %copy-done.17) | copy-start | bytes 589828
  44.6 0.9 %copy-start.20 = (bf16[256,384]{1,0:T(8,128)(2,1)S(1)}, bf16[256,384]{1,0:T(8,128)(2,1)}, u32[]{:S(2)}) copy-start(bf16[256,384]{1,0:T(8,128)(2,1)} %copy-done.19) | copy-start | bytes 589828
  47.3 26.7 %collective-permute-start.25 = (bf16[256,384]{1,0:T(8,128)(2,1)}, bf16[256,384]{1,0:T(8,128)(2,1)}, u32[]{:S(2)}, u32[]{:S(2)}) collective-permute-start(bf16[256,384]{1,0:T(8,128)(2,1)} %shard_map.74), channel_id=1, source_target_pairs={{0,0},{2,8},{4,4},{6,12},{8,2},{10,10},{12,6},{14,14},{16,20},{18,... | collective-permute-start | bytes 589832 | tf_op jit(solution)/shard_map/ppermute | solution.py:410
  50.3 0.9 %copy-start.2 = (bf16[256,384]{1,0:T(8,128)(2,1)S(1)}, bf16[256,384]{1,0:T(8,128)(2,1)}, u32[]{:S(2)}) copy-start(bf16[256,384]{1,0:T(8,128)(2,1)} %copy-done.1) | copy-start | bytes 589828
  51.3 0.9 %copy-start.6 = (bf16[256,384]{1,0:T(8,128)(2,1)S(1)}, bf16[256,384]{1,0:T(8,128)(2,1)}, u32[]{:S(2)}) copy-start(bf16[256,384]{1,0:T(8,128)(2,1)} %copy-done.5) | copy-start | bytes 589828
  52.2 0.9 %copy-start.10 = (bf16[256,384]{1,0:T(8,128)(2,1)S(1)}, bf16[256,384]{1,0:T(8,128)(2,1)}, u32[]{:S(2)}) copy-start(bf16[256,384]{1,0:T(8,128)(2,1)} %copy-done.9) | copy-start | bytes 589828
  53.1 0.9 %copy-start.14 = (bf16[256,384]{1,0:T(8,128)(2,1)S(1)}, bf16[256,384]{1,0:T(8,128)(2,1)}, u32[]{:S(2)}) copy-start(bf16[256,384]{1,0:T(8,128)(2,1)} %copy-done.13) | copy-start | bytes 589828
  60.9 6.0 %collective-permute-start.17 = (bf16[256,256]{1,0:T(8,128)(2,1)S(1)}, bf16[256,256]{1,0:T(8,128)(2,1)S(1)}, u32[]{:S(2)}, u32[]{:S(2)}) collective-permute-start(bf16[256,256]{1,0:T(8,128)(2,1)S(1)} %get-tuple-element.42.refs_2_), channel_id=1, source_target_pairs={{0,2},{2,0},{1,3},{3,1},{4,6},{6,4},{5,7},{7,5},{8,10},{10,8},{9,1... | collective-permute-start | bytes 393224 | tf_op jit(solution)/shard_map/ppermute | solution.py:451
  65.0 5.4 %collective-permute-start.18 = (bf16[256,256]{1,0:T(8,128)(2,1)S(1)}, bf16[256,256]{1,0:T(8,128)(2,1)S(1)}, u32[]{:S(2)}, u32[]{:S(2)}) collective-permute-start(bf16[256,256]{1,0:T(8,128)(2,1)S(1)} %get-tuple-element.43.refs_3_), channel_id=1, source_target_pairs={{0,2},{2,0},{1,3},{3,1},{4,6},{6,4},{5,7},{7,5},{8,10},{10,8},{9,1... | collective-permute-start | bytes 393224 | tf_op jit(solution)/shard_map/ppermute | solution.py:451
  71.4 6.5 %collective-permute-start.20 = (bf16[512,128]{1,0:T(8,128)(2,1)S(1)}, bf16[512,128]{1,0:T(8,128)(2,1)S(1)}, u32[]{:S(2)}, u32[]{:S(2)}) collective-permute-start(bf16[512,128]{1,0:T(8,128)(2,1)S(1)} %shard_map.72.refs_0_), channel_id=1, source_target_pairs={{4,12},{12,8},{8,0},{0,4},{5,13},{13,9},{9,1},{1,5},{6,14},{14,10}... | collective-permute-start | bytes 393224 | tf_op jit(solution)/shard_map/ppermute | solution.py:471
  74.1 7.6 %collective-permute-start.26 = (bf16[256,384]{1,0:T(8,128)(2,1)}, bf16[256,384]{1,0:T(8,128)(2,1)S(1)}, u32[]{:S(2)}, u32[]{:S(2)}) collective-permute-start(bf16[256,384]{1,0:T(8,128)(2,1)} %collective-permute-done.25.refs_6_), channel_id=1, source_target_pairs={{0,2},{2,0},{16,18},{18,16},{1,3},{3,1},{17,19},{19,17},{4,6},{6,4... | collective-permute-start | bytes 589832 | tf_op jit(solution)/shard_map/ppermute | solution.py:422
  75.0 8.1 %collective-permute-start.27 = (bf16[256,384]{1,0:T(8,128)(2,1)}, bf16[256,384]{1,0:T(8,128)(2,1)S(1)}, u32[]{:S(2)}, u32[]{:S(2)}) collective-permute-start(bf16[256,384]{1,0:T(8,128)(2,1)} %collective-permute-done.25.refs_6_), channel_id=1, source_target_pairs={{0,16},{2,18},{16,0},{18,2},{1,17},{3,19},{17,1},{19,3},{4,20},{6,... | collective-permute-start | bytes 589832 | tf_op jit(solution)/shard_map/ppermute | solution.py:422
  75.0 8.0 %collective-permute-start.22 = (bf16[512,128]{1,0:T(8,128)(2,1)S(1)}, bf16[512,128]{1,0:T(8,128)(2,1)S(1)}, u32[]{:S(2)}, u32[]{:S(2)}) collective-permute-start(bf16[512,128]{1,0:T(8,128)(2,1)S(1)} %shard_map.72.refs_0_), channel_id=1, source_target_pairs={{4,0},{12,4},{8,12},{0,8},{5,1},{13,5},{9,13},{1,9},{6,2},{14,6},{... | collective-permute-start | bytes 393224 | tf_op jit(solution)/shard_map/ppermute | solution.py:473
  77.8 6.1 %collective-permute-start.29 = (bf16[512,128]{1,0:T(8,128)(2,1)S(1)}, bf16[512,128]{1,0:T(8,128)(2,1)S(1)}, u32[]{:S(2)}, u32[]{:S(2)}) collective-permute-start(bf16[512,128]{1,0:T(8,128)(2,1)S(1)} %collective-permute-done.20.refs_2_), channel_id=1, source_target_pairs={{4,12},{12,8},{8,0},{0,4},{5,13},{13,9},{9,1},{1,5},{6,14},{14,10}... | collective-permute-start | bytes 393224 | tf_op jit(solution)/shard_map/ppermute | solution.py:471
  79.0 6.8 %collective-permute-start.28 = (bf16[256,384]{1,0:T(8,128)(2,1)}, bf16[256,384]{1,0:T(8,128)(2,1)S(1)}, u32[]{:S(2)}, u32[]{:S(2)}) collective-permute-start(bf16[256,384]{1,0:T(8,128)(2,1)} %collective-permute-done.25.refs_6_), channel_id=1, source_target_pairs={{0,18},{2,16},{16,2},{18,0},{1,19},{3,17},{17,3},{19,1},{4,22},{6,... | collective-permute-start | bytes 589832 | tf_op jit(solution)/shard_map/ppermute | solution.py:422
  81.7 4.1 %collective-permute-start.19 = (bf16[512,128]{1,0:T(8,128)(2,1)S(1)}, bf16[512,128]{1,0:T(8,128)(2,1)S(1)}, u32[]{:S(2)}, u32[]{:S(2)}) collective-permute-start(bf16[512,128]{1,0:T(8,128)(2,1)S(1)} %shard_map.72.refs_0_), channel_id=1, source_target_pairs={{0,1},{1,0},{2,3},{3,2},{4,5},{5,4},{6,7},{7,6},{8,9},{9,8},{10,11... | collective-permute-start | bytes 393224 | tf_op jit(solution)/shard_map/ppermute | solution.py:476
  83.0 2.8 %collective-permute-start.21 = (bf16[512,128]{1,0:T(8,128)(2,1)S(1)}, bf16[512,128]{1,0:T(8,128)(2,1)S(1)}, u32[]{:S(2)}, u32[]{:S(2)}) collective-permute-start(bf16[512,128]{1,0:T(8,128)(2,1)S(1)} %collective-permute-done.20.refs_2_), channel_id=1, source_target_pairs={{0,1},{1,0},{2,3},{3,2},{4,5},{5,4},{6,7},{7,6},{8,9},{9,8},{10,11... | collective-permute-start | bytes 393224 | tf_op jit(solution)/shard_map/ppermute | solution.py:476
  83.0 2.8 %collective-permute-start.23 = (bf16[512,128]{1,0:T(8,128)(2,1)S(1)}, bf16[512,128]{1,0:T(8,128)(2,1)S(1)}, u32[]{:S(2)}, u32[]{:S(2)}) collective-permute-start(bf16[512,128]{1,0:T(8,128)(2,1)S(1)} %collective-permute-done.22.refs_4_), channel_id=1, source_target_pairs={{0,1},{1,0},{2,3},{3,2},{4,5},{5,4},{6,7},{7,6},{8,9},{9,8},{10,11... | collective-permute-start | bytes 393224 | tf_op jit(solution)/shard_map/ppermute | solution.py:476
  83.9 3.5 %collective-permute-start.30 = (bf16[512,128]{1,0:T(8,128)(2,1)S(1)}, bf16[512,128]{1,0:T(8,128)(2,1)S(1)}, u32[]{:S(2)}, u32[]{:S(2)}) collective-permute-start(bf16[512,128]{1,0:T(8,128)(2,1)S(1)} %collective-permute-done.29.refs_0_), channel_id=1, source_target_pairs={{0,1},{1,0},{2,3},{3,2},{4,5},{5,4},{6,7},{7,6},{8,9},{9,8},{10,11... | collective-permute-start | bytes 393224 | tf_op jit(solution)/shard_map/ppermute | solution.py:476
  (8 other events, 5.4 us)

commit v2 on v1

--- a/solution.py
+++ b/solution.py
@@ -70,23 +70,28 @@
         copy.wait()
 
 
-def split_body(x_ref, top_ref, bottom_ref, sem):
+def split_body(shared, x_ref, w_ref, top_ref, bottom_ref, *refs):
     half = top_ref.shape[0]
-    run_copies(
-        [
-            pltpu.make_async_copy(x_ref.at[pl.ds(0, half)], top_ref, sem.at[0]),
-            pltpu.make_async_copy(x_ref.at[pl.ds(half, half)], bottom_ref, sem.at[1]),
+    sem = refs[-1]
+    copies = [
+        pltpu.make_async_copy(x_ref.at[pl.ds(0, half)], top_ref, sem.at[0]),
+        pltpu.make_async_copy(x_ref.at[pl.ds(half, half)], bottom_ref, sem.at[1]),
+    ]
+    if shared:
+        plane = lax.axis_index("group")
+        copies += [
+            pltpu.make_async_copy(w_ref.at[plane], refs[0], sem.at[2]),
+            pltpu.make_async_copy(w_ref.at[2], refs[1], sem.at[3]),
         ]
-    )
-
-
-def thirds_body(w_ref, relayed_ref, direct_ref, sem):
-    run_copies(
-        [
-            pltpu.make_async_copy(w_ref.at[lax.axis_index("group")], relayed_ref, sem.at[0]),
-            pltpu.make_async_copy(w_ref.at[2], direct_ref, sem.at[1]),
-        ]
-    )
+    run_copies(copies)
+
+
+def table_body(at, m_ref, out_ref):
+    _, slices, width = out_ref.shape
+    for i in range(3):
+        row = m_ref[i, pl.ds(at[0], 1), :]
+        for f in range(slices):
+            out_ref[i, f : f + 1, :] = row[:, f * width : (f + 1) * width]
 
 
 def column_of(sizes, shift, u, width):
@@ -175,7 +180,7 @@
     x_refs = refs[: len(slots)]
     y_ref, mean_ref, square_ref = refs[len(slots) :]
     rows, width = x_refs[0].shape
-    tile = 32 if rows % 32 == 0 else rows
+    tile = rows
     scales = [1.0 + table_ref[1, pl.ds(slot_place(sizes, *slot), 1), :] for slot in slots]
 
     def step(t, _):
@@ -226,7 +231,7 @@
     kv_ref[...] = result[:, head:]
 
 
-def attend_body(q_count, kv_count, factor, first, last, live_heads, *refs):
+def attend_body(sizes, q_count, kv_count, factor, first, last, padded, *refs):
     q_refs = refs[:q_count]
     kv_refs = refs[q_count : q_count + kv_count]
     refs = refs[q_count + kv_count :]
@@ -265,7 +270,8 @@
             total = total + old_refs[1][at, 0:1] * rescale
             weighted = weighted + old_refs[2][at, :] * rescale
         if last:
-            live = live_heads[0] > 0
+            own = lax.axis_index("seq") * sizes[3] + lax.axis_index("tp")
+            live = own < sizes[1] * sizes[3] - padded[0]
             refs[0][at, :] = jnp.where(live, weighted / total, 0.0).astype(bf16)
         else:
             refs[0][at, :] = jnp.broadcast_to(largest, (rows, LANES))
@@ -324,9 +330,14 @@
     forward, backward = ring_pairs(order), ring_pairs(order, -1)
     DMA = pltpu.SemaphoreType.DMA
 
-    current = list(
-        kernel(split_body, [((half, own_width), bf16)] * 2, [(tokens, "far")], [DMA((2,))])
-    )
+    by_two = shares_weights(sizes)
+    cut = kernel(
+        functools.partial(split_body, by_two),
+        [((half, own_width), bf16)] * 2 + [(qkv_weight.shape[1:], bf16)] * (2 if by_two else 0),
+        [(tokens, "far"), (qkv_weight, "far")],
+        [DMA((4,))],
+    )
+    current = list(cut[:2])
     slots = [{}, {}]
     for step in range(n_seq):
         for chunk in range(2):
@@ -336,14 +347,15 @@
             for u in range(1, n_tp):
                 slots[chunk][step, u] = lax.ppermute(current[chunk], "tp", rotation(n_tp, u))
 
-    table = lax.dynamic_index_in_dim(modulation, timestep[0], 0, keepdims=False)
-    table = table.reshape(3, slices, own_width)
+    (table,) = kernel(
+        table_body,
+        [((3, slices, own_width), f32)],
+        [(timestep, "smem"), (jnp.swapaxes(modulation, 0, 1), "near")],
+    )
 
     parts, pieces = [(qkv_weight, "far")], [(3, lambda b: b, None)]
-    if shares_weights(sizes):
-        relayed, direct = kernel(
-            thirds_body, [(qkv_weight.shape[1:], bf16)] * 2, [(qkv_weight, "far")], [DMA((2,))]
-        )
+    if by_two:
+        relayed, direct = cut[2:]
         first = lax.ppermute(relayed, "blk", rotation(2, 1))
         second = lax.ppermute(direct, "blk", rotation(2, 1))
         third = lax.ppermute(first, "group", rotation(2, 1))
@@ -450,18 +462,16 @@
         for j in range(1, n_blk):
             kv_rest.append(lax.ppermute(kv, "blk", rotation(n_blk, j)))
 
-    own_index = lax.axis_index("seq") * n_tp + lax.axis_index("tp")
-    live = (own_index < slices - padded_heads).astype(jnp.int32)
     factor = 1.0 / math.sqrt(head)
     state = kernel(
-        functools.partial(attend_body, 2, len(kv_own), factor, True, False),
+        functools.partial(attend_body, sizes, 2, len(kv_own), factor, True, False),
         [((2 * half, LANES), f32), ((2 * half, LANES), f32), ((2 * half, head), f32)],
-        [(live, "smem")] + [(x, "near") for x in q_parts + kv_own],
+        [(padded_heads, "smem")] + [(x, "near") for x in q_parts + kv_own],
     )
     (masked,) = kernel(
-        functools.partial(attend_body, 2, len(kv_rest), factor, False, True),
+        functools.partial(attend_body, sizes, 2, len(kv_rest), factor, False, True),
         [((2 * half, head), bf16)],
-        [(live, "smem")] + [(x, "near") for x in (*q_parts, *kv_rest, *state)],
+        [(padded_heads, "smem")] + [(x, "near") for x in (*q_parts, *kv_rest, *state)],
     )
 
     att = {(0, 0): masked}

time: 89.2 us -> 76.5 us (0.86)
  local copies, waits for them, and re-layouts: 17.2 us -> 1.57 us
  waiting for transfers between devices: 17.5 us -> 29 us
  Pallas kernels: 19.8 us -> 11.4 us
    unnamed x51 -> x2, local copies, waits for them, and re-layouts: 17.1 us -> 1.57 us
    pallas_call x12, Pallas kernels: 18.8 us -> 10.3 us  [kernel(): pl.pallas_call(body, out_shape=tuple((pltpu.VMEM(shape, dtype) for shape,...]
    ppermute x6, waiting for transfers between devices: 10.1 us -> 16.1 us  [block(): current[chunk] = lax.ppermute(current[chunk], 'seq', forward)]
    ppermute x2, waiting for transfers between devices: 3.79 us -> 6.33 us  [block(): kv_rest.append(lax.ppermute(kv, 'blk', rotation(n_blk, j)))]
    ppermute x2, waiting for transfers between devices: 0.38 us -> 2.85 us  [block(): up = att[step, 0] = lax.ppermute(up, 'seq', forward)]
    ppermute x1, starting transfers between devices: 2.98 us -> 0.66 us  [block(): arrived = lax.ppermute(rows, ('group', 'seq', 'blk'), pairs)]
    ppermute x2, starting transfers between devices: 2.16 us -> 4.39 us  [block(): kv_rest.append(lax.ppermute(kv, 'blk', rotation(n_blk, j)))]
    ppermute x3, starting transfers between devices: 3.58 us -> 2.61 us  [block(): o_parts.append(lax.ppermute(arrived, ('group', 'blk'), swap))]
  transfers between devices with their start and end apart: 31 -> 31, of which waited for: 9 -> 10; matrix products, arithmetic and copies ran while one was open for 0% -> 0% of each run, Pallas kernels for 20% -> 12%
where the time goes in v2:
time: 76.5 us; the launch traced here: 75.9 us
  starting transfers between devices  32.5 us (42%)
  waiting for transfers between devices  29 us (38%)
  Pallas kernels  11.4 us (15%)
  local copies, waits for them, and re-layouts  1.57 us (2%)
  between operations  1.45 us (2%)
    ppermute x6, waiting for transfers between devices, block(): current[chunk] = lax.ppermute(current[chunk], 'seq', forward)  16.1 us
    ppermute x6, starting transfers between devices, block(): current[chunk] = lax.ppermute(current[chunk], 'seq', forward)  11.6 us
    pallas_call x12, Pallas kernels, kernel(): pl.pallas_call(body, out_shape=tuple((pltpu.VMEM(shape, dtype) for shape,...  10.3 us
    ppermute x2, waiting for transfers between devices, block(): kv_rest.append(lax.ppermute(kv, 'blk', rotation(n_blk, j)))  6.33 us
    ppermute x2, starting transfers between devices, block(): up = att[step, 0] = lax.ppermute(up, 'seq', forward)  4.76 us
    ppermute x2, starting transfers between devices, block(): kv_rest.append(lax.ppermute(kv, 'blk', rotation(n_blk, j)))  4.39 us
    ppermute x3, waiting for transfers between devices, block(): o_parts.append(lax.ppermute(arrived, ('group', 'blk'), swap))  3.62 us
    ppermute x2, waiting for transfers between devices, block(): up = att[step, 0] = lax.ppermute(up, 'seq', forward)  2.85 us
  transfers between devices with their start and end apart: 31, of which 10 were waited for; matrix products, arithmetic and copies ran while one was open for 0% of the time, Pallas kernels for 12%

profile of v2, /device:TPU:0, one launch (start us, length us, event | category | flops | bytes accessed | tf_op | source)
XLA Modules:
  0.0 75.9 jit_solution(4641054471536063189)
XLA Ops:
  0.0 1.0 %shard_map.73 = (bf16[128,384]{1,0:T(8,128)(2,1)S(1)}, bf16[128,384]{1,0:T(8,128)(2,1)S(1)}) custom-call(bf16[128,1536]{1,0:T(8,128)(2,1)} %w_ref.3), custom_call_target="tpu_custom_call" | custom-call | tf_op jit(solution)/shard_map/pallas_call | solution.py:56
  1.0 0.6 collective-permute-start.24
  1.5 1.3 %shard_map.65 = (bf16[256,384]{1,0:T(8,128)(2,1)S(1)}, bf16[256,384]{1,0:T(8,128)(2,1)S(1)}, bf16[1536,128]{1,0:T(8,128)(2,1)S(1)}, bf16[1536,128]{1,0:T(8,128)(2,1)S(1)}) custom-call(bf16[512,384]{1,0:T(8,128)(2,1)} %x_ref.1, bf16[3,1536,128]{2,1,0:T(8,128)(2,1)} %refs_0_.1), custom_call_target="tpu_custom_call" | custom-call | tf_op jit(solution)/shard_map/pallas_call | solution.py:56
  2.9 2.6 %collective-permute-start.4 = (bf16[256,384]{1,0:T(8,128)(2,1)S(1)}, bf16[256,384]{1,0:T(8,128)(2,1)S(1)}, u32[]{:S(2)}, u32[]{:S(2)}) collective-permute-start(bf16[256,384]{1,0:T(8,128)(2,1)S(1)} %get-tuple-element.32.refs_0_), channel_id=1, source_target_pairs={{4,12},{12,8},{8,0},{0,4},{5,13},{13,9},{9,1},{1,5},{6,14},{14,10}... | collective-permute-start | bytes 589832 | tf_op jit(solution)/shard_map/ppermute | solution.py:345
  5.5 1.5 %collective-permute-start = (bf16[1536,128]{1,0:T(8,128)(2,1)S(1)}, bf16[1536,128]{1,0:T(8,128)(2,1)S(1)}, u32[]{:S(2)}, u32[]{:S(2)}) collective-permute-start(bf16[1536,128]{1,0:T(8,128)(2,1)S(1)} %get-tuple-element.28), channel_id=1, source_target_pairs={{0,2},{2,0},{1,3},{3,1},{4,6},{6,4},{5,7},{7,5},{8,10},{10,8},{9,1... | collective-permute-start | bytes 1179656 | tf_op jit(solution)/shard_map/ppermute | solution.py:359
  7.0 2.6 %collective-permute-start.11 = (bf16[256,384]{1,0:T(8,128)(2,1)S(1)}, bf16[256,384]{1,0:T(8,128)(2,1)S(1)}, u32[]{:S(2)}, u32[]{:S(2)}) collective-permute-start(bf16[256,384]{1,0:T(8,128)(2,1)S(1)} %get-tuple-element.37.refs_0_), channel_id=1, source_target_pairs={{4,12},{12,8},{8,0},{0,4},{5,13},{13,9},{9,1},{1,5},{6,14},{14,10}... | collective-permute-start | bytes 589832 | tf_op jit(solution)/shard_map/ppermute | solution.py:345
  9.6 0.0 collective-permute-done.24.refs_1_
  9.6 0.2 collective-permute-start.10
  9.8 2.4 %collective-permute-done.4.refs_2_ = bf16[256,384]{1,0:T(8,128)(2,1)S(1)} collective-permute-done((bf16[256,384]{1,0:T(8,128)(2,1)S(1)}, bf16[256,384]{1,0:T(8,128)(2,1)S(1)}, u32[]{:S(2)}, u32[]{:S(2)}) %collective-permute-start.4) | collective-permute-done | bytes 196640 | tf_op jit(solution)/shard_map/ppermute | solution.py:345
  12.3 1.1 %collective-permute-start.6 = (bf16[256,384]{1,0:T(8,128)(2,1)S(1)}, bf16[256,384]{1,0:T(8,128)(2,1)S(1)}, u32[]{:S(2)}, u32[]{:S(2)}) collective-permute-start(bf16[256,384]{1,0:T(8,128)(2,1)S(1)} %collective-permute-done.4.refs_2_), channel_id=1, source_target_pairs={{4,12},{12,8},{8,0},{0,4},{5,13},{13,9},{9,1},{1,5},{6,14},{14,10}... | collective-permute-start | bytes 589832 | tf_op jit(solution)/shard_map/ppermute | solution.py:345
  13.4 0.0 collective-permute-done.3.refs_1_
  13.4 0.0 collective-permute-start.5
  13.4 3.1 %collective-permute-done.11.refs_2_ = bf16[256,384]{1,0:T(8,128)(2,1)S(1)} collective-permute-done((bf16[256,384]{1,0:T(8,128)(2,1)S(1)}, bf16[256,384]{1,0:T(8,128)(2,1)S(1)}, u32[]{:S(2)}, u32[]{:S(2)}) %collective-permute-start.11) | collective-permute-done | bytes 196640 | tf_op jit(solution)/shard_map/ppermute | solution.py:345
  16.5 1.1 %collective-permute-start.13 = (bf16[256,384]{1,0:T(8,128)(2,1)S(1)}, bf16[256,384]{1,0:T(8,128)(2,1)S(1)}, u32[]{:S(2)}, u32[]{:S(2)}) collective-permute-start(bf16[256,384]{1,0:T(8,128)(2,1)S(1)} %collective-permute-done.11.refs_2_), channel_id=1, source_target_pairs={{4,12},{12,8},{8,0},{0,4},{5,13},{13,9},{9,1},{1,5},{6,14},{14,10}... | collective-permute-start | bytes 589832 | tf_op jit(solution)/shard_map/ppermute | solution.py:345
  17.6 2.9 %collective-permute-done.6.refs_4_ = bf16[256,384]{1,0:T(8,128)(2,1)S(1)} collective-permute-done((bf16[256,384]{1,0:T(8,128)(2,1)S(1)}, bf16[256,384]{1,0:T(8,128)(2,1)S(1)}, u32[]{:S(2)}, u32[]{:S(2)}) %collective-permute-start.6) | collective-permute-done | bytes 196640 | tf_op jit(solution)/shard_map/ppermute | solution.py:345
  20.5 1.5 %collective-permute-start.1 = (bf16[1536,128]{1,0:T(8,128)(2,1)S(1)}, bf16[1536,128]{1,0:T(8,128)(2,1)S(1)}, u32[]{:S(2)}, u32[]{:S(2)}) collective-permute-start(bf16[1536,128]{1,0:T(8,128)(2,1)S(1)} %get-tuple-element.29), channel_id=1, source_target_pairs={{0,2},{2,0},{1,3},{3,1},{4,6},{6,4},{5,7},{7,5},{8,10},{10,8},{9,1... | collective-permute-start | bytes 1179656 | tf_op jit(solution)/shard_map/ppermute | solution.py:360
  22.1 1.5 %collective-permute-start.2 = (bf16[1536,128]{1,0:T(8,128)(2,1)S(1)}, bf16[1536,128]{1,0:T(8,128)(2,1)S(1)}, u32[]{:S(2)}, u32[]{:S(2)}) collective-permute-start(bf16[1536,128]{1,0:T(8,128)(2,1)S(1)} %collective-permute-done.refs_1_), channel_id=1, source_target_pairs={{0,16},{16,0},{1,17},{17,1},{2,18},{18,2},{3,19},{19,3},{4,20},{20... | collective-permute-start | bytes 1179656 | tf_op jit(solution)/shard_map/ppermute | solution.py:361
  23.6 1.2 %collective-permute-start.8 = (bf16[256,384]{1,0:T(8,128)(2,1)S(1)}, bf16[256,384]{1,0:T(8,128)(2,1)S(1)}, u32[]{:S(2)}, u32[]{:S(2)}) collective-permute-start(bf16[256,384]{1,0:T(8,128)(2,1)S(1)} %collective-permute-done.6.refs_4_), channel_id=1, source_target_pairs={{4,12},{12,8},{8,0},{0,4},{5,13},{13,9},{9,1},{1,5},{6,14},{14,10}... | collective-permute-start | bytes 589832 | tf_op jit(solution)/shard_map/ppermute | solution.py:345
  24.7 3.0 %collective-permute-start.15 = (bf16[256,384]{1,0:T(8,128)(2,1)S(1)}, bf16[256,384]{1,0:T(8,128)(2,1)S(1)}, u32[]{:S(2)}, u32[]{:S(2)}) collective-permute-start(bf16[256,384]{1,0:T(8,128)(2,1)S(1)} %collective-permute-done.13.refs_4_), channel_id=1, source_target_pairs={{4,12},{12,8},{8,0},{0,4},{5,13},{13,9},{9,1},{1,5},{6,14},{14,10}... | collective-permute-start | bytes 589832 | tf_op jit(solution)/shard_map/ppermute | solution.py:345
  27.8 4.5 %collective-permute-done.8.refs_0_ = bf16[256,384]{1,0:T(8,128)(2,1)S(1)} collective-permute-done((bf16[256,384]{1,0:T(8,128)(2,1)S(1)}, bf16[256,384]{1,0:T(8,128)(2,1)S(1)}, u32[]{:S(2)}, u32[]{:S(2)}) %collective-permute-start.8) | collective-permute-done | bytes 196640 | tf_op jit(solution)/shard_map/ppermute | solution.py:345
  32.3 3.2 %collective-permute-done.15.refs_0_ = bf16[256,384]{1,0:T(8,128)(2,1)S(1)} collective-permute-done((bf16[256,384]{1,0:T(8,128)(2,1)S(1)}, bf16[256,384]{1,0:T(8,128)(2,1)S(1)}, u32[]{:S(2)}, u32[]{:S(2)}) %collective-permute-start.15) | collective-permute-done | bytes 196640 | tf_op jit(solution)/shard_map/ppermute | solution.py:345
  36.1 0.0 copy-start
  36.1 1.6 %copy-done = f32[50,3,3072]{2,0,1:T(8,128)S(1)} copy-done((f32[50,3,3072]{2,0,1:T(8,128)S(1)}, f32[50,3,3072]{2,0,1:T(8,128)}, u32[]{:S(2)}) %copy-start) | copy-done | bytes 1843224
  37.7 0.7 shard_map.67
  38.4 0.7 collective-permute-start.25
  39.1 0.7 shard_map.69
  39.8 1.8 %shard_map.66 = (bf16[3072,384]{1,0:T(8,128)(2,1)S(1)}, f32[8,384]{1,0:T(8,128)S(1)}) custom-call(f32[3,8,384]{2,1,0:T(8,128)S(1)} %shard_map.64.table_ref, bf16[3,1536,128]{2,1,0:T(8,128)(2,1)} %refs_0_.1, bf16[1536,128]{1,0:T(8,128)(2,1)S(1)} %collective-permute-done.refs_1_, bf16[1536,128]{1,0:T(8,128)(2,1)S(1)} %collective-permute-done.1.refs_2_, ...), custom_call_target="tpu_custom_call" | custom-call | tf_op jit(solution)/shard_map/pallas_call | solution.py:56
  41.6 1.2 %shard_map.68 = (bf16[256,128]{1,0:T(8,128)(2,1)S(1)}, bf16[256,256]{1,0:T(8,128)(2,1)S(1)}) custom-call(f32[3,8,384]{2,1,0:T(8,128)S(1)} %shard_map.64.table_ref, bf16[3072,384]{1,0:T(8,128)(2,1)S(1)} %get-tuple-element.30.w_ref, f32[8,384]{1,0:T(8,128)S(1)} %get-tuple-element.31.vec_ref, bf16[6,256,384]{2,1,0:T(8,128)(2,1)S(1)} %get-tuple-element.33.y_ref, ...), custom_call_target="tpu_custom_call" | custom-call | tf_op jit(solution)/shard_map/pallas_call | solution.py:56
  42.8 4.3 %collective-permute-start.17 = (bf16[256,256]{1,0:T(8,128)(2,1)S(1)}, bf16[256,256]{1,0:T(8,128)(2,1)S(1)}, u32[]{:S(2)}, u32[]{:S(2)}) collective-permute-start(bf16[256,256]{1,0:T(8,128)(2,1)S(1)} %get-tuple-element.42.refs_2_), channel_id=1, source_target_pairs={{0,2},{2,0},{1,3},{3,1},{4,6},{6,4},{5,7},{7,5},{8,10},{10,8},{9,1... | collective-permute-start | bytes 393224 | tf_op jit(solution)/shard_map/ppermute | solution.py:463
  47.1 1.2 %shard_map.70 = (bf16[256,128]{1,0:T(8,128)(2,1)S(1)}, bf16[256,256]{1,0:T(8,128)(2,1)S(1)}) custom-call(f32[3,8,384]{2,1,0:T(8,128)S(1)} %shard_map.64.table_ref, bf16[3072,384]{1,0:T(8,128)(2,1)S(1)} %get-tuple-element.30.w_ref, f32[8,384]{1,0:T(8,128)S(1)} %get-tuple-element.31.vec_ref, bf16[6,256,384]{2,1,0:T(8,128)(2,1)S(1)} %get-tuple-element.38.y_ref, ...), custom_call_target="tpu_custom_call" | custom-call | tf_op jit(solution)/shard_map/pallas_call | solution.py:56
  48.3 0.1 collective-permute-start.18
  49.0 0.8 %shard_map.71 = (f32[512,128]{1,0:T(8,128)S(1)}, f32[512,128]{1,0:T(8,128)S(1)}, f32[512,128]{1,0:T(8,128)S(1)}) custom-call(s32[1]{0:T(128)S(6)} %copy.8.padded, bf16[256,128]{1,0:T(8,128)(2,1)S(1)} %get-tuple-element.36.refs_0_, bf16[256,128]{1,0:T(8,128)(2,1)S(1)} %get-tuple-element.41.refs_1_, bf16[256,256]{1,0:T(8,128)(2,1)S(1)} %get-tuple-element.42.refs_2_, ...), custom_call_target="tpu_custom_call" | custom-call | tf_op jit(solution)/shard_map/pallas_call | solution.py:56
  49.8 4.3 %collective-permute-done.17.refs_2_ = bf16[256,256]{1,0:T(8,128)(2,1)S(1)} collective-permute-done((bf16[256,256]{1,0:T(8,128)(2,1)S(1)}, bf16[256,256]{1,0:T(8,128)(2,1)S(1)}, u32[]{:S(2)}, u32[]{:S(2)}) %collective-permute-start.17) | collective-permute-done | bytes 131104 | tf_op jit(solution)/shard_map/ppermute | solution.py:463
  54.1 2.1 %collective-permute-done.18.refs_3_ = bf16[256,256]{1,0:T(8,128)(2,1)S(1)} collective-permute-done((bf16[256,256]{1,0:T(8,128)(2,1)S(1)}, bf16[256,256]{1,0:T(8,128)(2,1)S(1)}, u32[]{:S(2)}, u32[]{:S(2)}) %collective-permute-start.18) | collective-permute-done | bytes 131104 | tf_op jit(solution)/shard_map/ppermute | solution.py:463
  56.2 1.0 %shard_map.72.refs_0_ = bf16[512,128]{1,0:T(8,128)(2,1)S(1)} custom-call(s32[1]{0:T(128)S(6)} %copy.8.padded, bf16[256,128]{1,0:T(8,128)(2,1)S(1)} %get-tuple-element.36.refs_0_, bf16[256,128]{1,0:T(8,128)(2,1)S(1)} %get-tuple-element.41.refs_1_, bf16[256,256]{1,0:T(8,128)(2,1)S(1)} %collective-permute-done.17.refs_2_, ...), custom_call_target="tpu_custom_call" | custom-call | tf_op jit(solution)/shard_map/pallas_call | solution.py:56
  57.1 0.3 collective-permute-start.20
  57.5 2.3 %collective-permute-start.26 = (bf16[256,384]{1,0:T(8,128)(2,1)S(1)}, bf16[256,384]{1,0:T(8,128)(2,1)S(1)}, u32[]{:S(2)}, u32[]{:S(2)}) collective-permute-start(bf16[256,384]{1,0:T(8,128)(2,1)S(1)} %collective-permute-done.25.refs_6_), channel_id=1, source_target_pairs={{0,2},{2,0},{16,18},{18,16},{1,3},{3,1},{17,19},{19,17},{4,6},{6,4... | collective-permute-start | bytes 589832 | tf_op jit(solution)/shard_map/ppermute | solution.py:434
  59.8 0.3 collective-permute-start.27
  60.1 2.5 %collective-permute-start.22 = (bf16[512,128]{1,0:T(8,128)(2,1)S(1)}, bf16[512,128]{1,0:T(8,128)(2,1)S(1)}, u32[]{:S(2)}, u32[]{:S(2)}) collective-permute-start(bf16[512,128]{1,0:T(8,128)(2,1)S(1)} %shard_map.72.refs_0_), channel_id=1, source_target_pairs={{4,0},{12,4},{8,12},{0,8},{5,1},{13,5},{9,13},{1,9},{6,2},{14,6},{... | collective-permute-start | bytes 393224 | tf_op jit(solution)/shard_map/ppermute | solution.py:483
  62.6 0.5 collective-permute-done.20.refs_2_
  63.1 4.4 %collective-permute-start.29 = (bf16[512,128]{1,0:T(8,128)(2,1)S(1)}, bf16[512,128]{1,0:T(8,128)(2,1)S(1)}, u32[]{:S(2)}, u32[]{:S(2)}) collective-permute-start(bf16[512,128]{1,0:T(8,128)(2,1)S(1)} %collective-permute-done.20.refs_2_), channel_id=1, source_target_pairs={{4,12},{12,8},{8,0},{0,4},{5,13},{13,9},{9,1},{1,5},{6,14},{14,10}... | collective-permute-start | bytes 393224 | tf_op jit(solution)/shard_map/ppermute | solution.py:481
  67.6 0.5 collective-permute-start.21
  68.1 0.1 collective-permute-start.23
  68.2 2.3 %collective-permute-done.29.refs_0_ = bf16[512,128]{1,0:T(8,128)(2,1)S(1)} collective-permute-done((bf16[512,128]{1,0:T(8,128)(2,1)S(1)}, bf16[512,128]{1,0:T(8,128)(2,1)S(1)}, u32[]{:S(2)}, u32[]{:S(2)}) %collective-permute-start.29) | collective-permute-done | bytes 131104 | tf_op jit(solution)/shard_map/ppermute | solution.py:481
  70.5 0.0 collective-permute-start.30
  70.5 3.6 %collective-permute-done.28.refs_9_ = bf16[256,384]{1,0:T(8,128)(2,1)S(1)} collective-permute-done((bf16[256,384]{1,0:T(8,128)(2,1)S(1)}, bf16[256,384]{1,0:T(8,128)(2,1)S(1)}, u32[]{:S(2)}, u32[]{:S(2)}) %collective-permute-start.28) | collective-permute-done | bytes 196640 | tf_op jit(solution)/shard_map/ppermute | solution.py:434
  74.2 0.7 shard_map.75
  74.9 1.1 %output.1 = bf16[512,384]{1,0:T(8,128)(2,1)} custom-call(f32[3,8,384]{2,1,0:T(8,128)S(1)} %shard_map.64.table_ref, f32[512,384]{1,0:T(8,128)S(1)} %get-tuple-element.49.acc_ref, bf16[256,384]{1,0:T(8,128)(2,1)S(1)} %get-tuple-element.50.w_ref, bf16[512,128]{1,0:T(8,128)(2,1)S(1)} %collective-permute-done.29.refs_0_, ...), custom_call_target="tpu_custom_call" | custom-call | tf_op jit(solution)/shard_map/output/pallas_call | solution.py:494
  (29 shorter events, 0.1 us)
Async XLA Ops:
  1.0 8.6 %collective-permute-start.24 = (bf16[128,384]{1,0:T(8,128)(2,1)S(1)}, bf16[128,384]{1,0:T(8,128)(2,1)S(1)}, u32[]{:S(2)}, u32[]{:S(2)}) collective-permute-start(bf16[128,384]{1,0:T(8,128)(2,1)S(1)} %get-tuple-element.48), channel_id=1, source_target_pairs={{0,1},{1,0},{2,3},{3,2},{4,5},{5,4},{6,7},{7,6},{8,9},{9,8},{10,11... | collective-permute-start | bytes 294920 | tf_op jit(solution)/shard_map/ppermute | solution.py:410
  2.9 9.4 %collective-permute-start.4 = (bf16[256,384]{1,0:T(8,128)(2,1)S(1)}, bf16[256,384]{1,0:T(8,128)(2,1)S(1)}, u32[]{:S(2)}, u32[]{:S(2)}) collective-permute-start(bf16[256,384]{1,0:T(8,128)(2,1)S(1)} %get-tuple-element.32.refs_0_), channel_id=1, source_target_pairs={{4,12},{12,8},{8,0},{0,4},{5,13},{13,9},{9,1},{1,5},{6,14},{14,10}... | collective-permute-start | bytes 589832 | tf_op jit(solution)/shard_map/ppermute | solution.py:345
  5.5 15.0 %collective-permute-start = (bf16[1536,128]{1,0:T(8,128)(2,1)S(1)}, bf16[1536,128]{1,0:T(8,128)(2,1)S(1)}, u32[]{:S(2)}, u32[]{:S(2)}) collective-permute-start(bf16[1536,128]{1,0:T(8,128)(2,1)S(1)} %get-tuple-element.28), channel_id=1, source_target_pairs={{0,2},{2,0},{1,3},{3,1},{4,6},{6,4},{5,7},{7,5},{8,10},{10,8},{9,1... | collective-permute-start | bytes 1179656 | tf_op jit(solution)/shard_map/ppermute | solution.py:359
  7.0 6.4 %collective-permute-start.3 = (bf16[256,384]{1,0:T(8,128)(2,1)S(1)}, bf16[256,384]{1,0:T(8,128)(2,1)S(1)}, u32[]{:S(2)}, u32[]{:S(2)}) collective-permute-start(bf16[256,384]{1,0:T(8,128)(2,1)S(1)} %get-tuple-element.32.refs_0_), channel_id=1, source_target_pairs={{0,1},{1,0},{2,3},{3,2},{4,5},{5,4},{6,7},{7,6},{8,9},{9,8},{10,11... | collective-permute-start | bytes 589832 | tf_op jit(solution)/shard_map/ppermute | solution.py:348
  7.0 9.5 %collective-permute-start.11 = (bf16[256,384]{1,0:T(8,128)(2,1)S(1)}, bf16[256,384]{1,0:T(8,128)(2,1)S(1)}, u32[]{:S(2)}, u32[]{:S(2)}) collective-permute-start(bf16[256,384]{1,0:T(8,128)(2,1)S(1)} %get-tuple-element.37.refs_0_), channel_id=1, source_target_pairs={{4,12},{12,8},{8,0},{0,4},{5,13},{13,9},{9,1},{1,5},{6,14},{14,10}... | collective-permute-start | bytes 589832 | tf_op jit(solution)/shard_map/ppermute | solution.py:345
  9.6 6.9 %collective-permute-start.10 = (bf16[256,384]{1,0:T(8,128)(2,1)S(1)}, bf16[256,384]{1,0:T(8,128)(2,1)S(1)}, u32[]{:S(2)}, u32[]{:S(2)}) collective-permute-start(bf16[256,384]{1,0:T(8,128)(2,1)S(1)} %get-tuple-element.37.refs_0_), channel_id=1, source_target_pairs={{0,1},{1,0},{2,3},{3,2},{4,5},{5,4},{6,7},{7,6},{8,9},{9,8},{10,11... | collective-permute-start | bytes 589832 | tf_op jit(solution)/shard_map/ppermute | solution.py:348
  12.3 8.2 %collective-permute-start.6 = (bf16[256,384]{1,0:T(8,128)(2,1)S(1)}, bf16[256,384]{1,0:T(8,128)(2,1)S(1)}, u32[]{:S(2)}, u32[]{:S(2)}) collective-permute-start(bf16[256,384]{1,0:T(8,128)(2,1)S(1)} %collective-permute-done.4.refs_2_), channel_id=1, source_target_pairs={{4,12},{12,8},{8,0},{0,4},{5,13},{13,9},{9,1},{1,5},{6,14},{14,10}... | collective-permute-start | bytes 589832 | tf_op jit(solution)/shard_map/ppermute | solution.py:345
  13.4 8.7 %collective-permute-start.5 = (bf16[256,384]{1,0:T(8,128)(2,1)S(1)}, bf16[256,384]{1,0:T(8,128)(2,1)S(1)}, u32[]{:S(2)}, u32[]{:S(2)}) collective-permute-start(bf16[256,384]{1,0:T(8,128)(2,1)S(1)} %collective-permute-done.4.refs_2_), channel_id=1, source_target_pairs={{0,1},{1,0},{2,3},{3,2},{4,5},{5,4},{6,7},{7,6},{8,9},{9,8},{10,11... | collective-permute-start | bytes 589832 | tf_op jit(solution)/shard_map/ppermute | solution.py:348
  16.5 7.1 %collective-permute-start.12 = (bf16[256,384]{1,0:T(8,128)(2,1)S(1)}, bf16[256,384]{1,0:T(8,128)(2,1)S(1)}, u32[]{:S(2)}, u32[]{:S(2)}) collective-permute-start(bf16[256,384]{1,0:T(8,128)(2,1)S(1)} %collective-permute-done.11.refs_2_), channel_id=1, source_target_pairs={{0,1},{1,0},{2,3},{3,2},{4,5},{5,4},{6,7},{7,6},{8,9},{9,8},{10,11... | collective-permute-start | bytes 589832 | tf_op jit(solution)/shard_map/ppermute | solution.py:348
  16.5 8.2 %collective-permute-start.13 = (bf16[256,384]{1,0:T(8,128)(2,1)S(1)}, bf16[256,384]{1,0:T(8,128)(2,1)S(1)}, u32[]{:S(2)}, u32[]{:S(2)}) collective-permute-start(bf16[256,384]{1,0:T(8,128)(2,1)S(1)} %collective-permute-done.11.refs_2_), channel_id=1, source_target_pairs={{4,12},{12,8},{8,0},{0,4},{5,13},{13,9},{9,1},{1,5},{6,14},{14,10}... | collective-permute-start | bytes 589832 | tf_op jit(solution)/shard_map/ppermute | solution.py:345
  20.5 7.2 %collective-permute-start.7 = (bf16[256,384]{1,0:T(8,128)(2,1)S(1)}, bf16[256,384]{1,0:T(8,128)(2,1)S(1)}, u32[]{:S(2)}, u32[]{:S(2)}) collective-permute-start(bf16[256,384]{1,0:T(8,128)(2,1)S(1)} %collective-permute-done.6.refs_4_), channel_id=1, source_target_pairs={{0,1},{1,0},{2,3},{3,2},{4,5},{5,4},{6,7},{7,6},{8,9},{9,8},{10,11... | collective-permute-start | bytes 589832 | tf_op jit(solution)/shard_map/ppermute | solution.py:348
  20.5 19.2 %collective-permute-start.1 = (bf16[1536,128]{1,0:T(8,128)(2,1)S(1)}, bf16[1536,128]{1,0:T(8,128)(2,1)S(1)}, u32[]{:S(2)}, u32[]{:S(2)}) collective-permute-start(bf16[1536,128]{1,0:T(8,128)(2,1)S(1)} %get-tuple-element.29), channel_id=1, source_target_pairs={{0,2},{2,0},{1,3},{3,1},{4,6},{6,4},{5,7},{7,5},{8,10},{10,8},{9,1... | collective-permute-start | bytes 1179656 | tf_op jit(solution)/shard_map/ppermute | solution.py:360
  22.1 17.7 %collective-permute-start.2 = (bf16[1536,128]{1,0:T(8,128)(2,1)S(1)}, bf16[1536,128]{1,0:T(8,128)(2,1)S(1)}, u32[]{:S(2)}, u32[]{:S(2)}) collective-permute-start(bf16[1536,128]{1,0:T(8,128)(2,1)S(1)} %collective-permute-done.refs_1_), channel_id=1, source_target_pairs={{0,16},{16,0},{1,17},{17,1},{2,18},{18,2},{3,19},{19,3},{4,20},{20... | collective-permute-start | bytes 1179656 | tf_op jit(solution)/shard_map/ppermute | solution.py:361
  23.6 8.7 %collective-permute-start.8 = (bf16[256,384]{1,0:T(8,128)(2,1)S(1)}, bf16[256,384]{1,0:T(8,128)(2,1)S(1)}, u32[]{:S(2)}, u32[]{:S(2)}) collective-permute-start(bf16[256,384]{1,0:T(8,128)(2,1)S(1)} %collective-permute-done.6.refs_4_), channel_id=1, source_target_pairs={{4,12},{12,8},{8,0},{0,4},{5,13},{13,9},{9,1},{1,5},{6,14},{14,10}... | collective-permute-start | bytes 589832 | tf_op jit(solution)/shard_map/ppermute | solution.py:345
  24.7 10.7 %collective-permute-start.15 = (bf16[256,384]{1,0:T(8,128)(2,1)S(1)}, bf16[256,384]{1,0:T(8,128)(2,1)S(1)}, u32[]{:S(2)}, u32[]{:S(2)}) collective-permute-start(bf16[256,384]{1,0:T(8,128)(2,1)S(1)} %collective-permute-done.13.refs_4_), channel_id=1, source_target_pairs={{4,12},{12,8},{8,0},{0,4},{5,13},{13,9},{9,1},{1,5},{6,14},{14,10}... | collective-permute-start | bytes 589832 | tf_op jit(solution)/shard_map/ppermute | solution.py:345
  27.8 10.7 %collective-permute-start.14 = (bf16[256,384]{1,0:T(8,128)(2,1)S(1)}, bf16[256,384]{1,0:T(8,128)(2,1)S(1)}, u32[]{:S(2)}, u32[]{:S(2)}) collective-permute-start(bf16[256,384]{1,0:T(8,128)(2,1)S(1)} %collective-permute-done.13.refs_4_), channel_id=1, source_target_pairs={{0,1},{1,0},{2,3},{3,2},{4,5},{5,4},{6,7},{7,6},{8,9},{9,8},{10,11... | collective-permute-start | bytes 589832 | tf_op jit(solution)/shard_map/ppermute | solution.py:348
  32.3 9.3 %collective-permute-start.9 = (bf16[256,384]{1,0:T(8,128)(2,1)S(1)}, bf16[256,384]{1,0:T(8,128)(2,1)S(1)}, u32[]{:S(2)}, u32[]{:S(2)}) collective-permute-start(bf16[256,384]{1,0:T(8,128)(2,1)S(1)} %collective-permute-done.8.refs_0_), channel_id=1, source_target_pairs={{0,1},{1,0},{2,3},{3,2},{4,5},{5,4},{6,7},{7,6},{8,9},{9,8},{10,11... | collective-permute-start | bytes 589832 | tf_op jit(solution)/shard_map/ppermute | solution.py:348
  35.4 11.6 %collective-permute-start.16 = (bf16[256,384]{1,0:T(8,128)(2,1)S(1)}, bf16[256,384]{1,0:T(8,128)(2,1)S(1)}, u32[]{:S(2)}, u32[]{:S(2)}) collective-permute-start(bf16[256,384]{1,0:T(8,128)(2,1)S(1)} %collective-permute-done.15.refs_0_), channel_id=1, source_target_pairs={{0,1},{1,0},{2,3},{3,2},{4,5},{5,4},{6,7},{7,6},{8,9},{9,8},{10,11... | collective-permute-start | bytes 589832 | tf_op jit(solution)/shard_map/ppermute | solution.py:348
  36.1 1.6 %copy-start = (f32[50,3,3072]{2,0,1:T(8,128)S(1)}, f32[50,3,3072]{2,0,1:T(8,128)}, u32[]{:S(2)}) copy-start(f32[50,3,3072]{2,0,1:T(8,128)} %param.9) | copy-start | bytes 5529604
  38.4 19.0 %collective-permute-start.25 = (bf16[256,384]{1,0:T(8,128)(2,1)S(1)}, bf16[256,384]{1,0:T(8,128)(2,1)S(1)}, u32[]{:S(2)}, u32[]{:S(2)}) collective-permute-start(bf16[256,384]{1,0:T(8,128)(2,1)S(1)} %shard_map.74), channel_id=1, source_target_pairs={{0,0},{2,8},{4,4},{6,12},{8,2},{10,10},{12,6},{14,14},{16,20},{18,... | collective-permute-start | bytes 589832 | tf_op jit(solution)/shard_map/ppermute | solution.py:422
  42.8 11.3 %collective-permute-start.17 = (bf16[256,256]{1,0:T(8,128)(2,1)S(1)}, bf16[256,256]{1,0:T(8,128)(2,1)S(1)}, u32[]{:S(2)}, u32[]{:S(2)}) collective-permute-start(bf16[256,256]{1,0:T(8,128)(2,1)S(1)} %get-tuple-element.42.refs_2_), channel_id=1, source_target_pairs={{0,2},{2,0},{1,3},{3,1},{4,6},{6,4},{5,7},{7,5},{8,10},{10,8},{9,1... | collective-permute-start | bytes 393224 | tf_op jit(solution)/shard_map/ppermute | solution.py:463
  48.3 7.9 %collective-permute-start.18 = (bf16[256,256]{1,0:T(8,128)(2,1)S(1)}, bf16[256,256]{1,0:T(8,128)(2,1)S(1)}, u32[]{:S(2)}, u32[]{:S(2)}) collective-permute-start(bf16[256,256]{1,0:T(8,128)(2,1)S(1)} %get-tuple-element.43.refs_3_), channel_id=1, source_target_pairs={{0,2},{2,0},{1,3},{3,1},{4,6},{6,4},{5,7},{7,5},{8,10},{10,8},{9,1... | collective-permute-start | bytes 393224 | tf_op jit(solution)/shard_map/ppermute | solution.py:463
  57.1 6.0 %collective-permute-start.20 = (bf16[512,128]{1,0:T(8,128)(2,1)S(1)}, bf16[512,128]{1,0:T(8,128)(2,1)S(1)}, u32[]{:S(2)}, u32[]{:S(2)}) collective-permute-start(bf16[512,128]{1,0:T(8,128)(2,1)S(1)} %shard_map.72.refs_0_), channel_id=1, source_target_pairs={{4,12},{12,8},{8,0},{0,4},{5,13},{13,9},{9,1},{1,5},{6,14},{14,10}... | collective-permute-start | bytes 393224 | tf_op jit(solution)/shard_map/ppermute | solution.py:481
  57.5 10.1 %collective-permute-start.26 = (bf16[256,384]{1,0:T(8,128)(2,1)S(1)}, bf16[256,384]{1,0:T(8,128)(2,1)S(1)}, u32[]{:S(2)}, u32[]{:S(2)}) collective-permute-start(bf16[256,384]{1,0:T(8,128)(2,1)S(1)} %collective-permute-done.25.refs_6_), channel_id=1, source_target_pairs={{0,2},{2,0},{16,18},{18,16},{1,3},{3,1},{17,19},{19,17},{4,6},{6,4... | collective-permute-start | bytes 589832 | tf_op jit(solution)/shard_map/ppermute | solution.py:434
  59.8 7.8 %collective-permute-start.27 = (bf16[256,384]{1,0:T(8,128)(2,1)S(1)}, bf16[256,384]{1,0:T(8,128)(2,1)S(1)}, u32[]{:S(2)}, u32[]{:S(2)}) collective-permute-start(bf16[256,384]{1,0:T(8,128)(2,1)S(1)} %collective-permute-done.25.refs_6_), channel_id=1, source_target_pairs={{0,16},{2,18},{16,0},{18,2},{1,17},{3,19},{17,1},{19,3},{4,20},{6,... | collective-permute-start | bytes 589832 | tf_op jit(solution)/shard_map/ppermute | solution.py:434
  60.1 8.0 %collective-permute-start.22 = (bf16[512,128]{1,0:T(8,128)(2,1)S(1)}, bf16[512,128]{1,0:T(8,128)(2,1)S(1)}, u32[]{:S(2)}, u32[]{:S(2)}) collective-permute-start(bf16[512,128]{1,0:T(8,128)(2,1)S(1)} %shard_map.72.refs_0_), channel_id=1, source_target_pairs={{4,0},{12,4},{8,12},{0,8},{5,1},{13,5},{9,13},{1,9},{6,2},{14,6},{... | collective-permute-start | bytes 393224 | tf_op jit(solution)/shard_map/ppermute | solution.py:483
  63.1 7.4 %collective-permute-start.29 = (bf16[512,128]{1,0:T(8,128)(2,1)S(1)}, bf16[512,128]{1,0:T(8,128)(2,1)S(1)}, u32[]{:S(2)}, u32[]{:S(2)}) collective-permute-start(bf16[512,128]{1,0:T(8,128)(2,1)S(1)} %collective-permute-done.20.refs_2_), channel_id=1, source_target_pairs={{4,12},{12,8},{8,0},{0,4},{5,13},{13,9},{9,1},{1,5},{6,14},{14,10}... | collective-permute-start | bytes 393224 | tf_op jit(solution)/shard_map/ppermute | solution.py:481
  67.6 6.6 %collective-permute-start.28 = (bf16[256,384]{1,0:T(8,128)(2,1)S(1)}, bf16[256,384]{1,0:T(8,128)(2,1)S(1)}, u32[]{:S(2)}, u32[]{:S(2)}) collective-permute-start(bf16[256,384]{1,0:T(8,128)(2,1)S(1)} %collective-permute-done.25.refs_6_), channel_id=1, source_target_pairs={{0,18},{2,16},{16,2},{18,0},{1,19},{3,17},{17,3},{19,1},{4,22},{6,... | collective-permute-start | bytes 589832 | tf_op jit(solution)/shard_map/ppermute | solution.py:434
  67.6 6.6 %collective-permute-start.19 = (bf16[512,128]{1,0:T(8,128)(2,1)S(1)}, bf16[512,128]{1,0:T(8,128)(2,1)S(1)}, u32[]{:S(2)}, u32[]{:S(2)}) collective-permute-start(bf16[512,128]{1,0:T(8,128)(2,1)S(1)} %shard_map.72.refs_0_), channel_id=1, source_target_pairs={{0,1},{1,0},{2,3},{3,2},{4,5},{5,4},{6,7},{7,6},{8,9},{9,8},{10,11... | collective-permute-start | bytes 393224 | tf_op jit(solution)/shard_map/ppermute | solution.py:486
  67.6 6.5 %collective-permute-start.21 = (bf16[512,128]{1,0:T(8,128)(2,1)S(1)}, bf16[512,128]{1,0:T(8,128)(2,1)S(1)}, u32[]{:S(2)}, u32[]{:S(2)}) collective-permute-start(bf16[512,128]{1,0:T(8,128)(2,1)S(1)} %collective-permute-done.20.refs_2_), channel_id=1, source_target_pairs={{0,1},{1,0},{2,3},{3,2},{4,5},{5,4},{6,7},{7,6},{8,9},{9,8},{10,11... | collective-permute-start | bytes 393224 | tf_op jit(solution)/shard_map/ppermute | solution.py:486
  68.1 6.1 %collective-permute-start.23 = (bf16[512,128]{1,0:T(8,128)(2,1)S(1)}, bf16[512,128]{1,0:T(8,128)(2,1)S(1)}, u32[]{:S(2)}, u32[]{:S(2)}) collective-permute-start(bf16[512,128]{1,0:T(8,128)(2,1)S(1)} %collective-permute-done.22.refs_4_), channel_id=1, source_target_pairs={{0,1},{1,0},{2,3},{3,2},{4,5},{5,4},{6,7},{7,6},{8,9},{9,8},{10,11... | collective-permute-start | bytes 393224 | tf_op jit(solution)/shard_map/ppermute | solution.py:486
  70.5 4.3 %collective-permute-start.30 = (bf16[512,128]{1,0:T(8,128)(2,1)S(1)}, bf16[512,128]{1,0:T(8,128)(2,1)S(1)}, u32[]{:S(2)}, u32[]{:S(2)}) collective-permute-start(bf16[512,128]{1,0:T(8,128)(2,1)S(1)} %collective-permute-done.29.refs_0_), channel_id=1, source_target_pairs={{0,1},{1,0},{2,3},{3,2},{4,5},{5,4},{6,7},{7,6},{8,9},{9,8},{10,11... | collective-permute-start | bytes 393224 | tf_op jit(solution)/shard_map/ppermute | solution.py:486

commit v3 on v2

--- a/solution.py
+++ b/solution.py
@@ -289,13 +289,15 @@
         buf[source()] = w_ref[...]
     seq_at = lax.axis_index("seq")
     acc = None
+    head = att_refs[0].shape[1]
     for i in range(0, len(slots), n_tp):
+        count = len(slots[i : i + n_tp])
         values = jnp.concatenate([r[...] for r in att_refs[i : i + n_tp]], axis=1)
-        weight = buf[ring_source(sizes[1], seq_at, slots[i][0])]
+        weight = buf[ring_source(sizes[1], seq_at, slots[i][0])][: count * head]
         part = jnp.dot(values, weight, preferred_element_type=f32)
         acc = part if acc is None else acc + part
     acc_ref[...] = acc
-    rest_ref[...] = buf[ring_source(sizes[1], seq_at, last_step)]
+    rest_ref[...] = buf[ring_source(sizes[1], seq_at, last_step)][head:]
 
 
 def output_body(sizes, table_ref, acc_ref, w_ref, *refs):
@@ -384,7 +386,9 @@
         def source():
             low = lax.rem(lax.axis_index("seq"), n_low)
             s = back(lax.axis_index("group"), -shift, n_grp) if shared else shift
-            return back(lax.axis_index("blk"), k3, n_blk) * n_low + lax.rem(low - s + n_low, n_low)
+            low = lax.rem(low - s + n_low, n_low)
+            high = lax.rem(lax.axis_index("blk") - k3 - low + (n_low + 1) * n_blk, n_blk)
+            return high * n_low + low
 
         return source
 
@@ -417,7 +421,8 @@
                 for z in range(n_seq):
                     for b in range(n_blk):
                         l2 = (z % n_low + (g if shared else k1)) % n_low
-                        target = (g * n_seq + b * n_low + l2) * n_blk + (z // n_low + k3) % n_blk
+                        x2 = (z // n_low + z % n_low + k3) % n_blk
+                        target = (g * n_seq + b * n_low + l2) * n_blk + x2
                         pairs.append(((g * n_seq + z) * n_blk + b, target))
             arrived = lax.ppermute(rows, ("group", "seq", "blk"), pairs)
             o_parts.append(arrived)
@@ -485,20 +490,21 @@
         for u in range(1, n_tp):
             att[step, u] = lax.ppermute(att[step, 0], "tp", rotation(n_tp, u))
     first_slots = [(s, u) for s in range(n_seq) if s != last_step for u in range(n_tp)]
+    first_slots.append((last_step, 0))
     acc, rest = kernel(
         functools.partial(output_early_body, sizes, first_slots, last_step, o_sources),
-        [((2 * half, own_width), f32), ((n_tp * head, own_width), bf16)],
+        [((2 * half, own_width), f32), (((n_tp - 1) * head, own_width), bf16)],
         [(att[slot], "near") for slot in first_slots] + [(x, "near") for x in o_parts],
         [pltpu.VMEM((n_seq, n_tp * head, own_width), bf16)],
     )
     return pl.pallas_call(
         functools.partial(output_body, sizes),
         out_shape=jax.ShapeDtypeStruct((2 * half, own_width), bf16),
-        in_specs=[VMEM] * (3 + n_tp),
+        in_specs=[VMEM] * (2 + n_tp),
         out_specs=VMEM,
         compiler_params=PARAMS,
         name="output",
-    )(near(table), near(acc), near(rest), *[near(att[last_step, u]) for u in range(n_tp)])
+    )(near(table), near(acc), near(rest), *[near(att[last_step, u]) for u in range(1, n_tp)])
 
 
 def solution(mesh):

time: 76.5 us -> 73.9 us (0.966)
  waiting for transfers between devices: 29 us -> 25.6 us
  starting transfers between devices: 32.5 us -> 33.6 us
    ppermute x3, starting transfers between devices: 2.61 us -> 8.09 us  [block(): o_parts.append(lax.ppermute(arrived, ('group', 'blk'), swap))]
    ppermute x2, starting transfers between devices: 4.76 us -> 0.06 us  [block(): up = att[step, 0] = lax.ppermute(up, 'seq', forward)]
    ppermute x3, waiting for transfers between devices: 3.62 us -> 1.9 us  [block(): o_parts.append(lax.ppermute(arrived, ('group', 'blk'), swap))]
    ppermute x2, waiting for transfers between devices: 2.85 us -> 1.16 us  [block(): up = att[step, 0] = lax.ppermute(up, 'seq', forward)]
  transfers between devices with their start and end apart: 31 -> 31, of which waited for: 10 -> 9; matrix products, arithmetic and copies ran while one was open for 0% -> 0% of each run, Pallas kernels for 12% -> 13%
where the time goes in v3:
time: 73.9 us; the launch traced here: 73.7 us
  starting transfers between devices  33.6 us (45%)
  waiting for transfers between devices  25.6 us (35%)
  Pallas kernels  11.5 us (16%)
  local copies, waits for them, and re-layouts  1.57 us (2%)
  between operations  1.46 us (2%)
    ppermute x6, waiting for transfers between devices, block(): current[chunk] = lax.ppermute(current[chunk], 'seq', forward)  16.1 us
    ppermute x6, starting transfers between devices, block(): current[chunk] = lax.ppermute(current[chunk], 'seq', forward)  11.6 us
    pallas_call x12, Pallas kernels, kernel(): pl.pallas_call(body, out_shape=tuple((pltpu.VMEM(shape, dtype) for shape,...  10.5 us
    ppermute x3, starting transfers between devices, block(): o_parts.append(lax.ppermute(arrived, ('group', 'blk'), swap))  8.09 us
    ppermute x2, waiting for transfers between devices, block(): kv_rest.append(lax.ppermute(kv, 'blk', rotation(n_blk, j)))  6.33 us
    ppermute x2, starting transfers between devices, block(): kv_rest.append(lax.ppermute(kv, 'blk', rotation(n_blk, j)))  4.39 us
    ppermute x1, starting transfers between devices, block(): down = att[n_seq - step, 0] = lax.ppermute(down, 'seq', backward)  2.84 us
    ppermute x3, waiting for transfers between devices, block(): o_parts.append(lax.ppermute(arrived, ('group', 'blk'), swap))  1.9 us
  transfers between devices with their start and end apart: 31, of which 9 were waited for; matrix products, arithmetic and copies ran while one was open for 0% of the time, Pallas kernels for 13%

profile of v3, /device:TPU:0, one launch (start us, length us, event | category | flops | bytes accessed | tf_op | source)
XLA Modules:
  0.0 73.7 jit_solution(14874859891222625837)
XLA Ops:
  0.0 1.0 %shard_map.73 = (bf16[128,384]{1,0:T(8,128)(2,1)S(1)}, bf16[128,384]{1,0:T(8,128)(2,1)S(1)}) custom-call(bf16[128,1536]{1,0:T(8,128)(2,1)} %w_ref.3), custom_call_target="tpu_custom_call" | custom-call | tf_op jit(solution)/shard_map/pallas_call | solution.py:56
  1.0 0.6 collective-permute-start.25
  1.5 1.3 %shard_map.65 = (bf16[256,384]{1,0:T(8,128)(2,1)S(1)}, bf16[256,384]{1,0:T(8,128)(2,1)S(1)}, bf16[1536,128]{1,0:T(8,128)(2,1)S(1)}, bf16[1536,128]{1,0:T(8,128)(2,1)S(1)}) custom-call(bf16[512,384]{1,0:T(8,128)(2,1)} %x_ref.1, bf16[3,1536,128]{2,1,0:T(8,128)(2,1)} %refs_0_.1), custom_call_target="tpu_custom_call" | custom-call | tf_op jit(solution)/shard_map/pallas_call | solution.py:56
  2.9 2.6 %collective-permute-start.4 = (bf16[256,384]{1,0:T(8,128)(2,1)S(1)}, bf16[256,384]{1,0:T(8,128)(2,1)S(1)}, u32[]{:S(2)}, u32[]{:S(2)}) collective-permute-start(bf16[256,384]{1,0:T(8,128)(2,1)S(1)} %get-tuple-element.32.refs_0_), channel_id=1, source_target_pairs={{4,12},{12,8},{8,0},{0,4},{5,13},{13,9},{9,1},{1,5},{6,14},{14,10}... | collective-permute-start | bytes 589832 | tf_op jit(solution)/shard_map/ppermute | solution.py:347
  5.5 1.5 %collective-permute-start = (bf16[1536,128]{1,0:T(8,128)(2,1)S(1)}, bf16[1536,128]{1,0:T(8,128)(2,1)S(1)}, u32[]{:S(2)}, u32[]{:S(2)}) collective-permute-start(bf16[1536,128]{1,0:T(8,128)(2,1)S(1)} %get-tuple-element.28), channel_id=1, source_target_pairs={{0,2},{2,0},{1,3},{3,1},{4,6},{6,4},{5,7},{7,5},{8,10},{10,8},{9,1... | collective-permute-start | bytes 1179656 | tf_op jit(solution)/shard_map/ppermute | solution.py:361
  7.0 2.6 %collective-permute-start.11 = (bf16[256,384]{1,0:T(8,128)(2,1)S(1)}, bf16[256,384]{1,0:T(8,128)(2,1)S(1)}, u32[]{:S(2)}, u32[]{:S(2)}) collective-permute-start(bf16[256,384]{1,0:T(8,128)(2,1)S(1)} %get-tuple-element.37.refs_0_), channel_id=1, source_target_pairs={{4,12},{12,8},{8,0},{0,4},{5,13},{13,9},{9,1},{1,5},{6,14},{14,10}... | collective-permute-start | bytes 589832 | tf_op jit(solution)/shard_map/ppermute | solution.py:347
  9.6 0.0 collective-permute-done.25.refs_1_
  9.6 0.2 collective-permute-start.10
  9.8 2.4 %collective-permute-done.4.refs_2_ = bf16[256,384]{1,0:T(8,128)(2,1)S(1)} collective-permute-done((bf16[256,384]{1,0:T(8,128)(2,1)S(1)}, bf16[256,384]{1,0:T(8,128)(2,1)S(1)}, u32[]{:S(2)}, u32[]{:S(2)}) %collective-permute-start.4) | collective-permute-done | bytes 196640 | tf_op jit(solution)/shard_map/ppermute | solution.py:347
  12.3 1.1 %collective-permute-start.6 = (bf16[256,384]{1,0:T(8,128)(2,1)S(1)}, bf16[256,384]{1,0:T(8,128)(2,1)S(1)}, u32[]{:S(2)}, u32[]{:S(2)}) collective-permute-start(bf16[256,384]{1,0:T(8,128)(2,1)S(1)} %collective-permute-done.4.refs_2_), channel_id=1, source_target_pairs={{4,12},{12,8},{8,0},{0,4},{5,13},{13,9},{9,1},{1,5},{6,14},{14,10}... | collective-permute-start | bytes 589832 | tf_op jit(solution)/shard_map/ppermute | solution.py:347
  13.4 0.0 collective-permute-done.3.refs_1_
  13.4 0.0 collective-permute-start.5
  13.4 3.1 %collective-permute-done.11.refs_2_ = bf16[256,384]{1,0:T(8,128)(2,1)S(1)} collective-permute-done((bf16[256,384]{1,0:T(8,128)(2,1)S(1)}, bf16[256,384]{1,0:T(8,128)(2,1)S(1)}, u32[]{:S(2)}, u32[]{:S(2)}) %collective-permute-start.11) | collective-permute-done | bytes 196640 | tf_op jit(solution)/shard_map/ppermute | solution.py:347
  16.5 1.1 %collective-permute-start.13 = (bf16[256,384]{1,0:T(8,128)(2,1)S(1)}, bf16[256,384]{1,0:T(8,128)(2,1)S(1)}, u32[]{:S(2)}, u32[]{:S(2)}) collective-permute-start(bf16[256,384]{1,0:T(8,128)(2,1)S(1)} %collective-permute-done.11.refs_2_), channel_id=1, source_target_pairs={{4,12},{12,8},{8,0},{0,4},{5,13},{13,9},{9,1},{1,5},{6,14},{14,10}... | collective-permute-start | bytes 589832 | tf_op jit(solution)/shard_map/ppermute | solution.py:347
  17.6 2.9 %collective-permute-done.6.refs_4_ = bf16[256,384]{1,0:T(8,128)(2,1)S(1)} collective-permute-done((bf16[256,384]{1,0:T(8,128)(2,1)S(1)}, bf16[256,384]{1,0:T(8,128)(2,1)S(1)}, u32[]{:S(2)}, u32[]{:S(2)}) %collective-permute-start.6) | collective-permute-done | bytes 196640 | tf_op jit(solution)/shard_map/ppermute | solution.py:347
  20.5 1.5 %collective-permute-start.1 = (bf16[1536,128]{1,0:T(8,128)(2,1)S(1)}, bf16[1536,128]{1,0:T(8,128)(2,1)S(1)}, u32[]{:S(2)}, u32[]{:S(2)}) collective-permute-start(bf16[1536,128]{1,0:T(8,128)(2,1)S(1)} %get-tuple-element.29), channel_id=1, source_target_pairs={{0,2},{2,0},{1,3},{3,1},{4,6},{6,4},{5,7},{7,5},{8,10},{10,8},{9,1... | collective-permute-start | bytes 1179656 | tf_op jit(solution)/shard_map/ppermute | solution.py:362
  22.1 0.0 collective-permute-done.5.refs_3_
  22.1 1.5 %collective-permute-start.2 = (bf16[1536,128]{1,0:T(8,128)(2,1)S(1)}, bf16[1536,128]{1,0:T(8,128)(2,1)S(1)}, u32[]{:S(2)}, u32[]{:S(2)}) collective-permute-start(bf16[1536,128]{1,0:T(8,128)(2,1)S(1)} %collective-permute-done.refs_1_), channel_id=1, source_target_pairs={{0,16},{16,0},{1,17},{17,1},{2,18},{18,2},{3,19},{19,3},{4,20},{20... | collective-permute-start | bytes 1179656 | tf_op jit(solution)/shard_map/ppermute | solution.py:363
  23.6 0.0 collective-permute-done.12.refs_3_
  23.6 1.2 %collective-permute-start.8 = (bf16[256,384]{1,0:T(8,128)(2,1)S(1)}, bf16[256,384]{1,0:T(8,128)(2,1)S(1)}, u32[]{:S(2)}, u32[]{:S(2)}) collective-permute-start(bf16[256,384]{1,0:T(8,128)(2,1)S(1)} %collective-permute-done.6.refs_4_), channel_id=1, source_target_pairs={{4,12},{12,8},{8,0},{0,4},{5,13},{13,9},{9,1},{1,5},{6,14},{14,10}... | collective-permute-start | bytes 589832 | tf_op jit(solution)/shard_map/ppermute | solution.py:347
  24.7 3.0 %collective-permute-start.15 = (bf16[256,384]{1,0:T(8,128)(2,1)S(1)}, bf16[256,384]{1,0:T(8,128)(2,1)S(1)}, u32[]{:S(2)}, u32[]{:S(2)}) collective-permute-start(bf16[256,384]{1,0:T(8,128)(2,1)S(1)} %collective-permute-done.13.refs_4_), channel_id=1, source_target_pairs={{4,12},{12,8},{8,0},{0,4},{5,13},{13,9},{9,1},{1,5},{6,14},{14,10}... | collective-permute-start | bytes 589832 | tf_op jit(solution)/shard_map/ppermute | solution.py:347
  27.8 4.5 %collective-permute-done.8.refs_0_ = bf16[256,384]{1,0:T(8,128)(2,1)S(1)} collective-permute-done((bf16[256,384]{1,0:T(8,128)(2,1)S(1)}, bf16[256,384]{1,0:T(8,128)(2,1)S(1)}, u32[]{:S(2)}, u32[]{:S(2)}) %collective-permute-start.8) | collective-permute-done | bytes 196640 | tf_op jit(solution)/shard_map/ppermute | solution.py:347
  32.3 3.2 %collective-permute-done.15.refs_0_ = bf16[256,384]{1,0:T(8,128)(2,1)S(1)} collective-permute-done((bf16[256,384]{1,0:T(8,128)(2,1)S(1)}, bf16[256,384]{1,0:T(8,128)(2,1)S(1)}, u32[]{:S(2)}, u32[]{:S(2)}) %collective-permute-start.15) | collective-permute-done | bytes 196640 | tf_op jit(solution)/shard_map/ppermute | solution.py:347
  36.1 0.0 copy-start
  36.1 1.6 %copy-done = f32[50,3,3072]{2,0,1:T(8,128)S(1)} copy-done((f32[50,3,3072]{2,0,1:T(8,128)S(1)}, f32[50,3,3072]{2,0,1:T(8,128)}, u32[]{:S(2)}) %copy-start) | copy-done | bytes 1843224
  37.7 0.7 shard_map.67
  38.4 0.7 collective-permute-start.26
  39.1 0.7 shard_map.69
  39.8 1.8 %shard_map.66 = (bf16[3072,384]{1,0:T(8,128)(2,1)S(1)}, f32[8,384]{1,0:T(8,128)S(1)}) custom-call(f32[3,8,384]{2,1,0:T(8,128)S(1)} %shard_map.64.table_ref, bf16[3,1536,128]{2,1,0:T(8,128)(2,1)} %refs_0_.1, bf16[1536,128]{1,0:T(8,128)(2,1)S(1)} %collective-permute-done.refs_1_, bf16[1536,128]{1,0:T(8,128)(2,1)S(1)} %collective-permute-done.1.refs_2_, ...), custom_call_target="tpu_custom_call" | custom-call | tf_op jit(solution)/shard_map/pallas_call | solution.py:56
  41.6 1.2 %shard_map.68 = (bf16[256,128]{1,0:T(8,128)(2,1)S(1)}, bf16[256,256]{1,0:T(8,128)(2,1)S(1)}) custom-call(f32[3,8,384]{2,1,0:T(8,128)S(1)} %shard_map.64.table_ref, bf16[3072,384]{1,0:T(8,128)(2,1)S(1)} %get-tuple-element.30.w_ref, f32[8,384]{1,0:T(8,128)S(1)} %get-tuple-element.31.vec_ref, bf16[6,256,384]{2,1,0:T(8,128)(2,1)S(1)} %get-tuple-element.33.y_ref, ...), custom_call_target="tpu_custom_call" | custom-call | tf_op jit(solution)/shard_map/pallas_call | solution.py:56
  42.8 4.3 %collective-permute-start.17 = (bf16[256,256]{1,0:T(8,128)(2,1)S(1)}, bf16[256,256]{1,0:T(8,128)(2,1)S(1)}, u32[]{:S(2)}, u32[]{:S(2)}) collective-permute-start(bf16[256,256]{1,0:T(8,128)(2,1)S(1)} %get-tuple-element.42.refs_2_), channel_id=1, source_target_pairs={{0,2},{2,0},{1,3},{3,1},{4,6},{6,4},{5,7},{7,5},{8,10},{10,8},{9,1... | collective-permute-start | bytes 393224 | tf_op jit(solution)/shard_map/ppermute | solution.py:468
  47.1 1.2 %shard_map.70 = (bf16[256,128]{1,0:T(8,128)(2,1)S(1)}, bf16[256,256]{1,0:T(8,128)(2,1)S(1)}) custom-call(f32[3,8,384]{2,1,0:T(8,128)S(1)} %shard_map.64.table_ref, bf16[3072,384]{1,0:T(8,128)(2,1)S(1)} %get-tuple-element.30.w_ref, f32[8,384]{1,0:T(8,128)S(1)} %get-tuple-element.31.vec_ref, bf16[6,256,384]{2,1,0:T(8,128)(2,1)S(1)} %get-tuple-element.38.y_ref, ...), custom_call_target="tpu_custom_call" | custom-call | tf_op jit(solution)/shard_map/pallas_call | solution.py:56
  48.3 0.1 collective-permute-start.18
  49.0 0.8 %shard_map.71 = (f32[512,128]{1,0:T(8,128)S(1)}, f32[512,128]{1,0:T(8,128)S(1)}, f32[512,128]{1,0:T(8,128)S(1)}) custom-call(s32[1]{0:T(128)S(6)} %copy.8.padded, bf16[256,128]{1,0:T(8,128)(2,1)S(1)} %get-tuple-element.36.refs_0_, bf16[256,128]{1,0:T(8,128)(2,1)S(1)} %get-tuple-element.41.refs_1_, bf16[256,256]{1,0:T(8,128)(2,1)S(1)} %get-tuple-element.42.refs_2_, ...), custom_call_target="tpu_custom_call" | custom-call | tf_op jit(solution)/shard_map/pallas_call | solution.py:56
  49.8 4.3 %collective-permute-done.17.refs_2_ = bf16[256,256]{1,0:T(8,128)(2,1)S(1)} collective-permute-done((bf16[256,256]{1,0:T(8,128)(2,1)S(1)}, bf16[256,256]{1,0:T(8,128)(2,1)S(1)}, u32[]{:S(2)}, u32[]{:S(2)}) %collective-permute-start.17) | collective-permute-done | bytes 131104 | tf_op jit(solution)/shard_map/ppermute | solution.py:468
  54.1 2.1 %collective-permute-done.18.refs_3_ = bf16[256,256]{1,0:T(8,128)(2,1)S(1)} collective-permute-done((bf16[256,256]{1,0:T(8,128)(2,1)S(1)}, bf16[256,256]{1,0:T(8,128)(2,1)S(1)}, u32[]{:S(2)}, u32[]{:S(2)}) %collective-permute-start.18) | collective-permute-done | bytes 131104 | tf_op jit(solution)/shard_map/ppermute | solution.py:468
  56.2 1.0 %shard_map.72.refs_0_ = bf16[512,128]{1,0:T(8,128)(2,1)S(1)} custom-call(s32[1]{0:T(128)S(6)} %copy.8.padded, bf16[256,128]{1,0:T(8,128)(2,1)S(1)} %get-tuple-element.36.refs_0_, bf16[256,128]{1,0:T(8,128)(2,1)S(1)} %get-tuple-element.41.refs_1_, bf16[256,256]{1,0:T(8,128)(2,1)S(1)} %collective-permute-done.17.refs_2_, ...), custom_call_target="tpu_custom_call" | custom-call | tf_op jit(solution)/shard_map/pallas_call | solution.py:56
  57.1 0.1 collective-permute-start.20
  57.2 2.5 %collective-permute-start.27 = (bf16[256,384]{1,0:T(8,128)(2,1)S(1)}, bf16[256,384]{1,0:T(8,128)(2,1)S(1)}, u32[]{:S(2)}, u32[]{:S(2)}) collective-permute-start(bf16[256,384]{1,0:T(8,128)(2,1)S(1)} %collective-permute-done.26.refs_7_), channel_id=1, source_target_pairs={{0,2},{2,0},{16,18},{18,16},{1,3},{3,1},{17,19},{19,17},{4,6},{6,4... | collective-permute-start | bytes 589832 | tf_op jit(solution)/shard_map/ppermute | solution.py:439
  59.8 0.7 collective-permute-start.28
  60.5 2.8 %collective-permute-start.22 = (bf16[512,128]{1,0:T(8,128)(2,1)S(1)}, bf16[512,128]{1,0:T(8,128)(2,1)S(1)}, u32[]{:S(2)}, u32[]{:S(2)}) collective-permute-start(bf16[512,128]{1,0:T(8,128)(2,1)S(1)} %shard_map.72.refs_0_), channel_id=1, source_target_pairs={{4,0},{12,4},{8,12},{0,8},{5,1},{13,5},{9,13},{1,9},{6,2},{14,6},{... | collective-permute-start | bytes 393224 | tf_op jit(solution)/shard_map/ppermute | solution.py:488
  63.3 4.8 %collective-permute-start.29 = (bf16[256,384]{1,0:T(8,128)(2,1)S(1)}, bf16[256,384]{1,0:T(8,128)(2,1)S(1)}, u32[]{:S(2)}, u32[]{:S(2)}) collective-permute-start(bf16[256,384]{1,0:T(8,128)(2,1)S(1)} %collective-permute-done.26.refs_7_), channel_id=1, source_target_pairs={{0,18},{2,16},{16,2},{18,0},{1,19},{3,17},{17,3},{19,1},{4,22},{6,... | collective-permute-start | bytes 589832 | tf_op jit(solution)/shard_map/ppermute | solution.py:439
  68.2 0.5 collective-permute-start.21
  68.7 0.1 collective-permute-start.23
  68.7 1.2 %collective-permute-done.24.refs_6_ = bf16[512,128]{1,0:T(8,128)(2,1)S(1)} collective-permute-done((bf16[512,128]{1,0:T(8,128)(2,1)S(1)}, bf16[512,128]{1,0:T(8,128)(2,1)S(1)}, u32[]{:S(2)}, u32[]{:S(2)}) %collective-permute-start.24) | collective-permute-done | bytes 131104 | tf_op jit(solution)/shard_map/ppermute | solution.py:486
  69.9 1.9 %collective-permute-done.29.refs_10_ = bf16[256,384]{1,0:T(8,128)(2,1)S(1)} collective-permute-done((bf16[256,384]{1,0:T(8,128)(2,1)S(1)}, bf16[256,384]{1,0:T(8,128)(2,1)S(1)}, u32[]{:S(2)}, u32[]{:S(2)}) %collective-permute-start.29) | collective-permute-done | bytes 196640 | tf_op jit(solution)/shard_map/ppermute | solution.py:439
  71.8 0.8 %shard_map.75 = (f32[512,384]{1,0:T(8,128)S(1)}, bf16[128,384]{1,0:T(8,128)(2,1)S(1)}) custom-call(bf16[512,128]{1,0:T(8,128)(2,1)S(1)} %shard_map.72.refs_0_, bf16[512,128]{1,0:T(8,128)(2,1)S(1)} %collective-permute-done.19.refs_1_, bf16[512,128]{1,0:T(8,128)(2,1)S(1)} %collective-permute-done.20.refs_2_, ...), custom_call_target="tpu_custom_call" | custom-call | tf_op jit(solution)/shard_map/pallas_call | solution.py:56
  72.7 1.0 %output.1 = bf16[512,384]{1,0:T(8,128)(2,1)} custom-call(f32[3,8,384]{2,1,0:T(8,128)S(1)} %shard_map.64.table_ref, f32[512,384]{1,0:T(8,128)S(1)} %get-tuple-element.49.acc_ref, bf16[128,384]{1,0:T(8,128)(2,1)S(1)} %get-tuple-element.50.w_ref, bf16[512,128]{1,0:T(8,128)(2,1)S(1)} %collective-permute-done.30.refs_0_), custom_call_target="tpu_custom_call" | custom-call | tf_op jit(solution)/shard_map/output/pallas_call | solution.py:500
  (29 shorter events, 0.1 us)
Async XLA Ops:
  1.0 8.6 %collective-permute-start.25 = (bf16[128,384]{1,0:T(8,128)(2,1)S(1)}, bf16[128,384]{1,0:T(8,128)(2,1)S(1)}, u32[]{:S(2)}, u32[]{:S(2)}) collective-permute-start(bf16[128,384]{1,0:T(8,128)(2,1)S(1)} %get-tuple-element.48), channel_id=1, source_target_pairs={{0,1},{1,0},{2,3},{3,2},{4,5},{5,4},{6,7},{7,6},{8,9},{9,8},{10,11... | collective-permute-start | bytes 294920 | tf_op jit(solution)/shard_map/ppermute | solution.py:414
  2.9 9.4 %collective-permute-start.4 = (bf16[256,384]{1,0:T(8,128)(2,1)S(1)}, bf16[256,384]{1,0:T(8,128)(2,1)S(1)}, u32[]{:S(2)}, u32[]{:S(2)}) collective-permute-start(bf16[256,384]{1,0:T(8,128)(2,1)S(1)} %get-tuple-element.32.refs_0_), channel_id=1, source_target_pairs={{4,12},{12,8},{8,0},{0,4},{5,13},{13,9},{9,1},{1,5},{6,14},{14,10}... | collective-permute-start | bytes 589832 | tf_op jit(solution)/shard_map/ppermute | solution.py:347
  5.5 15.0 %collective-permute-start = (bf16[1536,128]{1,0:T(8,128)(2,1)S(1)}, bf16[1536,128]{1,0:T(8,128)(2,1)S(1)}, u32[]{:S(2)}, u32[]{:S(2)}) collective-permute-start(bf16[1536,128]{1,0:T(8,128)(2,1)S(1)} %get-tuple-element.28), channel_id=1, source_target_pairs={{0,2},{2,0},{1,3},{3,1},{4,6},{6,4},{5,7},{7,5},{8,10},{10,8},{9,1... | collective-permute-start | bytes 1179656 | tf_op jit(solution)/shard_map/ppermute | solution.py:361
  7.0 6.4 %collective-permute-start.3 = (bf16[256,384]{1,0:T(8,128)(2,1)S(1)}, bf16[256,384]{1,0:T(8,128)(2,1)S(1)}, u32[]{:S(2)}, u32[]{:S(2)}) collective-permute-start(bf16[256,384]{1,0:T(8,128)(2,1)S(1)} %get-tuple-element.32.refs_0_), channel_id=1, source_target_pairs={{0,1},{1,0},{2,3},{3,2},{4,5},{5,4},{6,7},{7,6},{8,9},{9,8},{10,11... | collective-permute-start | bytes 589832 | tf_op jit(solution)/shard_map/ppermute | solution.py:350
  7.0 9.5 %collective-permute-start.11 = (bf16[256,384]{1,0:T(8,128)(2,1)S(1)}, bf16[256,384]{1,0:T(8,128)(2,1)S(1)}, u32[]{:S(2)}, u32[]{:S(2)}) collective-permute-start(bf16[256,384]{1,0:T(8,128)(2,1)S(1)} %get-tuple-element.37.refs_0_), channel_id=1, source_target_pairs={{4,12},{12,8},{8,0},{0,4},{5,13},{13,9},{9,1},{1,5},{6,14},{14,10}... | collective-permute-start | bytes 589832 | tf_op jit(solution)/shard_map/ppermute | solution.py:347
  9.6 6.9 %collective-permute-start.10 = (bf16[256,384]{1,0:T(8,128)(2,1)S(1)}, bf16[256,384]{1,0:T(8,128)(2,1)S(1)}, u32[]{:S(2)}, u32[]{:S(2)}) collective-permute-start(bf16[256,384]{1,0:T(8,128)(2,1)S(1)} %get-tuple-element.37.refs_0_), channel_id=1, source_target_pairs={{0,1},{1,0},{2,3},{3,2},{4,5},{5,4},{6,7},{7,6},{8,9},{9,8},{10,11... | collective-permute-start | bytes 589832 | tf_op jit(solution)/shard_map/ppermute | solution.py:350
  12.3 8.2 %collective-permute-start.6 = (bf16[256,384]{1,0:T(8,128)(2,1)S(1)}, bf16[256,384]{1,0:T(8,128)(2,1)S(1)}, u32[]{:S(2)}, u32[]{:S(2)}) collective-permute-start(bf16[256,384]{1,0:T(8,128)(2,1)S(1)} %collective-permute-done.4.refs_2_), channel_id=1, source_target_pairs={{4,12},{12,8},{8,0},{0,4},{5,13},{13,9},{9,1},{1,5},{6,14},{14,10}... | collective-permute-start | bytes 589832 | tf_op jit(solution)/shard_map/ppermute | solution.py:347
  13.4 8.7 %collective-permute-start.5 = (bf16[256,384]{1,0:T(8,128)(2,1)S(1)}, bf16[256,384]{1,0:T(8,128)(2,1)S(1)}, u32[]{:S(2)}, u32[]{:S(2)}) collective-permute-start(bf16[256,384]{1,0:T(8,128)(2,1)S(1)} %collective-permute-done.4.refs_2_), channel_id=1, source_target_pairs={{0,1},{1,0},{2,3},{3,2},{4,5},{5,4},{6,7},{7,6},{8,9},{9,8},{10,11... | collective-permute-start | bytes 589832 | tf_op jit(solution)/shard_map/ppermute | solution.py:350
  16.5 7.1 %collective-permute-start.12 = (bf16[256,384]{1,0:T(8,128)(2,1)S(1)}, bf16[256,384]{1,0:T(8,128)(2,1)S(1)}, u32[]{:S(2)}, u32[]{:S(2)}) collective-permute-start(bf16[256,384]{1,0:T(8,128)(2,1)S(1)} %collective-permute-done.11.refs_2_), channel_id=1, source_target_pairs={{0,1},{1,0},{2,3},{3,2},{4,5},{5,4},{6,7},{7,6},{8,9},{9,8},{10,11... | collective-permute-start | bytes 589832 | tf_op jit(solution)/shard_map/ppermute | solution.py:350
  16.5 8.2 %collective-permute-start.13 = (bf16[256,384]{1,0:T(8,128)(2,1)S(1)}, bf16[256,384]{1,0:T(8,128)(2,1)S(1)}, u32[]{:S(2)}, u32[]{:S(2)}) collective-permute-start(bf16[256,384]{1,0:T(8,128)(2,1)S(1)} %collective-permute-done.11.refs_2_), channel_id=1, source_target_pairs={{4,12},{12,8},{8,0},{0,4},{5,13},{13,9},{9,1},{1,5},{6,14},{14,10}... | collective-permute-start | bytes 589832 | tf_op jit(solution)/shard_map/ppermute | solution.py:347
  20.5 7.2 %collective-permute-start.7 = (bf16[256,384]{1,0:T(8,128)(2,1)S(1)}, bf16[256,384]{1,0:T(8,128)(2,1)S(1)}, u32[]{:S(2)}, u32[]{:S(2)}) collective-permute-start(bf16[256,384]{1,0:T(8,128)(2,1)S(1)} %collective-permute-done.6.refs_4_), channel_id=1, source_target_pairs={{0,1},{1,0},{2,3},{3,2},{4,5},{5,4},{6,7},{7,6},{8,9},{9,8},{10,11... | collective-permute-start | bytes 589832 | tf_op jit(solution)/shard_map/ppermute | solution.py:350
  20.5 19.2 %collective-permute-start.1 = (bf16[1536,128]{1,0:T(8,128)(2,1)S(1)}, bf16[1536,128]{1,0:T(8,128)(2,1)S(1)}, u32[]{:S(2)}, u32[]{:S(2)}) collective-permute-start(bf16[1536,128]{1,0:T(8,128)(2,1)S(1)} %get-tuple-element.29), channel_id=1, source_target_pairs={{0,2},{2,0},{1,3},{3,1},{4,6},{6,4},{5,7},{7,5},{8,10},{10,8},{9,1... | collective-permute-start | bytes 1179656 | tf_op jit(solution)/shard_map/ppermute | solution.py:362
  22.1 17.7 %collective-permute-start.2 = (bf16[1536,128]{1,0:T(8,128)(2,1)S(1)}, bf16[1536,128]{1,0:T(8,128)(2,1)S(1)}, u32[]{:S(2)}, u32[]{:S(2)}) collective-permute-start(bf16[1536,128]{1,0:T(8,128)(2,1)S(1)} %collective-permute-done.refs_1_), channel_id=1, source_target_pairs={{0,16},{16,0},{1,17},{17,1},{2,18},{18,2},{3,19},{19,3},{4,20},{20... | collective-permute-start | bytes 1179656 | tf_op jit(solution)/shard_map/ppermute | solution.py:363
  23.6 8.7 %collective-permute-start.8 = (bf16[256,384]{1,0:T(8,128)(2,1)S(1)}, bf16[256,384]{1,0:T(8,128)(2,1)S(1)}, u32[]{:S(2)}, u32[]{:S(2)}) collective-permute-start(bf16[256,384]{1,0:T(8,128)(2,1)S(1)} %collective-permute-done.6.refs_4_), channel_id=1, source_target_pairs={{4,12},{12,8},{8,0},{0,4},{5,13},{13,9},{9,1},{1,5},{6,14},{14,10}... | collective-permute-start | bytes 589832 | tf_op jit(solution)/shard_map/ppermute | solution.py:347
  24.7 10.7 %collective-permute-start.15 = (bf16[256,384]{1,0:T(8,128)(2,1)S(1)}, bf16[256,384]{1,0:T(8,128)(2,1)S(1)}, u32[]{:S(2)}, u32[]{:S(2)}) collective-permute-start(bf16[256,384]{1,0:T(8,128)(2,1)S(1)} %collective-permute-done.13.refs_4_), channel_id=1, source_target_pairs={{4,12},{12,8},{8,0},{0,4},{5,13},{13,9},{9,1},{1,5},{6,14},{14,10}... | collective-permute-start | bytes 589832 | tf_op jit(solution)/shard_map/ppermute | solution.py:347
  27.8 10.7 %collective-permute-start.14 = (bf16[256,384]{1,0:T(8,128)(2,1)S(1)}, bf16[256,384]{1,0:T(8,128)(2,1)S(1)}, u32[]{:S(2)}, u32[]{:S(2)}) collective-permute-start(bf16[256,384]{1,0:T(8,128)(2,1)S(1)} %collective-permute-done.13.refs_4_), channel_id=1, source_target_pairs={{0,1},{1,0},{2,3},{3,2},{4,5},{5,4},{6,7},{7,6},{8,9},{9,8},{10,11... | collective-permute-start | bytes 589832 | tf_op jit(solution)/shard_map/ppermute | solution.py:350
  32.3 9.3 %collective-permute-start.9 = (bf16[256,384]{1,0:T(8,128)(2,1)S(1)}, bf16[256,384]{1,0:T(8,128)(2,1)S(1)}, u32[]{:S(2)}, u32[]{:S(2)}) collective-permute-start(bf16[256,384]{1,0:T(8,128)(2,1)S(1)} %collective-permute-done.8.refs_0_), channel_id=1, source_target_pairs={{0,1},{1,0},{2,3},{3,2},{4,5},{5,4},{6,7},{7,6},{8,9},{9,8},{10,11... | collective-permute-start | bytes 589832 | tf_op jit(solution)/shard_map/ppermute | solution.py:350
  35.4 11.6 %collective-permute-start.16 = (bf16[256,384]{1,0:T(8,128)(2,1)S(1)}, bf16[256,384]{1,0:T(8,128)(2,1)S(1)}, u32[]{:S(2)}, u32[]{:S(2)}) collective-permute-start(bf16[256,384]{1,0:T(8,128)(2,1)S(1)} %collective-permute-done.15.refs_0_), channel_id=1, source_target_pairs={{0,1},{1,0},{2,3},{3,2},{4,5},{5,4},{6,7},{7,6},{8,9},{9,8},{10,11... | collective-permute-start | bytes 589832 | tf_op jit(solution)/shard_map/ppermute | solution.py:350
  36.1 1.6 %copy-start = (f32[50,3,3072]{2,0,1:T(8,128)S(1)}, f32[50,3,3072]{2,0,1:T(8,128)}, u32[]{:S(2)}) copy-start(f32[50,3,3072]{2,0,1:T(8,128)} %param.9) | copy-start | bytes 5529604
  38.4 18.8 %collective-permute-start.26 = (bf16[256,384]{1,0:T(8,128)(2,1)S(1)}, bf16[256,384]{1,0:T(8,128)(2,1)S(1)}, u32[]{:S(2)}, u32[]{:S(2)}) collective-permute-start(bf16[256,384]{1,0:T(8,128)(2,1)S(1)} %shard_map.74), channel_id=1, source_target_pairs={{0,0},{2,8},{4,6},{6,14},{8,2},{10,10},{12,4},{14,12},{16,20},{18,... | collective-permute-start | bytes 589832 | tf_op jit(solution)/shard_map/ppermute | solution.py:427
  42.8 11.3 %collective-permute-start.17 = (bf16[256,256]{1,0:T(8,128)(2,1)S(1)}, bf16[256,256]{1,0:T(8,128)(2,1)S(1)}, u32[]{:S(2)}, u32[]{:S(2)}) collective-permute-start(bf16[256,256]{1,0:T(8,128)(2,1)S(1)} %get-tuple-element.42.refs_2_), channel_id=1, source_target_pairs={{0,2},{2,0},{1,3},{3,1},{4,6},{6,4},{5,7},{7,5},{8,10},{10,8},{9,1... | collective-permute-start | bytes 393224 | tf_op jit(solution)/shard_map/ppermute | solution.py:468
  48.3 7.9 %collective-permute-start.18 = (bf16[256,256]{1,0:T(8,128)(2,1)S(1)}, bf16[256,256]{1,0:T(8,128)(2,1)S(1)}, u32[]{:S(2)}, u32[]{:S(2)}) collective-permute-start(bf16[256,256]{1,0:T(8,128)(2,1)S(1)} %get-tuple-element.43.refs_3_), channel_id=1, source_target_pairs={{0,2},{2,0},{1,3},{3,1},{4,6},{6,4},{5,7},{7,5},{8,10},{10,8},{9,1... | collective-permute-start | bytes 393224 | tf_op jit(solution)/shard_map/ppermute | solution.py:468
  57.1 6.2 %collective-permute-start.20 = (bf16[512,128]{1,0:T(8,128)(2,1)S(1)}, bf16[512,128]{1,0:T(8,128)(2,1)S(1)}, u32[]{:S(2)}, u32[]{:S(2)}) collective-permute-start(bf16[512,128]{1,0:T(8,128)(2,1)S(1)} %shard_map.72.refs_0_), channel_id=1, source_target_pairs={{4,12},{12,8},{8,0},{0,4},{5,13},{13,9},{9,1},{1,5},{6,14},{14,10}... | collective-permute-start | bytes 393224 | tf_op jit(solution)/shard_map/ppermute | solution.py:486
  57.2 10.9 %collective-permute-start.27 = (bf16[256,384]{1,0:T(8,128)(2,1)S(1)}, bf16[256,384]{1,0:T(8,128)(2,1)S(1)}, u32[]{:S(2)}, u32[]{:S(2)}) collective-permute-start(bf16[256,384]{1,0:T(8,128)(2,1)S(1)} %collective-permute-done.26.refs_7_), channel_id=1, source_target_pairs={{0,2},{2,0},{16,18},{18,16},{1,3},{3,1},{17,19},{19,17},{4,6},{6,4... | collective-permute-start | bytes 589832 | tf_op jit(solution)/shard_map/ppermute | solution.py:439
  59.8 8.4 %collective-permute-start.28 = (bf16[256,384]{1,0:T(8,128)(2,1)S(1)}, bf16[256,384]{1,0:T(8,128)(2,1)S(1)}, u32[]{:S(2)}, u32[]{:S(2)}) collective-permute-start(bf16[256,384]{1,0:T(8,128)(2,1)S(1)} %collective-permute-done.26.refs_7_), channel_id=1, source_target_pairs={{0,16},{2,18},{16,0},{18,2},{1,17},{3,19},{17,1},{19,3},{4,20},{6,... | collective-permute-start | bytes 589832 | tf_op jit(solution)/shard_map/ppermute | solution.py:439
  60.5 8.2 %collective-permute-start.22 = (bf16[512,128]{1,0:T(8,128)(2,1)S(1)}, bf16[512,128]{1,0:T(8,128)(2,1)S(1)}, u32[]{:S(2)}, u32[]{:S(2)}) collective-permute-start(bf16[512,128]{1,0:T(8,128)(2,1)S(1)} %shard_map.72.refs_0_), channel_id=1, source_target_pairs={{4,0},{12,4},{8,12},{0,8},{5,1},{13,5},{9,13},{1,9},{6,2},{14,6},{... | collective-permute-start | bytes 393224 | tf_op jit(solution)/shard_map/ppermute | solution.py:488
  63.3 6.6 %collective-permute-start.24 = (bf16[512,128]{1,0:T(8,128)(2,1)S(1)}, bf16[512,128]{1,0:T(8,128)(2,1)S(1)}, u32[]{:S(2)}, u32[]{:S(2)}) collective-permute-start(bf16[512,128]{1,0:T(8,128)(2,1)S(1)} %collective-permute-done.20.refs_2_), channel_id=1, source_target_pairs={{4,12},{12,8},{8,0},{0,4},{5,13},{13,9},{9,1},{1,5},{6,14},{14,10}... | collective-permute-start | bytes 393224 | tf_op jit(solution)/shard_map/ppermute | solution.py:486
  63.3 8.5 %collective-permute-start.29 = (bf16[256,384]{1,0:T(8,128)(2,1)S(1)}, bf16[256,384]{1,0:T(8,128)(2,1)S(1)}, u32[]{:S(2)}, u32[]{:S(2)}) collective-permute-start(bf16[256,384]{1,0:T(8,128)(2,1)S(1)} %collective-permute-done.26.refs_7_), channel_id=1, source_target_pairs={{0,18},{2,16},{16,2},{18,0},{1,19},{3,17},{17,3},{19,1},{4,22},{6,... | collective-permute-start | bytes 589832 | tf_op jit(solution)/shard_map/ppermute | solution.py:439
  68.2 3.6 %collective-permute-start.19 = (bf16[512,128]{1,0:T(8,128)(2,1)S(1)}, bf16[512,128]{1,0:T(8,128)(2,1)S(1)}, u32[]{:S(2)}, u32[]{:S(2)}) collective-permute-start(bf16[512,128]{1,0:T(8,128)(2,1)S(1)} %shard_map.72.refs_0_), channel_id=1, source_target_pairs={{0,1},{1,0},{2,3},{3,2},{4,5},{5,4},{6,7},{7,6},{8,9},{9,8},{10,11... | collective-permute-start | bytes 393224 | tf_op jit(solution)/shard_map/ppermute | solution.py:491
  68.2 3.6 %collective-permute-start.21 = (bf16[512,128]{1,0:T(8,128)(2,1)S(1)}, bf16[512,128]{1,0:T(8,128)(2,1)S(1)}, u32[]{:S(2)}, u32[]{:S(2)}) collective-permute-start(bf16[512,128]{1,0:T(8,128)(2,1)S(1)} %collective-permute-done.20.refs_2_), channel_id=1, source_target_pairs={{0,1},{1,0},{2,3},{3,2},{4,5},{5,4},{6,7},{7,6},{8,9},{9,8},{10,11... | collective-permute-start | bytes 393224 | tf_op jit(solution)/shard_map/ppermute | solution.py:491
  68.7 3.1 %collective-permute-start.23 = (bf16[512,128]{1,0:T(8,128)(2,1)S(1)}, bf16[512,128]{1,0:T(8,128)(2,1)S(1)}, u32[]{:S(2)}, u32[]{:S(2)}) collective-permute-start(bf16[512,128]{1,0:T(8,128)(2,1)S(1)} %collective-permute-done.22.refs_4_), channel_id=1, source_target_pairs={{0,1},{1,0},{2,3},{3,2},{4,5},{5,4},{6,7},{7,6},{8,9},{9,8},{10,11... | collective-permute-start | bytes 393224 | tf_op jit(solution)/shard_map/ppermute | solution.py:491
  69.9 2.8 %collective-permute-start.30 = (bf16[512,128]{1,0:T(8,128)(2,1)S(1)}, bf16[512,128]{1,0:T(8,128)(2,1)S(1)}, u32[]{:S(2)}, u32[]{:S(2)}) collective-permute-start(bf16[512,128]{1,0:T(8,128)(2,1)S(1)} %collective-permute-done.24.refs_6_), channel_id=1, source_target_pairs={{0,1},{1,0},{2,3},{3,2},{4,5},{5,4},{6,7},{7,6},{8,9},{9,8},{10,11... | collective-permute-start | bytes 393224 | tf_op jit(solution)/shard_map/ppermute | solution.py:491

commit v4 on v3

--- a/solution.py
+++ b/solution.py
@@ -14,6 +14,7 @@
 SMEM = pl.BlockSpec(memory_space=pltpu.SMEM)
 PARAMS = pltpu.CompilerParams(vmem_limit_bytes=16 << 20)
 LANES = 128
+VECTORS = 16
 f32, bf16 = jnp.float32, jnp.bfloat16
 
 
@@ -86,12 +87,20 @@
     run_copies(copies)
 
 
-def table_body(at, m_ref, out_ref):
+def table_body(at, m_ref, out_ref, vec_ref):
     _, slices, width = out_ref.shape
-    for i in range(3):
-        row = m_ref[i, pl.ds(at[0], 1), :]
-        for f in range(slices):
-            out_ref[i, f : f + 1, :] = row[:, f * width : (f + 1) * width]
+    rows = [m_ref[i, pl.ds(at[0], 1), :] for i in range(3)]
+    for f in range(slices):
+        cut = [row[:, f * width : (f + 1) * width] for row in rows]
+        for i in range(3):
+            out_ref[i, f : f + 1, :] = cut[i]
+        rest = jnp.concatenate([1.0 + cut[1], cut[0]], axis=0)
+        parts = []
+        for _ in range(3):
+            parts.append(rest.astype(bf16).astype(f32))
+            rest = rest - parts[-1]
+        parts.append(jnp.zeros((VECTORS - 6, width), f32))
+        vec_ref[f] = jnp.concatenate(parts, axis=0).astype(bf16)
 
 
 def column_of(sizes, shift, u, width):
@@ -124,14 +133,14 @@
         out_ref[i * rows : (i + 1) * rows, :] = in_ref[...]
 
 
-def merge_body(pieces, table_ref, *refs):
+def merge_body(pieces, *refs):
     w_refs = refs[: len(pieces)]
-    out_ref, vec_ref, sem = refs[len(pieces) :]
+    out_ref, sem = refs[len(pieces) :]
     blk_at, grp_at = lax.axis_index("blk"), lax.axis_index("group")
     copies = []
-    for j, (planes, place, column) in enumerate(pieces):
+    for j, (planes, offset, column) in enumerate(pieces):
         rows, head = w_refs[j].shape[-2:]
-        first = pl.multiple_of(place(blk_at) * rows, rows)
+        first = pl.multiple_of(back(blk_at, offset, w_blocks(pieces)) * rows, rows)
         for i in range(planes):
             source = w_refs[j].at[i] if planes > 1 else w_refs[j]
             at = i * head if planes > 1 else pl.multiple_of(column(grp_at) * head, head)
@@ -141,24 +150,10 @@
                 )
             )
     run_copies(copies)
-    _, slices, width = table_ref.shape
-    total = None
-    for f in range(slices):
-        shift, scale = table_ref[0, f : f + 1, :], 1.0 + table_ref[1, f : f + 1, :]
-        rest = jnp.concatenate([scale, shift], axis=0)
-        parts = []
-        for _ in range(3):
-            part = rest.astype(bf16)
-            parts.append(part)
-            rest = rest - part.astype(f32)
-        vectors = jnp.concatenate(
-            [p.astype(f32) for p in parts] + [jnp.zeros((2, width), f32)], axis=0
-        ).astype(bf16)
-        part = jnp.dot(
-            vectors, out_ref[f * width : (f + 1) * width, :], preferred_element_type=f32
-        )
-        total = part if total is None else total + part
-    vec_ref[0:2, :] = total[0:2] + total[2:4] + total[4:6]
+
+
+def w_blocks(pieces):
+    return 1 + max(offset for _, offset, _ in pieces)
 
 
 def fold(values):
@@ -202,10 +197,10 @@
     lax.fori_loop(0, rows // tile, step, 0)
 
 
-def project_body(sizes, early, last, table_ref, w_ref, vec_ref, y_ref, mean_ref, square_ref, *refs):
+def project_body(sizes, early, last, first, table_ref, w_ref, vec_ref, y_ref, mean_ref, square_ref, *refs):
     x_refs = refs[: len(last)]
-    q_ref, kv_ref, buf = refs[len(last) :]
-    _, width = x_refs[0].shape
+    q_ref, kv_ref, *made_ref, buf = refs[len(last) :]
+    rows, width = x_refs[0].shape
     head = q_ref.shape[1]
     features = (len(early) + len(last)) * width
     centre = mean_ref[:, 0:1]
@@ -222,11 +217,19 @@
     inverse = lax.rsqrt(spread - delta * delta + epsilon)
     acc = None
     for s, slot in enumerate(early + last):
-        first = pl.multiple_of(slot_place(sizes, *slot) * width, width)
+        place = slot_place(sizes, *slot)
         values = y_ref[s] if s < len(early) else buf[s - len(early)]
-        part = jnp.dot(values, w_ref[pl.ds(first, width), :], preferred_element_type=f32)
+        if first:
+            values = jnp.concatenate([values, vec_ref[place]], axis=0)
+        at = pl.ds(pl.multiple_of(place * width, width), width)
+        part = jnp.dot(values, w_ref[at, :], preferred_element_type=f32)
         acc = part if acc is None else acc + part
-    result = ((acc - delta * vec_ref[0:1, :]) * inverse + vec_ref[1:2, :]).astype(bf16)
+    if first:
+        vectors = acc[rows : rows + 2] + acc[rows + 2 : rows + 4] + acc[rows + 4 : rows + 6]
+        made_ref[0][0:2] = vectors
+    else:
+        vectors = vec_ref[0:2]
+    result = ((acc[:rows] - delta * vectors[0:1]) * inverse + vectors[1:2]).astype(bf16)
     q_ref[...] = result[:, :head]
     kv_ref[...] = result[:, head:]
 
@@ -349,13 +352,13 @@
             for u in range(1, n_tp):
                 slots[chunk][step, u] = lax.ppermute(current[chunk], "tp", rotation(n_tp, u))
 
-    (table,) = kernel(
+    table, vectors = kernel(
         table_body,
-        [((3, slices, own_width), f32)],
+        [((3, slices, own_width), f32), ((slices, VECTORS, own_width), bf16)],
         [(timestep, "smem"), (jnp.swapaxes(modulation, 0, 1), "near")],
     )
 
-    parts, pieces = [(qkv_weight, "far")], [(3, lambda b: b, None)]
+    parts, pieces = [(qkv_weight, "far")], [(3, 0, None)]
     if by_two:
         relayed, direct = cut[2:]
         first = lax.ppermute(relayed, "blk", rotation(2, 1))
@@ -363,18 +366,18 @@
         third = lax.ppermute(first, "group", rotation(2, 1))
         parts += [(first, "near"), (second, "near"), (third, "near")]
         pieces += [
-            (1, lambda b: 1 - b, lambda g: g),
-            (1, lambda b: 1 - b, lambda g: 2),
-            (1, lambda b: 1 - b, lambda g: 1 - g),
+            (1, 1, lambda g: g),
+            (1, 1, lambda g: 2),
+            (1, 1, lambda g: 1 - g),
         ]
     else:
         for j in range(1, n_blk):
             parts.append((lax.ppermute(qkv_weight, "blk", rotation(n_blk, j)), "near"))
-            pieces.append((3, lambda b, j=j: back(b, j, n_blk), None))
-    weight, vectors = kernel(
+            pieces.append((3, j, None))
+    (weight,) = kernel(
         functools.partial(merge_body, pieces),
-        [((slices * own_width, 3 * head), bf16), ((8, 3 * head), f32)],
-        [(table, "near")] + parts,
+        [((slices * own_width, 3 * head), bf16)],
+        parts,
         [DMA((len(pieces), 3))],
     )
 
@@ -387,7 +390,8 @@
             low = lax.rem(lax.axis_index("seq"), n_low)
             s = back(lax.axis_index("group"), -shift, n_grp) if shared else shift
             low = lax.rem(low - s + n_low, n_low)
-            high = lax.rem(lax.axis_index("blk") - k3 - low + (n_low + 1) * n_blk, n_blk)
+            own = lax.div(lax.axis_index("seq"), n_low)
+            high = lax.rem(lax.axis_index("blk") - own - k3 - low + (n_low + 2) * n_blk, n_blk)
             return high * n_low + low
 
         return source
@@ -416,15 +420,22 @@
             stack_body, [((n_tp * head, own_width), bf16)], [(x, "near") for x in received]
         )
         for k3 in range(1 if shared else n_blk):
-            pairs = []
+            hops, pairs, whole = [], [], []
             for g in range(n_grp):
                 for z in range(n_seq):
                     for b in range(n_blk):
                         l2 = (z % n_low + (g if shared else k1)) % n_low
-                        x2 = (z // n_low + z % n_low + k3) % n_blk
+                        x2 = (b + z // n_low + z % n_low + k3) % n_blk
+                        there = (g * n_seq + z) * n_blk
                         target = (g * n_seq + b * n_low + l2) * n_blk + x2
-                        pairs.append(((g * n_seq + z) * n_blk + b, target))
-            arrived = lax.ppermute(rows, ("group", "seq", "blk"), pairs)
+                        hops.append((z * n_blk + b, z * n_blk + x2))
+                        pairs.append((there + x2, target))
+                        whole.append((there + b, target))
+            if shared:
+                moved = lax.ppermute(rows, ("seq", "blk"), hops[: n_seq * n_blk])
+                arrived = lax.ppermute(moved, ("group", "seq", "blk"), pairs)
+            else:
+                arrived = lax.ppermute(rows, ("group", "seq", "blk"), whole)
             o_parts.append(arrived)
             o_sources.append(source_of(k3, 0 if shared else k1))
         if shared:
@@ -455,13 +466,16 @@
     ]
     q_parts, kv_own, kv_rest = [], [], []
     for chunk in range(2):
-        q, kv = kernel(
-            functools.partial(project_body, sizes, early, last),
-            [((half, head), bf16), ((half, 2 * head), bf16)],
+        q, kv, *made = kernel(
+            functools.partial(project_body, sizes, early, last, chunk == 0),
+            [((half, head), bf16), ((half, 2 * head), bf16)]
+            + [((8, 3 * head), f32)] * (chunk == 0),
             [(x, "near") for x in (table, weight, vectors, *starts[chunk])]
             + [(slots[chunk][slot], "near") for slot in last],
             [pltpu.VMEM((len(last), half, own_width), bf16)],
         )
+        if made:
+            (vectors,) = made
         q_parts.append(q)
         kv_own.append(kv)
         for j in range(1, n_blk):

time: 73.9 us -> 71.7 us (0.970)
  the two profiles are of different devices: /device:TPU:0 before, /device:TPU:12 now
where the time goes in v4:
time: 71.7 us; the launch traced here: 71.5 us
  waiting for transfers between devices  31.1 us (43%)
  starting transfers between devices  27.5 us (38%)
  Pallas kernels  11.4 us (16%)
  between operations  1.49 us (2%)
    ppermute x6, waiting for transfers between devices, block(): current[chunk] = lax.ppermute(current[chunk], 'seq', forward)  12.1 us
    pallas_call x12, Pallas kernels, kernel(): pl.pallas_call(body, out_shape=tuple((pltpu.VMEM(shape, dtype) for shape,...  10.5 us
    ppermute x6, starting transfers between devices, block(): current[chunk] = lax.ppermute(current[chunk], 'seq', forward)  8.09 us
    ppermute x2, starting transfers between devices, block(): up = att[step, 0] = lax.ppermute(up, 'seq', forward)  7.19 us
    ppermute x1, waiting for transfers between devices, block(): moved = lax.ppermute(rows, ('seq', 'blk'), hops[:n_seq * n_blk])  5.51 us
    ppermute x2, waiting for transfers between devices, block(): up = att[step, 0] = lax.ppermute(up, 'seq', forward)  5.45 us
    ppermute x3, waiting for transfers between devices, block(): o_parts.append(lax.ppermute(arrived, ('group', 'blk'), swap))  4.05 us
    ppermute x2, waiting for transfers between devices, block(): kv_rest.append(lax.ppermute(kv, 'blk', rotation(n_blk, j)))  3.96 us
  transfers between devices with their start and end apart: 32, of which 11 were waited for; matrix products, arithmetic and copies ran while one was open for 0% of the time, Pallas kernels for 13%

profile of v4, /device:TPU:12, one launch (start us, length us, event | category | flops | bytes accessed | tf_op | source)
XLA Modules:
  0.0 71.5 jit_solution(16882551631819294301)
XLA Ops:
  0.0 1.5 %shard_map.65 = (bf16[256,384]{1,0:T(8,128)(2,1)S(1)}, bf16[256,384]{1,0:T(8,128)(2,1)S(1)}, bf16[1536,128]{1,0:T(8,128)(2,1)S(1)}, bf16[1536,128]{1,0:T(8,128)(2,1)S(1)}) custom-call(bf16[512,384]{1,0:T(8,128)(2,1)} %x_ref.1, bf16[3,1536,128]{2,1,0:T(8,128)(2,1)} %refs_0_.1), custom_call_target="tpu_custom_call" | custom-call | tf_op jit(solution)/shard_map/pallas_call | solution.py:57
  1.5 0.1 collective-permute-start.3
  1.6 1.0 %shard_map.73 = (bf16[128,384]{1,0:T(8,128)(2,1)S(1)}, bf16[128,384]{1,0:T(8,128)(2,1)S(1)}) custom-call(bf16[128,1536]{1,0:T(8,128)(2,1)} %w_ref.3), custom_call_target="tpu_custom_call" | custom-call | tf_op jit(solution)/shard_map/pallas_call | solution.py:57
  2.6 0.5 collective-permute-start.25
  3.1 2.6 %collective-permute-start.4 = (bf16[256,384]{1,0:T(8,128)(2,1)S(1)}, bf16[256,384]{1,0:T(8,128)(2,1)S(1)}, u32[]{:S(2)}, u32[]{:S(2)}) collective-permute-start(bf16[256,384]{1,0:T(8,128)(2,1)S(1)} %get-tuple-element.33.refs_0_), channel_id=1, source_target_pairs={{4,12},{12,8},{8,0},{0,4},{5,13},{13,9},{9,1},{1,5},{6,14},{14,10}... | collective-permute-start | bytes 589832 | tf_op jit(solution)/shard_map/ppermute | solution.py:350
  5.7 1.5 %collective-permute-start = (bf16[1536,128]{1,0:T(8,128)(2,1)S(1)}, bf16[1536,128]{1,0:T(8,128)(2,1)S(1)}, u32[]{:S(2)}, u32[]{:S(2)}) collective-permute-start(bf16[1536,128]{1,0:T(8,128)(2,1)S(1)} %get-tuple-element.30), channel_id=1, source_target_pairs={{0,2},{2,0},{1,3},{3,1},{4,6},{6,4},{5,7},{7,5},{8,10},{10,8},{9,1... | collective-permute-start | bytes 1179656 | tf_op jit(solution)/shard_map/ppermute | solution.py:364
  7.2 0.0 collective-permute-start.10
  7.2 0.5 collective-permute-start.11
  7.7 0.0 collective-permute-done.3.refs_1_
  7.7 2.4 %collective-permute-start.26 = (bf16[256,384]{1,0:T(8,128)(2,1)S(1)}, bf16[256,384]{1,0:T(8,128)(2,1)S(1)}, u32[]{:S(2)}, u32[]{:S(2)}) collective-permute-start(bf16[256,384]{1,0:T(8,128)(2,1)S(1)} %shard_map.74), channel_id=1, source_target_pairs={{0,0},{2,2},{4,6},{6,4},{8,10},{10,8},{12,12},{14,14},{1,1},{3,3},... | collective-permute-start | bytes 589832 | tf_op jit(solution)/shard_map/ppermute | solution.py:435
  10.1 0.9 %collective-permute-done.4.refs_2_ = bf16[256,384]{1,0:T(8,128)(2,1)S(1)} collective-permute-done((bf16[256,384]{1,0:T(8,128)(2,1)S(1)}, bf16[256,384]{1,0:T(8,128)(2,1)S(1)}, u32[]{:S(2)}, u32[]{:S(2)}) %collective-permute-start.4) | collective-permute-done | bytes 196640 | tf_op jit(solution)/shard_map/ppermute | solution.py:350
  11.0 3.4 %collective-permute-start.6 = (bf16[256,384]{1,0:T(8,128)(2,1)S(1)}, bf16[256,384]{1,0:T(8,128)(2,1)S(1)}, u32[]{:S(2)}, u32[]{:S(2)}) collective-permute-start(bf16[256,384]{1,0:T(8,128)(2,1)S(1)} %collective-permute-done.4.refs_2_), channel_id=1, source_target_pairs={{4,12},{12,8},{8,0},{0,4},{5,13},{13,9},{9,1},{1,5},{6,14},{14,10}... | collective-permute-start | bytes 589832 | tf_op jit(solution)/shard_map/ppermute | solution.py:350
  14.4 0.0 collective-permute-done.10.refs_1_
  14.4 0.8 %collective-permute-done.11.refs_2_ = bf16[256,384]{1,0:T(8,128)(2,1)S(1)} collective-permute-done((bf16[256,384]{1,0:T(8,128)(2,1)S(1)}, bf16[256,384]{1,0:T(8,128)(2,1)S(1)}, u32[]{:S(2)}, u32[]{:S(2)}) %collective-permute-start.11) | collective-permute-done | bytes 196640 | tf_op jit(solution)/shard_map/ppermute | solution.py:350
  15.2 5.5 %collective-permute-done.26 = bf16[256,384]{1,0:T(8,128)(2,1)S(1)} collective-permute-done((bf16[256,384]{1,0:T(8,128)(2,1)S(1)}, bf16[256,384]{1,0:T(8,128)(2,1)S(1)}, u32[]{:S(2)}, u32[]{:S(2)}) %collective-permute-start.26) | collective-permute-done | bytes 196640 | tf_op jit(solution)/shard_map/ppermute | solution.py:435
  20.7 0.0 collective-permute-start.7
  20.7 0.0 collective-permute-done.refs_1_
  20.7 1.6 %collective-permute-start.1 = (bf16[1536,128]{1,0:T(8,128)(2,1)S(1)}, bf16[1536,128]{1,0:T(8,128)(2,1)S(1)}, u32[]{:S(2)}, u32[]{:S(2)}) collective-permute-start(bf16[1536,128]{1,0:T(8,128)(2,1)S(1)} %get-tuple-element.31), channel_id=1, source_target_pairs={{0,2},{2,0},{1,3},{3,1},{4,6},{6,4},{5,7},{7,5},{8,10},{10,8},{9,1... | collective-permute-start | bytes 1179656 | tf_op jit(solution)/shard_map/ppermute | solution.py:365
  22.3 0.5 collective-permute-start.2
  22.8 1.1 %collective-permute-start.8 = (bf16[256,384]{1,0:T(8,128)(2,1)S(1)}, bf16[256,384]{1,0:T(8,128)(2,1)S(1)}, u32[]{:S(2)}, u32[]{:S(2)}) collective-permute-start(bf16[256,384]{1,0:T(8,128)(2,1)S(1)} %collective-permute-done.6.refs_4_), channel_id=1, source_target_pairs={{4,12},{12,8},{8,0},{0,4},{5,13},{13,9},{9,1},{1,5},{6,14},{14,10}... | collective-permute-start | bytes 589832 | tf_op jit(solution)/shard_map/ppermute | solution.py:350
  23.9 3.4 %collective-permute-done.13.refs_4_ = bf16[256,384]{1,0:T(8,128)(2,1)S(1)} collective-permute-done((bf16[256,384]{1,0:T(8,128)(2,1)S(1)}, bf16[256,384]{1,0:T(8,128)(2,1)S(1)}, u32[]{:S(2)}, u32[]{:S(2)}) %collective-permute-start.13) | collective-permute-done | bytes 196640 | tf_op jit(solution)/shard_map/ppermute | solution.py:350
  27.3 0.6 collective-permute-start.15
  27.9 3.6 %collective-permute-done.8.refs_0_ = bf16[256,384]{1,0:T(8,128)(2,1)S(1)} collective-permute-done((bf16[256,384]{1,0:T(8,128)(2,1)S(1)}, bf16[256,384]{1,0:T(8,128)(2,1)S(1)}, u32[]{:S(2)}, u32[]{:S(2)}) %collective-permute-start.8) | collective-permute-done | bytes 196640 | tf_op jit(solution)/shard_map/ppermute | solution.py:350
  31.6 3.3 %collective-permute-done.15.refs_0_ = bf16[256,384]{1,0:T(8,128)(2,1)S(1)} collective-permute-done((bf16[256,384]{1,0:T(8,128)(2,1)S(1)}, bf16[256,384]{1,0:T(8,128)(2,1)S(1)}, u32[]{:S(2)}, u32[]{:S(2)}) %collective-permute-start.15) | collective-permute-done | bytes 196640 | tf_op jit(solution)/shard_map/ppermute | solution.py:350
  35.5 0.1 shard_map.64
  35.6 0.7 shard_map.67
  36.3 1.9 %collective-permute-start.27 = (bf16[256,384]{1,0:T(8,128)(2,1)S(1)}, bf16[256,384]{1,0:T(8,128)(2,1)S(1)}, u32[]{:S(2)}, u32[]{:S(2)}) collective-permute-start(bf16[256,384]{1,0:T(8,128)(2,1)S(1)} %collective-permute-done.26), channel_id=1, source_target_pairs={{0,0},{2,10},{6,6},{4,12},{10,2},{8,8},{12,4},{14,14},{16,20},{18,... | collective-permute-start | bytes 589832 | tf_op jit(solution)/shard_map/ppermute | solution.py:436
  38.2 0.7 shard_map.69
  38.9 1.4 %shard_map.66.w_ref = bf16[3072,384]{1,0:T(8,128)(2,1)S(1)} custom-call(bf16[3,1536,128]{2,1,0:T(8,128)(2,1)} %refs_0_.1, bf16[1536,128]{1,0:T(8,128)(2,1)S(1)} %collective-permute-done.refs_1_, bf16[1536,128]{1,0:T(8,128)(2,1)S(1)} %collective-permute-done.1.refs_2_, bf16[1536,128]{1,0:T(8,128)(2,1)S(1)} %collective-permute-done.2.refs_3_), custom_call_target="tpu_custom_call" | custom-call | tf_op jit(solution)/shard_map/pallas_call | solution.py:57
  40.3 1.4 %shard_map.68 = (bf16[256,128]{1,0:T(8,128)(2,1)S(1)}, bf16[256,256]{1,0:T(8,128)(2,1)S(1)}, f32[8,384]{1,0:T(8,128)S(1)}) custom-call(f32[3,8,384]{2,1,0:T(8,128)S(1)} %get-tuple-element.29.table_ref, bf16[3072,384]{1,0:T(8,128)(2,1)S(1)} %shard_map.66.w_ref, bf16[8,16,384]{2,1,0:T(8,128)(2,1)S(1)} %get-tuple-element.32.vec_ref, ...), custom_call_target="tpu_custom_call" | custom-call | tf_op jit(solution)/shard_map/pallas_call | solution.py:57
  41.7 2.3 %collective-permute-start.17 = (bf16[256,256]{1,0:T(8,128)(2,1)S(1)}, bf16[256,256]{1,0:T(8,128)(2,1)S(1)}, u32[]{:S(2)}, u32[]{:S(2)}) collective-permute-start(bf16[256,256]{1,0:T(8,128)(2,1)S(1)} %get-tuple-element.44.refs_2_), channel_id=1, source_target_pairs={{0,2},{2,0},{1,3},{3,1},{4,6},{6,4},{5,7},{7,5},{8,10},{10,8},{9,1... | collective-permute-start | bytes 393224 | tf_op jit(solution)/shard_map/ppermute | solution.py:482
  44.1 1.2 %shard_map.70 = (bf16[256,128]{1,0:T(8,128)(2,1)S(1)}, bf16[256,256]{1,0:T(8,128)(2,1)S(1)}) custom-call(f32[3,8,384]{2,1,0:T(8,128)S(1)} %get-tuple-element.29.table_ref, bf16[3072,384]{1,0:T(8,128)(2,1)S(1)} %shard_map.66.w_ref, f32[8,384]{1,0:T(8,128)S(1)} %get-tuple-element.38.vec_ref, bf16[6,256,384]{2,1,0:T(8,128)(2,1)S(1)} %get-tuple-element.40.y_ref, ...), custom_call_target="tpu_custom_call" | custom-call | tf_op jit(solution)/shard_map/pallas_call | solution.py:57
  45.2 0.1 collective-permute-start.18
  46.0 0.8 %shard_map.71 = (f32[512,128]{1,0:T(8,128)S(1)}, f32[512,128]{1,0:T(8,128)S(1)}, f32[512,128]{1,0:T(8,128)S(1)}) custom-call(s32[1]{0:T(128)S(6)} %copy.8.padded, bf16[256,128]{1,0:T(8,128)(2,1)S(1)} %get-tuple-element.37.refs_0_, bf16[256,128]{1,0:T(8,128)(2,1)S(1)} %get-tuple-element.43.refs_1_, bf16[256,256]{1,0:T(8,128)(2,1)S(1)} %get-tuple-element.44.refs_2_, ...), custom_call_target="tpu_custom_call" | custom-call | tf_op jit(solution)/shard_map/pallas_call | solution.py:57
  46.8 1.2 %collective-permute-done.17.refs_2_ = bf16[256,256]{1,0:T(8,128)(2,1)S(1)} collective-permute-done((bf16[256,256]{1,0:T(8,128)(2,1)S(1)}, bf16[256,256]{1,0:T(8,128)(2,1)S(1)}, u32[]{:S(2)}, u32[]{:S(2)}) %collective-permute-start.17) | collective-permute-done | bytes 131104 | tf_op jit(solution)/shard_map/ppermute | solution.py:482
  48.0 2.7 %collective-permute-done.18.refs_3_ = bf16[256,256]{1,0:T(8,128)(2,1)S(1)} collective-permute-done((bf16[256,256]{1,0:T(8,128)(2,1)S(1)}, bf16[256,256]{1,0:T(8,128)(2,1)S(1)}, u32[]{:S(2)}, u32[]{:S(2)}) %collective-permute-start.18) | collective-permute-done | bytes 131104 | tf_op jit(solution)/shard_map/ppermute | solution.py:482
  50.8 1.0 %shard_map.72.refs_0_ = bf16[512,128]{1,0:T(8,128)(2,1)S(1)} custom-call(s32[1]{0:T(128)S(6)} %copy.8.padded, bf16[256,128]{1,0:T(8,128)(2,1)S(1)} %get-tuple-element.37.refs_0_, bf16[256,128]{1,0:T(8,128)(2,1)S(1)} %get-tuple-element.43.refs_1_, bf16[256,256]{1,0:T(8,128)(2,1)S(1)} %collective-permute-done.17.refs_2_, ...), custom_call_target="tpu_custom_call" | custom-call | tf_op jit(solution)/shard_map/pallas_call | solution.py:57
  51.7 3.6 %collective-permute-start.20 = (bf16[512,128]{1,0:T(8,128)(2,1)S(1)}, bf16[512,128]{1,0:T(8,128)(2,1)S(1)}, u32[]{:S(2)}, u32[]{:S(2)}) collective-permute-start(bf16[512,128]{1,0:T(8,128)(2,1)S(1)} %shard_map.72.refs_0_), channel_id=1, source_target_pairs={{4,12},{12,8},{8,0},{0,4},{5,13},{13,9},{9,1},{1,5},{6,14},{14,10}... | collective-permute-start | bytes 393224 | tf_op jit(solution)/shard_map/ppermute | solution.py:500
  55.4 0.3 collective-permute-start.28
  55.6 0.3 collective-permute-start.22
  56.0 3.5 %collective-permute-done.20.refs_2_ = bf16[512,128]{1,0:T(8,128)(2,1)S(1)} collective-permute-done((bf16[512,128]{1,0:T(8,128)(2,1)S(1)}, bf16[512,128]{1,0:T(8,128)(2,1)S(1)}, u32[]{:S(2)}, u32[]{:S(2)}) %collective-permute-start.20) | collective-permute-done | bytes 131104 | tf_op jit(solution)/shard_map/ppermute | solution.py:500
  59.5 3.6 %collective-permute-start.24 = (bf16[512,128]{1,0:T(8,128)(2,1)S(1)}, bf16[512,128]{1,0:T(8,128)(2,1)S(1)}, u32[]{:S(2)}, u32[]{:S(2)}) collective-permute-start(bf16[512,128]{1,0:T(8,128)(2,1)S(1)} %collective-permute-done.20.refs_2_), channel_id=1, source_target_pairs={{4,12},{12,8},{8,0},{0,4},{5,13},{13,9},{9,1},{1,5},{6,14},{14,10}... | collective-permute-start | bytes 393224 | tf_op jit(solution)/shard_map/ppermute | solution.py:500
  63.1 0.5 collective-permute-start.21
  63.6 0.1 collective-permute-start.23
  63.7 1.9 %collective-permute-done.24.refs_6_ = bf16[512,128]{1,0:T(8,128)(2,1)S(1)} collective-permute-done((bf16[512,128]{1,0:T(8,128)(2,1)S(1)}, bf16[512,128]{1,0:T(8,128)(2,1)S(1)}, u32[]{:S(2)}, u32[]{:S(2)}) %collective-permute-start.24) | collective-permute-done | bytes 131104 | tf_op jit(solution)/shard_map/ppermute | solution.py:500
  65.6 4.0 %collective-permute-done.30.refs_10_ = bf16[256,384]{1,0:T(8,128)(2,1)S(1)} collective-permute-done((bf16[256,384]{1,0:T(8,128)(2,1)S(1)}, bf16[256,384]{1,0:T(8,128)(2,1)S(1)}, u32[]{:S(2)}, u32[]{:S(2)}) %collective-permute-start.30) | collective-permute-done | bytes 196640 | tf_op jit(solution)/shard_map/ppermute | solution.py:450
  69.7 0.8 %shard_map.75 = (f32[512,384]{1,0:T(8,128)S(1)}, bf16[128,384]{1,0:T(8,128)(2,1)S(1)}) custom-call(bf16[512,128]{1,0:T(8,128)(2,1)S(1)} %shard_map.72.refs_0_, bf16[512,128]{1,0:T(8,128)(2,1)S(1)} %collective-permute-done.19.refs_1_, bf16[512,128]{1,0:T(8,128)(2,1)S(1)} %collective-permute-done.20.refs_2_, ...), custom_call_target="tpu_custom_call" | custom-call | tf_op jit(solution)/shard_map/pallas_call | solution.py:57
  70.5 1.0 %output.1 = bf16[512,384]{1,0:T(8,128)(2,1)} custom-call(f32[3,8,384]{2,1,0:T(8,128)S(1)} %get-tuple-element.29.table_ref, f32[512,384]{1,0:T(8,128)S(1)} %get-tuple-element.51.acc_ref, bf16[128,384]{1,0:T(8,128)(2,1)S(1)} %get-tuple-element.52.w_ref, bf16[512,128]{1,0:T(8,128)(2,1)S(1)} %collective-permute-done.31.refs_0_), custom_call_target="tpu_custom_call" | custom-call | tf_op jit(solution)/shard_map/output/pallas_call | solution.py:514
  (31 shorter events, 0.1 us)
Async XLA Ops:
  0.0 35.5 %copy-start = (f32[50,3,3072]{2,0,1:T(8,128)S(1)}, f32[50,3,3072]{2,0,1:T(8,128)}, u32[]{:S(2)}) copy-start(f32[50,3,3072]{2,0,1:T(8,128)} %param.9) | copy-start | bytes 5529604
  1.5 6.2 %collective-permute-start.3 = (bf16[256,384]{1,0:T(8,128)(2,1)S(1)}, bf16[256,384]{1,0:T(8,128)(2,1)S(1)}, u32[]{:S(2)}, u32[]{:S(2)}) collective-permute-start(bf16[256,384]{1,0:T(8,128)(2,1)S(1)} %get-tuple-element.33.refs_0_), channel_id=1, source_target_pairs={{0,1},{1,0},{2,3},{3,2},{4,5},{5,4},{6,7},{7,6},{8,9},{9,8},{10,11... | collective-permute-start | bytes 589832 | tf_op jit(solution)/shard_map/ppermute | solution.py:353
  2.6 4.6 %collective-permute-start.25 = (bf16[128,384]{1,0:T(8,128)(2,1)S(1)}, bf16[128,384]{1,0:T(8,128)(2,1)S(1)}, u32[]{:S(2)}, u32[]{:S(2)}) collective-permute-start(bf16[128,384]{1,0:T(8,128)(2,1)S(1)} %get-tuple-element.50), channel_id=1, source_target_pairs={{0,1},{1,0},{2,3},{3,2},{4,5},{5,4},{6,7},{7,6},{8,9},{9,8},{10,11... | collective-permute-start | bytes 294920 | tf_op jit(solution)/shard_map/ppermute | solution.py:418
  3.1 7.9 %collective-permute-start.4 = (bf16[256,384]{1,0:T(8,128)(2,1)S(1)}, bf16[256,384]{1,0:T(8,128)(2,1)S(1)}, u32[]{:S(2)}, u32[]{:S(2)}) collective-permute-start(bf16[256,384]{1,0:T(8,128)(2,1)S(1)} %get-tuple-element.33.refs_0_), channel_id=1, source_target_pairs={{4,12},{12,8},{8,0},{0,4},{5,13},{13,9},{9,1},{1,5},{6,14},{14,10}... | collective-permute-start | bytes 589832 | tf_op jit(solution)/shard_map/ppermute | solution.py:350
  5.7 15.0 %collective-permute-start = (bf16[1536,128]{1,0:T(8,128)(2,1)S(1)}, bf16[1536,128]{1,0:T(8,128)(2,1)S(1)}, u32[]{:S(2)}, u32[]{:S(2)}) collective-permute-start(bf16[1536,128]{1,0:T(8,128)(2,1)S(1)} %get-tuple-element.30), channel_id=1, source_target_pairs={{0,2},{2,0},{1,3},{3,1},{4,6},{6,4},{5,7},{7,5},{8,10},{10,8},{9,1... | collective-permute-start | bytes 1179656 | tf_op jit(solution)/shard_map/ppermute | solution.py:364
  7.2 7.2 %collective-permute-start.10 = (bf16[256,384]{1,0:T(8,128)(2,1)S(1)}, bf16[256,384]{1,0:T(8,128)(2,1)S(1)}, u32[]{:S(2)}, u32[]{:S(2)}) collective-permute-start(bf16[256,384]{1,0:T(8,128)(2,1)S(1)} %get-tuple-element.39.refs_0_), channel_id=1, source_target_pairs={{0,1},{1,0},{2,3},{3,2},{4,5},{5,4},{6,7},{7,6},{8,9},{9,8},{10,11... | collective-permute-start | bytes 589832 | tf_op jit(solution)/shard_map/ppermute | solution.py:353
  7.2 8.0 %collective-permute-start.11 = (bf16[256,384]{1,0:T(8,128)(2,1)S(1)}, bf16[256,384]{1,0:T(8,128)(2,1)S(1)}, u32[]{:S(2)}, u32[]{:S(2)}) collective-permute-start(bf16[256,384]{1,0:T(8,128)(2,1)S(1)} %get-tuple-element.39.refs_0_), channel_id=1, source_target_pairs={{4,12},{12,8},{8,0},{0,4},{5,13},{13,9},{9,1},{1,5},{6,14},{14,10}... | collective-permute-start | bytes 589832 | tf_op jit(solution)/shard_map/ppermute | solution.py:350
  7.7 13.0 %collective-permute-start.26 = (bf16[256,384]{1,0:T(8,128)(2,1)S(1)}, bf16[256,384]{1,0:T(8,128)(2,1)S(1)}, u32[]{:S(2)}, u32[]{:S(2)}) collective-permute-start(bf16[256,384]{1,0:T(8,128)(2,1)S(1)} %shard_map.74), channel_id=1, source_target_pairs={{0,0},{2,2},{4,6},{6,4},{8,10},{10,8},{12,12},{14,14},{1,1},{3,3},... | collective-permute-start | bytes 589832 | tf_op jit(solution)/shard_map/ppermute | solution.py:435
  11.0 9.7 %collective-permute-start.6 = (bf16[256,384]{1,0:T(8,128)(2,1)S(1)}, bf16[256,384]{1,0:T(8,128)(2,1)S(1)}, u32[]{:S(2)}, u32[]{:S(2)}) collective-permute-start(bf16[256,384]{1,0:T(8,128)(2,1)S(1)} %collective-permute-done.4.refs_2_), channel_id=1, source_target_pairs={{4,12},{12,8},{8,0},{0,4},{5,13},{13,9},{9,1},{1,5},{6,14},{14,10}... | collective-permute-start | bytes 589832 | tf_op jit(solution)/shard_map/ppermute | solution.py:350
  14.4 7.9 %collective-permute-start.5 = (bf16[256,384]{1,0:T(8,128)(2,1)S(1)}, bf16[256,384]{1,0:T(8,128)(2,1)S(1)}, u32[]{:S(2)}, u32[]{:S(2)}) collective-permute-start(bf16[256,384]{1,0:T(8,128)(2,1)S(1)} %collective-permute-done.4.refs_2_), channel_id=1, source_target_pairs={{0,1},{1,0},{2,3},{3,2},{4,5},{5,4},{6,7},{7,6},{8,9},{9,8},{10,11... | collective-permute-start | bytes 589832 | tf_op jit(solution)/shard_map/ppermute | solution.py:353
  15.2 7.6 %collective-permute-start.12 = (bf16[256,384]{1,0:T(8,128)(2,1)S(1)}, bf16[256,384]{1,0:T(8,128)(2,1)S(1)}, u32[]{:S(2)}, u32[]{:S(2)}) collective-permute-start(bf16[256,384]{1,0:T(8,128)(2,1)S(1)} %collective-permute-done.11.refs_2_), channel_id=1, source_target_pairs={{0,1},{1,0},{2,3},{3,2},{4,5},{5,4},{6,7},{7,6},{8,9},{9,8},{10,11... | collective-permute-start | bytes 589832 | tf_op jit(solution)/shard_map/ppermute | solution.py:353
  20.7 6.6 %collective-permute-start.13 = (bf16[256,384]{1,0:T(8,128)(2,1)S(1)}, bf16[256,384]{1,0:T(8,128)(2,1)S(1)}, u32[]{:S(2)}, u32[]{:S(2)}) collective-permute-start(bf16[256,384]{1,0:T(8,128)(2,1)S(1)} %collective-permute-done.11.refs_2_), channel_id=1, source_target_pairs={{4,12},{12,8},{8,0},{0,4},{5,13},{13,9},{9,1},{1,5},{6,14},{14,10}... | collective-permute-start | bytes 589832 | tf_op jit(solution)/shard_map/ppermute | solution.py:350
  20.7 7.2 %collective-permute-start.7 = (bf16[256,384]{1,0:T(8,128)(2,1)S(1)}, bf16[256,384]{1,0:T(8,128)(2,1)S(1)}, u32[]{:S(2)}, u32[]{:S(2)}) collective-permute-start(bf16[256,384]{1,0:T(8,128)(2,1)S(1)} %collective-permute-done.6.refs_4_), channel_id=1, source_target_pairs={{0,1},{1,0},{2,3},{3,2},{4,5},{5,4},{6,7},{7,6},{8,9},{9,8},{10,11... | collective-permute-start | bytes 589832 | tf_op jit(solution)/shard_map/ppermute | solution.py:353
  20.7 18.2 %collective-permute-start.1 = (bf16[1536,128]{1,0:T(8,128)(2,1)S(1)}, bf16[1536,128]{1,0:T(8,128)(2,1)S(1)}, u32[]{:S(2)}, u32[]{:S(2)}) collective-permute-start(bf16[1536,128]{1,0:T(8,128)(2,1)S(1)} %get-tuple-element.31), channel_id=1, source_target_pairs={{0,2},{2,0},{1,3},{3,1},{4,6},{6,4},{5,7},{7,5},{8,10},{10,8},{9,1... | collective-permute-start | bytes 1179656 | tf_op jit(solution)/shard_map/ppermute | solution.py:365
  22.3 16.6 %collective-permute-start.2 = (bf16[1536,128]{1,0:T(8,128)(2,1)S(1)}, bf16[1536,128]{1,0:T(8,128)(2,1)S(1)}, u32[]{:S(2)}, u32[]{:S(2)}) collective-permute-start(bf16[1536,128]{1,0:T(8,128)(2,1)S(1)} %collective-permute-done.refs_1_), channel_id=1, source_target_pairs={{0,16},{16,0},{1,17},{17,1},{2,18},{18,2},{3,19},{19,3},{4,20},{20... | collective-permute-start | bytes 1179656 | tf_op jit(solution)/shard_map/ppermute | solution.py:366
  22.8 8.7 %collective-permute-start.8 = (bf16[256,384]{1,0:T(8,128)(2,1)S(1)}, bf16[256,384]{1,0:T(8,128)(2,1)S(1)}, u32[]{:S(2)}, u32[]{:S(2)}) collective-permute-start(bf16[256,384]{1,0:T(8,128)(2,1)S(1)} %collective-permute-done.6.refs_4_), channel_id=1, source_target_pairs={{4,12},{12,8},{8,0},{0,4},{5,13},{13,9},{9,1},{1,5},{6,14},{14,10}... | collective-permute-start | bytes 589832 | tf_op jit(solution)/shard_map/ppermute | solution.py:350
  27.3 7.5 %collective-permute-start.15 = (bf16[256,384]{1,0:T(8,128)(2,1)S(1)}, bf16[256,384]{1,0:T(8,128)(2,1)S(1)}, u32[]{:S(2)}, u32[]{:S(2)}) collective-permute-start(bf16[256,384]{1,0:T(8,128)(2,1)S(1)} %collective-permute-done.13.refs_4_), channel_id=1, source_target_pairs={{4,12},{12,8},{8,0},{0,4},{5,13},{13,9},{9,1},{1,5},{6,14},{14,10}... | collective-permute-start | bytes 589832 | tf_op jit(solution)/shard_map/ppermute | solution.py:350
  27.9 8.4 %collective-permute-start.14 = (bf16[256,384]{1,0:T(8,128)(2,1)S(1)}, bf16[256,384]{1,0:T(8,128)(2,1)S(1)}, u32[]{:S(2)}, u32[]{:S(2)}) collective-permute-start(bf16[256,384]{1,0:T(8,128)(2,1)S(1)} %collective-permute-done.13.refs_4_), channel_id=1, source_target_pairs={{0,1},{1,0},{2,3},{3,2},{4,5},{5,4},{6,7},{7,6},{8,9},{9,8},{10,11... | collective-permute-start | bytes 589832 | tf_op jit(solution)/shard_map/ppermute | solution.py:353
  31.6 8.7 %collective-permute-start.9 = (bf16[256,384]{1,0:T(8,128)(2,1)S(1)}, bf16[256,384]{1,0:T(8,128)(2,1)S(1)}, u32[]{:S(2)}, u32[]{:S(2)}) collective-permute-start(bf16[256,384]{1,0:T(8,128)(2,1)S(1)} %collective-permute-done.8.refs_0_), channel_id=1, source_target_pairs={{0,1},{1,0},{2,3},{3,2},{4,5},{5,4},{6,7},{7,6},{8,9},{9,8},{10,11... | collective-permute-start | bytes 589832 | tf_op jit(solution)/shard_map/ppermute | solution.py:353
  34.9 9.2 %collective-permute-start.16 = (bf16[256,384]{1,0:T(8,128)(2,1)S(1)}, bf16[256,384]{1,0:T(8,128)(2,1)S(1)}, u32[]{:S(2)}, u32[]{:S(2)}) collective-permute-start(bf16[256,384]{1,0:T(8,128)(2,1)S(1)} %collective-permute-done.15.refs_0_), channel_id=1, source_target_pairs={{0,1},{1,0},{2,3},{3,2},{4,5},{5,4},{6,7},{7,6},{8,9},{9,8},{10,11... | collective-permute-start | bytes 589832 | tf_op jit(solution)/shard_map/ppermute | solution.py:353
  36.3 19.1 %collective-permute-start.27 = (bf16[256,384]{1,0:T(8,128)(2,1)S(1)}, bf16[256,384]{1,0:T(8,128)(2,1)S(1)}, u32[]{:S(2)}, u32[]{:S(2)}) collective-permute-start(bf16[256,384]{1,0:T(8,128)(2,1)S(1)} %collective-permute-done.26), channel_id=1, source_target_pairs={{0,0},{2,10},{6,6},{4,12},{10,2},{8,8},{12,4},{14,14},{16,20},{18,... | collective-permute-start | bytes 589832 | tf_op jit(solution)/shard_map/ppermute | solution.py:436
  41.7 6.3 %collective-permute-start.17 = (bf16[256,256]{1,0:T(8,128)(2,1)S(1)}, bf16[256,256]{1,0:T(8,128)(2,1)S(1)}, u32[]{:S(2)}, u32[]{:S(2)}) collective-permute-start(bf16[256,256]{1,0:T(8,128)(2,1)S(1)} %get-tuple-element.44.refs_2_), channel_id=1, source_target_pairs={{0,2},{2,0},{1,3},{3,1},{4,6},{6,4},{5,7},{7,5},{8,10},{10,8},{9,1... | collective-permute-start | bytes 393224 | tf_op jit(solution)/shard_map/ppermute | solution.py:482
  45.2 5.5 %collective-permute-start.18 = (bf16[256,256]{1,0:T(8,128)(2,1)S(1)}, bf16[256,256]{1,0:T(8,128)(2,1)S(1)}, u32[]{:S(2)}, u32[]{:S(2)}) collective-permute-start(bf16[256,256]{1,0:T(8,128)(2,1)S(1)} %get-tuple-element.45.refs_3_), channel_id=1, source_target_pairs={{0,2},{2,0},{1,3},{3,1},{4,6},{6,4},{5,7},{7,5},{8,10},{10,8},{9,1... | collective-permute-start | bytes 393224 | tf_op jit(solution)/shard_map/ppermute | solution.py:482
  51.7 7.8 %collective-permute-start.20 = (bf16[512,128]{1,0:T(8,128)(2,1)S(1)}, bf16[512,128]{1,0:T(8,128)(2,1)S(1)}, u32[]{:S(2)}, u32[]{:S(2)}) collective-permute-start(bf16[512,128]{1,0:T(8,128)(2,1)S(1)} %shard_map.72.refs_0_), channel_id=1, source_target_pairs={{4,12},{12,8},{8,0},{0,4},{5,13},{13,9},{9,1},{1,5},{6,14},{14,10}... | collective-permute-start | bytes 393224 | tf_op jit(solution)/shard_map/ppermute | solution.py:500
  55.4 7.7 %collective-permute-start.28 = (bf16[256,384]{1,0:T(8,128)(2,1)S(1)}, bf16[256,384]{1,0:T(8,128)(2,1)S(1)}, u32[]{:S(2)}, u32[]{:S(2)}) collective-permute-start(bf16[256,384]{1,0:T(8,128)(2,1)S(1)} %collective-permute-done.27.refs_7_), channel_id=1, source_target_pairs={{0,2},{2,0},{16,18},{18,16},{1,3},{3,1},{17,19},{19,17},{4,6},{6,4... | collective-permute-start | bytes 589832 | tf_op jit(solution)/shard_map/ppermute | solution.py:450
  55.6 7.5 %collective-permute-start.29 = (bf16[256,384]{1,0:T(8,128)(2,1)S(1)}, bf16[256,384]{1,0:T(8,128)(2,1)S(1)}, u32[]{:S(2)}, u32[]{:S(2)}) collective-permute-start(bf16[256,384]{1,0:T(8,128)(2,1)S(1)} %collective-permute-done.27.refs_7_), channel_id=1, source_target_pairs={{0,16},{2,18},{16,0},{18,2},{1,17},{3,19},{17,1},{19,3},{4,20},{6,... | collective-permute-start | bytes 589832 | tf_op jit(solution)/shard_map/ppermute | solution.py:450
  55.6 8.0 %collective-permute-start.22 = (bf16[512,128]{1,0:T(8,128)(2,1)S(1)}, bf16[512,128]{1,0:T(8,128)(2,1)S(1)}, u32[]{:S(2)}, u32[]{:S(2)}) collective-permute-start(bf16[512,128]{1,0:T(8,128)(2,1)S(1)} %shard_map.72.refs_0_), channel_id=1, source_target_pairs={{4,0},{12,4},{8,12},{0,8},{5,1},{13,5},{9,13},{1,9},{6,2},{14,6},{... | collective-permute-start | bytes 393224 | tf_op jit(solution)/shard_map/ppermute | solution.py:502
  59.5 6.1 %collective-permute-start.24 = (bf16[512,128]{1,0:T(8,128)(2,1)S(1)}, bf16[512,128]{1,0:T(8,128)(2,1)S(1)}, u32[]{:S(2)}, u32[]{:S(2)}) collective-permute-start(bf16[512,128]{1,0:T(8,128)(2,1)S(1)} %collective-permute-done.20.refs_2_), channel_id=1, source_target_pairs={{4,12},{12,8},{8,0},{0,4},{5,13},{13,9},{9,1},{1,5},{6,14},{14,10}... | collective-permute-start | bytes 393224 | tf_op jit(solution)/shard_map/ppermute | solution.py:500
  63.1 6.6 %collective-permute-start.30 = (bf16[256,384]{1,0:T(8,128)(2,1)S(1)}, bf16[256,384]{1,0:T(8,128)(2,1)S(1)}, u32[]{:S(2)}, u32[]{:S(2)}) collective-permute-start(bf16[256,384]{1,0:T(8,128)(2,1)S(1)} %collective-permute-done.27.refs_7_), channel_id=1, source_target_pairs={{0,18},{2,16},{16,2},{18,0},{1,19},{3,17},{17,3},{19,1},{4,22},{6,... | collective-permute-start | bytes 589832 | tf_op jit(solution)/shard_map/ppermute | solution.py:450
  63.1 6.6 %collective-permute-start.19 = (bf16[512,128]{1,0:T(8,128)(2,1)S(1)}, bf16[512,128]{1,0:T(8,128)(2,1)S(1)}, u32[]{:S(2)}, u32[]{:S(2)}) collective-permute-start(bf16[512,128]{1,0:T(8,128)(2,1)S(1)} %shard_map.72.refs_0_), channel_id=1, source_target_pairs={{0,1},{1,0},{2,3},{3,2},{4,5},{5,4},{6,7},{7,6},{8,9},{9,8},{10,11... | collective-permute-start | bytes 393224 | tf_op jit(solution)/shard_map/ppermute | solution.py:505
  63.1 6.5 %collective-permute-start.21 = (bf16[512,128]{1,0:T(8,128)(2,1)S(1)}, bf16[512,128]{1,0:T(8,128)(2,1)S(1)}, u32[]{:S(2)}, u32[]{:S(2)}) collective-permute-start(bf16[512,128]{1,0:T(8,128)(2,1)S(1)} %collective-permute-done.20.refs_2_), channel_id=1, source_target_pairs={{0,1},{1,0},{2,3},{3,2},{4,5},{5,4},{6,7},{7,6},{8,9},{9,8},{10,11... | collective-permute-start | bytes 393224 | tf_op jit(solution)/shard_map/ppermute | solution.py:505
  63.6 6.1 %collective-permute-start.23 = (bf16[512,128]{1,0:T(8,128)(2,1)S(1)}, bf16[512,128]{1,0:T(8,128)(2,1)S(1)}, u32[]{:S(2)}, u32[]{:S(2)}) collective-permute-start(bf16[512,128]{1,0:T(8,128)(2,1)S(1)} %collective-permute-done.22.refs_4_), channel_id=1, source_target_pairs={{0,1},{1,0},{2,3},{3,2},{4,5},{5,4},{6,7},{7,6},{8,9},{9,8},{10,11... | collective-permute-start | bytes 393224 | tf_op jit(solution)/shard_map/ppermute | solution.py:505
  65.6 4.9 %collective-permute-start.31 = (bf16[512,128]{1,0:T(8,128)(2,1)S(1)}, bf16[512,128]{1,0:T(8,128)(2,1)S(1)}, u32[]{:S(2)}, u32[]{:S(2)}) collective-permute-start(bf16[512,128]{1,0:T(8,128)(2,1)S(1)} %collective-permute-done.24.refs_6_), channel_id=1, source_target_pairs={{0,1},{1,0},{2,3},{3,2},{4,5},{5,4},{6,7},{7,6},{8,9},{9,8},{10,11... | collective-permute-start | bytes 393224 | tf_op jit(solution)/shard_map/ppermute | solution.py:505
